TPU v7x, 32 devices: a whole 2x2x4 slice. The times are simulated.
32 devices in a mesh: col: 8 (over z, x), row: 4 (over y, core).
Axes of the slice: x: 2, y: 2, z: 4, core: 2. Of those that a mesh axis runs over, the one named last changes fastest.
Arguments:
- vorticity: float32 [2, 8, 1024, 2048], P(None, 'row', 'col'), may hold values from -0.0017578125 to 0.0017578125
- divergence: float32 [2, 8, 1024, 2048], P(None, 'row', 'col'), may hold values from -0.0017578125 to 0.0017578125
- trunc_cut: int32 [1024], P('col'), may hold values from -1 to 1023, as said below
- level_slot: int32 [8], replicated, may hold values from 0 to 7, each once
Outputs:
- u_wind: float32 [8, 2048, 2048], P(None, ('col', 'row'))
- v_wind: float32 [8, 2048, 2048], P(None, ('col', 'row'))
- u_slope: float32 [8, 2048, 2048], P(None, ('col', 'row'))
- v_slope: float32 [8, 2048, 2048], P(None, ('col', 'row'))
Inputs may be any that keep to these rules, and one draw needn't show every extreme that they name: trunc_cut never rises with m, is 1023 at m = 0 and -1 (nothing kept) at the last m. level_slot is a permutation of the model levels.
All inputs are finite; a program needn't handle non-finite values.
Results may differ from a plain program's by a relative error of at most 0.0001.
Values sent between devices are 32-bit elements; how exact they have to be, the bound alone decides.
No kernel may reach another device: no remote copies, remote signals or barrier semaphores. Data moves between devices by JAX's collectives and lax.ppermute only.
A program may use at most 128 MiB of HBM per device.

v0:
```python
import math

import jax
import jax.numpy as jnp
from jax import lax
from jax.sharding import PartitionSpec as P

HIGHEST = lax.Precision.HIGHEST


def spectral_winds(vorticity, divergence, trunc_cut, first_wave, east_cells):
    local_count = vorticity.shape[2]
    north_cells = vorticity.shape[3]
    wave_index = first_wave + jnp.arange(local_count, dtype=jnp.int32)
    north_index = jnp.arange(north_cells, dtype=jnp.int32)
    north_wave = jnp.where(north_index < north_cells // 2, north_index, north_index - north_cells)
    wave_east = 2.0 * math.pi / east_cells * wave_index.astype(jnp.float32)
    wave_north = 2.0 * math.pi / north_cells * north_wave.astype(jnp.float32)
    east_col = wave_east[:, None]
    north_row = wave_north[None, :]
    square_wave = east_col * east_col + north_row * north_row
    retained = (jnp.abs(north_wave)[None, :] <= trunc_cut[:, None]) & (square_wave > 0)
    inverse_square = jnp.where(retained, 1.0 / jnp.where(square_wave > 0, square_wave, 1.0), 0.0)
    curl_real = vorticity[0]
    curl_imag = vorticity[1]
    source_real = divergence[0]
    source_imag = divergence[1]
    east_real = (-north_row * curl_imag + east_col * source_imag) * inverse_square
    east_imag = (north_row * curl_real - east_col * source_real) * inverse_square
    north_real = (east_col * curl_imag + north_row * source_imag) * inverse_square
    north_imag = (-east_col * curl_real - north_row * source_real) * inverse_square
    return jnp.stack([east_real, east_imag, north_real, north_imag], axis=1)


def north_transform(flattened, local_waves):
    slot_count = flattened.shape[0]
    north_cells = flattened.shape[2]
    block_size = math.gcd(north_cells, 256)
    block_count = north_cells // block_size
    north_index = jnp.arange(north_cells, dtype=jnp.int32)

    def north_one_block(block_index, result):
        row_index = block_index * block_size + jnp.arange(block_size, dtype=jnp.int32)
        phase_steps = row_index[:, None] * north_index[None, :] % north_cells
        angles = 2.0 * math.pi / north_cells * phase_steps.astype(jnp.float32)
        cosine_table = jnp.cos(angles)
        sine_table = jnp.sin(angles)
        with_cosine = jnp.einsum("yn,lkn->lyk", cosine_table, flattened, precision=HIGHEST)
        with_sine = jnp.einsum("yn,lkn->lyk", sine_table, flattened, precision=HIGHEST)
        with_cosine = with_cosine.reshape(slot_count, block_size, 2, 2, local_waves)
        with_sine = with_sine.reshape(slot_count, block_size, 2, 2, local_waves)
        real_part = with_cosine[:, :, :, 0] - with_sine[:, :, :, 1]
        imag_part = with_sine[:, :, :, 0] + with_cosine[:, :, :, 1]
        joined = jnp.concatenate([real_part, imag_part], axis=3)
        return lax.dynamic_update_slice_in_dim(result, joined, block_index * block_size, 1)

    initial = jnp.zeros((slot_count, north_cells, 2, 2 * local_waves), jnp.float32)
    return lax.fori_loop(0, block_count, north_one_block, initial)


def east_transform(stacked, local_waves, east_cells):
    columns = stacked.shape[0]
    slot_count = stacked.shape[1]
    row_count = stacked.shape[2]
    field_count = stacked.shape[3]
    block_size = math.gcd(east_cells, 256)
    block_count = east_cells // block_size
    wave_number = (
        jnp.arange(columns, dtype=jnp.int32)[:, None] * local_waves
        + jnp.arange(local_waves, dtype=jnp.int32)[None, :]
    )
    weights = jnp.where(wave_number == 0, 1.0, 2.0)[:, :, None]
    wave_east = 2.0 * math.pi / east_cells * wave_number.astype(jnp.float32)[:, :, None]

    def east_one_block(block_index, result):
        east_index = block_index * block_size + jnp.arange(block_size, dtype=jnp.int32)
        phase_steps = wave_number[:, :, None] * east_index[None, None, :] % east_cells
        angles = 2.0 * math.pi / east_cells * phase_steps.astype(jnp.float32)
        cosine_table = jnp.cos(angles)
        sine_table = jnp.sin(angles)
        value_real = weights * cosine_table
        value_imag = -weights * sine_table
        slope_real = -weights * wave_east * sine_table
        slope_imag = -weights * wave_east * cosine_table
        value_table = jnp.stack([value_real, value_imag], axis=1)
        slope_table = jnp.stack([slope_real, slope_imag], axis=1)
        east_table = jnp.stack([value_table, slope_table], axis=3).reshape(
            columns, 2 * local_waves, 2, block_size
        )
        product = jnp.einsum("clyfk,ckab->falyb", stacked, east_table, precision=HIGHEST)
        return lax.dynamic_update_slice_in_dim(result, product, block_index * block_size, 4)

    initial = jnp.zeros((field_count, 2, slot_count, row_count, east_cells), jnp.float32)
    return lax.fori_loop(0, block_count, east_one_block, initial)


def place_levels(grid_all, level_slot):
    slot_count = grid_all.shape[2]
    selector = (level_slot[None, :] == jnp.arange(slot_count, dtype=jnp.int32)[:, None]).astype(
        jnp.float32
    )
    return jnp.einsum("ls,fasyx->falyx", selector, grid_all, precision=HIGHEST)


def on_device(vorticity, divergence, trunc_cut, level_slot):
    columns = lax.axis_size("col")
    row_count = lax.axis_size("row")
    local_waves = vorticity.shape[2]
    north_cells = vorticity.shape[3]
    east_cells = 2 * local_waves * columns
    first_wave = lax.axis_index("col") * local_waves
    spectra = spectral_winds(vorticity, divergence, trunc_cut, first_wave, east_cells)
    slot_count = spectra.shape[0]
    flattened = spectra.reshape(slot_count, 4 * local_waves, north_cells)
    fourier = north_transform(flattened, local_waves)
    outgoing = fourier[None]
    received = lax.all_to_all(outgoing, ("col", "row"), split_axis=2, concat_axis=0, tiled=True)
    shaped = received.reshape(
        columns,
        row_count * received.shape[1],
        received.shape[2],
        received.shape[3],
        received.shape[4],
    )
    grid_all = east_transform(shaped, local_waves, east_cells)
    placed = place_levels(grid_all, level_slot)
    return (placed[0, 0], placed[1, 0], placed[0, 1], placed[1, 1])


def solution(mesh):
    return jax.shard_map(
        on_device,
        mesh=mesh,
        in_specs=(P(None, "row", "col", None), P(None, "row", "col", None), P("col"), P()),
        out_specs=(
            P(None, ("col", "row"), None),
            P(None, ("col", "row"), None),
            P(None, ("col", "row"), None),
            P(None, ("col", "row"), None),
        ),
        check_vma=False,
    )
```

profile of v0, /device:TPU:6, one launch (start us, length us, event | category | flops | bytes accessed | tf_op | source)
XLA Modules:
  0.0 820.9 jit_solution(6526795939070336605)
XLA Ops:
  1.7 4.5 fusion.57
  6.8 3.8 copy.46
  10.6 5.5 broadcast_in_dim.32.clone
  16.1 356.5 %while.35 = (s32[]{:T(128)}, f32[2,2048,2,256]{3,2,0,1:T(2,128)}, f32[2,512,2048]{2,1,0:T(8,128)}, s32[]{:T(128)}, s32[]{:T(128)}, /*index=5*/s32[]{:T(128)}, s32[]{:T(128)}) while((s32[]{:T(128)}, f32[2,2048,2,256]{3,2,0,1:T(2,128)}, f32[2,512,2048]{2,1,0:T(8,128)}, s32[]{:T(128)}, s32[]{:T(128)}, /*index=5*/s32[]{:T(128)}, ...), condition=%wide.region_1.2_spmd.clone, body=%wide.region_0.1_spmd.clone.sunk | while | flops 12900106240 | bytes 32509060 | solution.py:58
  38.5 18.1 %fusion.96 = f32[2,256,512]{2,1,0:T(8,128)S(1)} fusion(f32[2,512,2048]{2,1,0:T(8,128)} %get-tuple-element.528, s32[256]{0:T(256)S(1)} %iota_add_fusion.7), kind=kOutput, calls=%fused_computation.21.clone.1 | convolution fusion | flops 6449790976 | bytes 9438208 | tf_op jit(solution)/shard_map/while/body/eval_jaxpr/yn,lkn->lyk/dot_general | solution.py:48
  58.1 18.2 %fusion.94 = f32[2,256,512]{2,1,0:T(8,128)S(1)} fusion(f32[2,512,2048]{2,1,0:T(8,128)} %get-tuple-element.528, s32[256]{0:T(256)S(1)} %iota_add_fusion.7), kind=kOutput, calls=%fused_computation.22.clone.1 | convolution fusion | flops 6449790976 | bytes 9438208 | tf_op jit(solution)/shard_map/while/body/eval_jaxpr/yn,lkn->lyk/dot_general | solution.py:49
  79.9 18.1 %fusion.96 = f32[2,256,512]{2,1,0:T(8,128)S(1)} fusion(f32[2,512,2048]{2,1,0:T(8,128)} %get-tuple-element.528, s32[256]{0:T(256)S(1)} %iota_add_fusion.7), kind=kOutput, calls=%fused_computation.21.clone.1 | convolution fusion | flops 6449790976 | bytes 9438208 | tf_op jit(solution)/shard_map/while/body/eval_jaxpr/yn,lkn->lyk/dot_general | solution.py:48
  99.5 18.2 %fusion.94 = f32[2,256,512]{2,1,0:T(8,128)S(1)} fusion(f32[2,512,2048]{2,1,0:T(8,128)} %get-tuple-element.528, s32[256]{0:T(256)S(1)} %iota_add_fusion.7), kind=kOutput, calls=%fused_computation.22.clone.1 | convolution fusion | flops 6449790976 | bytes 9438208 | tf_op jit(solution)/shard_map/while/body/eval_jaxpr/yn,lkn->lyk/dot_general | solution.py:49
  121.1 18.1 %fusion.96 = f32[2,256,512]{2,1,0:T(8,128)S(1)} fusion(f32[2,512,2048]{2,1,0:T(8,128)} %get-tuple-element.528, s32[256]{0:T(256)S(1)} %iota_add_fusion.7), kind=kOutput, calls=%fused_computation.21.clone.1 | convolution fusion | flops 6449790976 | bytes 9438208 | tf_op jit(solution)/shard_map/while/body/eval_jaxpr/yn,lkn->lyk/dot_general | solution.py:48
  140.7 18.2 %fusion.94 = f32[2,256,512]{2,1,0:T(8,128)S(1)} fusion(f32[2,512,2048]{2,1,0:T(8,128)} %get-tuple-element.528, s32[256]{0:T(256)S(1)} %iota_add_fusion.7), kind=kOutput, calls=%fused_computation.22.clone.1 | convolution fusion | flops 6449790976 | bytes 9438208 | tf_op jit(solution)/shard_map/while/body/eval_jaxpr/yn,lkn->lyk/dot_general | solution.py:49
  162.4 18.1 %fusion.96 = f32[2,256,512]{2,1,0:T(8,128)S(1)} fusion(f32[2,512,2048]{2,1,0:T(8,128)} %get-tuple-element.528, s32[256]{0:T(256)S(1)} %iota_add_fusion.7), kind=kOutput, calls=%fused_computation.21.clone.1 | convolution fusion | flops 6449790976 | bytes 9438208 | tf_op jit(solution)/shard_map/while/body/eval_jaxpr/yn,lkn->lyk/dot_general | solution.py:48
  182.0 18.2 %fusion.94 = f32[2,256,512]{2,1,0:T(8,128)S(1)} fusion(f32[2,512,2048]{2,1,0:T(8,128)} %get-tuple-element.528, s32[256]{0:T(256)S(1)} %iota_add_fusion.7), kind=kOutput, calls=%fused_computation.22.clone.1 | convolution fusion | flops 6449790976 | bytes 9438208 | tf_op jit(solution)/shard_map/while/body/eval_jaxpr/yn,lkn->lyk/dot_general | solution.py:49
  203.7 18.1 %fusion.96 = f32[2,256,512]{2,1,0:T(8,128)S(1)} fusion(f32[2,512,2048]{2,1,0:T(8,128)} %get-tuple-element.528, s32[256]{0:T(256)S(1)} %iota_add_fusion.7), kind=kOutput, calls=%fused_computation.21.clone.1 | convolution fusion | flops 6449790976 | bytes 9438208 | tf_op jit(solution)/shard_map/while/body/eval_jaxpr/yn,lkn->lyk/dot_general | solution.py:48
  223.3 18.2 %fusion.94 = f32[2,256,512]{2,1,0:T(8,128)S(1)} fusion(f32[2,512,2048]{2,1,0:T(8,128)} %get-tuple-element.528, s32[256]{0:T(256)S(1)} %iota_add_fusion.7), kind=kOutput, calls=%fused_computation.22.clone.1 | convolution fusion | flops 6449790976 | bytes 9438208 | tf_op jit(solution)/shard_map/while/body/eval_jaxpr/yn,lkn->lyk/dot_general | solution.py:49
  245.1 18.1 %fusion.96 = f32[2,256,512]{2,1,0:T(8,128)S(1)} fusion(f32[2,512,2048]{2,1,0:T(8,128)} %get-tuple-element.528, s32[256]{0:T(256)S(1)} %iota_add_fusion.7), kind=kOutput, calls=%fused_computation.21.clone.1 | convolution fusion | flops 6449790976 | bytes 9438208 | tf_op jit(solution)/shard_map/while/body/eval_jaxpr/yn,lkn->lyk/dot_general | solution.py:48
  264.7 18.2 %fusion.94 = f32[2,256,512]{2,1,0:T(8,128)S(1)} fusion(f32[2,512,2048]{2,1,0:T(8,128)} %get-tuple-element.528, s32[256]{0:T(256)S(1)} %iota_add_fusion.7), kind=kOutput, calls=%fused_computation.22.clone.1 | convolution fusion | flops 6449790976 | bytes 9438208 | tf_op jit(solution)/shard_map/while/body/eval_jaxpr/yn,lkn->lyk/dot_general | solution.py:49
  286.4 18.1 %fusion.96 = f32[2,256,512]{2,1,0:T(8,128)S(1)} fusion(f32[2,512,2048]{2,1,0:T(8,128)} %get-tuple-element.528, s32[256]{0:T(256)S(1)} %iota_add_fusion.7), kind=kOutput, calls=%fused_computation.21.clone.1 | convolution fusion | flops 6449790976 | bytes 9438208 | tf_op jit(solution)/shard_map/while/body/eval_jaxpr/yn,lkn->lyk/dot_general | solution.py:48
  306.0 18.2 %fusion.94 = f32[2,256,512]{2,1,0:T(8,128)S(1)} fusion(f32[2,512,2048]{2,1,0:T(8,128)} %get-tuple-element.528, s32[256]{0:T(256)S(1)} %iota_add_fusion.7), kind=kOutput, calls=%fused_computation.22.clone.1 | convolution fusion | flops 6449790976 | bytes 9438208 | tf_op jit(solution)/shard_map/while/body/eval_jaxpr/yn,lkn->lyk/dot_general | solution.py:49
  327.7 18.1 %fusion.96 = f32[2,256,512]{2,1,0:T(8,128)S(1)} fusion(f32[2,512,2048]{2,1,0:T(8,128)} %get-tuple-element.528, s32[256]{0:T(256)S(1)} %iota_add_fusion.7), kind=kOutput, calls=%fused_computation.21.clone.1 | convolution fusion | flops 6449790976 | bytes 9438208 | tf_op jit(solution)/shard_map/while/body/eval_jaxpr/yn,lkn->lyk/dot_general | solution.py:48
  347.3 18.2 %fusion.94 = f32[2,256,512]{2,1,0:T(8,128)S(1)} fusion(f32[2,512,2048]{2,1,0:T(8,128)} %get-tuple-element.528, s32[256]{0:T(256)S(1)} %iota_add_fusion.7), kind=kOutput, calls=%fused_computation.22.clone.1 | convolution fusion | flops 6449790976 | bytes 9438208 | tf_op jit(solution)/shard_map/while/body/eval_jaxpr/yn,lkn->lyk/dot_general | solution.py:49
  372.6 6.1 all-to-all-start
  378.7 188.5 %all-to-all-done = f32[1,2,2048,2,256]{4,3,1,0,2:T(2,128)} async-done(((f32[1,2,2048,2,256]{4,3,1,0,2:T(2,128)}), f32[1,2,2048,2,256]{4,3,1,0,2:T(2,128)}, u32[]{:S(2)}, u32[]{:S(2)}) %all-to-all-start) | async-done | bytes 8388640 | tf_op jit(solution)/shard_map/all_to_all | solution.py:117
  567.2 5.0 copy.48
  573.3 3.8 copy.50
  577.2 7.9 broadcast_in_dim.27.clone
  585.0 192.5 %while.36 = (s32[]{:T(128)}, f32[2,2,8,64,2048]{4,2,3,1,0:T(8,128)}, f32[8,8,64,2,256]{4,2,0,3,1:T(8,128)}, s32[8]{0:T(128)S(1)}, s32[]{:T(128)}, /*index=5*/s32[]{:T(128)}, s32[]{:T(128)}, s32[]{:T(128)}) while((s32[]{:T(128)}, f32[2,2,8,64,2048]{4,2,3,1,0:T(8,128)}, f32[8,8,64,2,256]{4,2,0,3,1:T(8,128)}, ...), condition=%wide.region_3.4_spmd.clone.clone.clone, body=%wide.region_2.3_spmd.clone.clone.clone.sunk | while | flops 12891725824 | bytes 65046760 | solution.py:94
  585.6 4.3 broadcast_multiply_fusion.4
  593.3 13.6 %fusion.99 = f32[2,2,8,64,256]{4,3,0,2,1:T(8,128)S(1)} fusion(f32[8,8,64,2,256]{4,2,0,3,1:T(8,128)S(1)} %copy-done, f32[8,256,1,256]{3,1,0,2:T(8,128)S(1)} %bitcast.142, f32[8,256,1,256]{3,1,0,2:T(8,128)S(1)} %bitcast.141), kind=kOutput, calls=%fused_computation.47.clone.1 | convolution fusion | flops 12885950464 | bytes 14680064 | tf_op jit(solution)/shard_map/while/body/eval_jaxpr/clyfk,ckab->falyb/dot_general | solution.py:90
  609.6 4.3 broadcast_multiply_fusion.4
  617.3 13.5 %fusion.99 = f32[2,2,8,64,256]{4,3,0,2,1:T(8,128)S(1)} fusion(f32[8,8,64,2,256]{4,2,0,3,1:T(8,128)S(1)} %copy-done, f32[8,256,1,256]{3,1,0,2:T(8,128)S(1)} %bitcast.142, f32[8,256,1,256]{3,1,0,2:T(8,128)S(1)} %bitcast.141), kind=kOutput, calls=%fused_computation.47.clone.1 | convolution fusion | flops 12885950464 | bytes 14680064 | tf_op jit(solution)/shard_map/while/body/eval_jaxpr/clyfk,ckab->falyb/dot_general | solution.py:90
  633.6 4.3 broadcast_multiply_fusion.4
  641.3 13.5 %fusion.99 = f32[2,2,8,64,256]{4,3,0,2,1:T(8,128)S(1)} fusion(f32[8,8,64,2,256]{4,2,0,3,1:T(8,128)S(1)} %copy-done, f32[8,256,1,256]{3,1,0,2:T(8,128)S(1)} %bitcast.142, f32[8,256,1,256]{3,1,0,2:T(8,128)S(1)} %bitcast.141), kind=kOutput, calls=%fused_computation.47.clone.1 | convolution fusion | flops 12885950464 | bytes 14680064 | tf_op jit(solution)/shard_map/while/body/eval_jaxpr/clyfk,ckab->falyb/dot_general | solution.py:90
  657.6 4.3 broadcast_multiply_fusion.4
  665.2 13.6 %fusion.99 = f32[2,2,8,64,256]{4,3,0,2,1:T(8,128)S(1)} fusion(f32[8,8,64,2,256]{4,2,0,3,1:T(8,128)S(1)} %copy-done, f32[8,256,1,256]{3,1,0,2:T(8,128)S(1)} %bitcast.142, f32[8,256,1,256]{3,1,0,2:T(8,128)S(1)} %bitcast.141), kind=kOutput, calls=%fused_computation.47.clone.1 | convolution fusion | flops 12885950464 | bytes 14680064 | tf_op jit(solution)/shard_map/while/body/eval_jaxpr/clyfk,ckab->falyb/dot_general | solution.py:90
  681.5 4.3 broadcast_multiply_fusion.4
  689.2 13.6 %fusion.99 = f32[2,2,8,64,256]{4,3,0,2,1:T(8,128)S(1)} fusion(f32[8,8,64,2,256]{4,2,0,3,1:T(8,128)S(1)} %copy-done, f32[8,256,1,256]{3,1,0,2:T(8,128)S(1)} %bitcast.142, f32[8,256,1,256]{3,1,0,2:T(8,128)S(1)} %bitcast.141), kind=kOutput, calls=%fused_computation.47.clone.1 | convolution fusion | flops 12885950464 | bytes 14680064 | tf_op jit(solution)/shard_map/while/body/eval_jaxpr/clyfk,ckab->falyb/dot_general | solution.py:90
  705.6 4.3 broadcast_multiply_fusion.4
  713.2 13.6 %fusion.99 = f32[2,2,8,64,256]{4,3,0,2,1:T(8,128)S(1)} fusion(f32[8,8,64,2,256]{4,2,0,3,1:T(8,128)S(1)} %copy-done, f32[8,256,1,256]{3,1,0,2:T(8,128)S(1)} %bitcast.142, f32[8,256,1,256]{3,1,0,2:T(8,128)S(1)} %bitcast.141), kind=kOutput, calls=%fused_computation.47.clone.1 | convolution fusion | flops 12885950464 | bytes 14680064 | tf_op jit(solution)/shard_map/while/body/eval_jaxpr/clyfk,ckab->falyb/dot_general | solution.py:90
  729.6 4.3 broadcast_multiply_fusion.4
  737.2 13.6 %fusion.99 = f32[2,2,8,64,256]{4,3,0,2,1:T(8,128)S(1)} fusion(f32[8,8,64,2,256]{4,2,0,3,1:T(8,128)S(1)} %copy-done, f32[8,256,1,256]{3,1,0,2:T(8,128)S(1)} %bitcast.142, f32[8,256,1,256]{3,1,0,2:T(8,128)S(1)} %bitcast.141), kind=kOutput, calls=%fused_computation.47.clone.1 | convolution fusion | flops 12885950464 | bytes 14680064 | tf_op jit(solution)/shard_map/while/body/eval_jaxpr/clyfk,ckab->falyb/dot_general | solution.py:90
  753.6 4.3 broadcast_multiply_fusion.4
  761.2 13.6 %fusion.99 = f32[2,2,8,64,256]{4,3,0,2,1:T(8,128)S(1)} fusion(f32[8,8,64,2,256]{4,2,0,3,1:T(8,128)S(1)} %copy-done, f32[8,256,1,256]{3,1,0,2:T(8,128)S(1)} %bitcast.142, f32[8,256,1,256]{3,1,0,2:T(8,128)S(1)} %bitcast.141), kind=kOutput, calls=%fused_computation.47.clone.1 | convolution fusion | flops 12885950464 | bytes 14680064 | tf_op jit(solution)/shard_map/while/body/eval_jaxpr/clyfk,ckab->falyb/dot_general | solution.py:90
  777.6 19.0 %convolution_bitcast_fusion = f32[2,2,8,64,2048]{4,2,3,1,0:T(8,128)} fusion(f32[2,2,8,64,2048]{4,2,3,1,0:T(8,128)} %get-tuple-element.306, s32[8]{0:T(128)S(1)} %copy-done.1), kind=kOutput, calls=%fused_computation.70 | convolution fusion | flops 402653248 | bytes 33554464 | tf_op jit(solution)/shard_map/ls,fasyx->falyx/dot_general | solution.py:102
  796.5 6.5 slice_bitcast_fusion
  803.0 4.4 copy.55
  807.4 4.4 copy.54
  811.9 4.4 copy.53
  816.3 4.4 copy.52
  (123 shorter events, 91.9 us)
Async XLA Ops:
  372.6 194.6 %all-to-all-start = ((f32[1,2,2048,2,256]{4,3,1,0,2:T(2,128)}), f32[1,2,2048,2,256]{4,3,1,0,2:T(2,128)}, u32[]{:S(2)}, u32[]{:S(2)}) async-start(f32[1,2,2048,2,256]{4,3,1,0,2:T(2,128)} %bitcast.147), calls=%async_computation | async-start | bytes 16777216 | tf_op jit(solution)/shard_map/all_to_all | solution.py:117
  585.0 192.5 %copy-start.1 = (s32[8]{0:T(128)S(1)}, s32[8]{0:T(128)}, u32[]{:S(2)}) copy-start(s32[8]{0:T(128)} %param.11) | copy-start | bytes 100
  589.9 3.4 copy-start
  613.9 3.4 copy-start
  637.9 3.4 copy-start
  661.8 3.4 copy-start
  685.8 3.4 copy-start
  709.8 3.4 copy-start
  733.8 3.4 copy-start
  757.9 3.4 copy-start
where the time goes:
time: 824 us; the launch traced here: 821 us
  matrix products  417 us (51%)
  waiting for transfers between devices  188 us (23%)
  local copies, waits for them, and re-layouts  119 us (14%)
  other arithmetic  61.3 us (7%)
  loops' own time  27.3 us (3%)
    all_to_all x1, waiting for transfers between devices, on_device(): lax.all_to_all(outgoing, ('col', 'row'), split_axis=2, concat_axis=0, til...  188 us
    dot_general x8, matrix products, north_one_block(): jnp.einsum('yn,lkn->lyk', sine_table, flattened, precision=HIGHEST)  145 us
    dot_general x8, matrix products, north_one_block(): jnp.einsum('yn,lkn->lyk', cosine_table, flattened, precision=HIGHEST)  145 us
    dot_general x8, matrix products, east_one_block(): jnp.einsum('clyfk,ckab->falyb', stacked, east_table, precision=HIGHEST)  108 us
    mul x8, other arithmetic, east_one_block(): slope_real = -weights * wave_east * sine_table  34.2 us
    another operation x1, loops' own time, north_transform(): return lax.fori_loop(0, block_count, north_one_block, initial)  26.5 us
    while x16, local copies, waits for them, and re-layouts  23.4 us
    unnamed x7, local copies, waits for them, and re-layouts  21.6 us
  transfers between devices with their start and end apart: 1, of which 1 were waited for; matrix products, arithmetic and copies ran while one was open for 0% of the time, Pallas kernels for 0%

commit v1 on v0

--- a/solution.py
+++ b/solution.py
@@ -1,11 +1,454 @@
+import functools
 import math
 
 import jax
 import jax.numpy as jnp
+import numpy as np
 from jax import lax
-from jax.sharding import PartitionSpec as P
+from jax.experimental import pallas as pl
+from jax.experimental.pallas import tpu as pltpu
+from jax.sharding import Mesh, PartitionSpec as P
+
 
 HIGHEST = lax.Precision.HIGHEST
+LANES = 128
+SUBLANES = 8
+EAST_RADIX = 8
+ROW_STEP = 16
+F32 = jnp.float32
+BF16 = jnp.bfloat16
+ANY = pl.ANY
+
+
+def cmul_root(value, k, n):
+    re, im = value
+    k = k % n
+    if k == 0:
+        return re, im
+    if 4 * k == n:
+        return -im, re
+    if 2 * k == n:
+        return -re, -im
+    half = math.sqrt(0.5)
+    if 8 * k == n:
+        return (re - im) * half, (re + im) * half
+    if 8 * k == 3 * n:
+        return (re + im) * -half, (re - im) * half
+    c = math.cos(2.0 * math.pi * k / n)
+    s = math.sin(2.0 * math.pi * k / n)
+    return re * c - im * s, re * s + im * c
+
+
+def small_dft(values):
+    n = len(values)
+    if n == 1:
+        return values
+    even = small_dft(values[0::2])
+    odd = small_dft(values[1::2])
+    low, high = [], []
+    for k in range(n // 2):
+        er, ei = even[k]
+        tr, ti = cmul_root(odd[k], k, n)
+        low.append((er + tr, ei + ti))
+        high.append((er - tr, ei - ti))
+    return low + high
+
+
+def small_dft_real(values):
+    (r0, _), (r1, i1), (r2, i2), (r3, i3), (r4, _), (r5, i5), (r6, i6), (r7, i7) = values
+    half = math.sqrt(0.5)
+    s0, d0 = r0 + r4, r0 - r4
+    s2, d2 = r2 + r6, i2 - i6
+    s1r, d1r = r1 + r5, r1 - r5
+    s1i, d1i = i1 + i5, i1 - i5
+    s3r, d3r = r3 + r7, r3 - r7
+    s3i, d3i = i3 + i7, i3 - i7
+    p, q = s0 + s2, s1r + s3r
+    e, f = s0 - s2, s1i - s3i
+    g1r, g1i = (d1r - d1i) * half, (d1r + d1i) * half
+    g3r, g3i = (d3r + d3i) * -half, (d3r - d3i) * half
+    t, u = d0 - d2, g1r + g3r
+    v, w = d0 + d2, g1i - g3i
+    return [p + q, t + u, e - f, v - w, p - q, t - u, e + f, v + w]
+
+
+def split_f32(value):
+    high = value.astype(BF16)
+    low = (value - high.astype(F32)).astype(BF16)
+    return high, low
+
+
+def north_tables(north_cells, radix, rows_out, devices):
+    fast = north_cells // radix
+    per_owner = rows_out // radix
+    n2 = np.arange(fast)
+    y2 = np.arange(devices)[:, None] * per_owner + np.arange(per_owner)[None, :]
+    angle = 2.0 * np.pi / fast * ((y2[:, :, None] * n2[None, None, :]) % fast)
+    c, s = np.cos(angle), np.sin(angle)
+    real_rows = np.concatenate([c, -s], axis=2)
+    imag_rows = np.concatenate([s, c], axis=2)
+    matrix = np.concatenate([real_rows, imag_rows], axis=1).reshape(2 * fast, 2 * fast)
+    matrix = matrix.astype(np.float32)
+    high = matrix.astype(BF16)
+    low = (matrix - high.astype(np.float32)).astype(BF16)
+    turn = 2.0 * np.pi / north_cells * (np.arange(radix)[:, None] * n2[None, :])
+    twiddle = np.stack([np.cos(turn), np.sin(turn)]).astype(np.float32)
+    return np.stack([high, low]), twiddle
+
+
+def north_kernel(
+    wind, radix, east_cells, north_cells, steps,
+    place_ref, cut_ref, vort_ref, div_ref, matrix_ref, twiddle_ref, *rest,
+):
+    *out_refs, cut_rows, g_high, g_low = rest
+    step = pl.program_id(0)
+    waves = cut_ref.shape[1]
+    fast = north_cells // radix
+    block_rows = vort_ref.shape[2]
+    east_unit = 2.0 * math.pi / east_cells
+    north_unit = 2.0 * math.pi / north_cells
+
+    @pl.when(step == 0)
+    def _():
+        cut_rows[...] = jnp.broadcast_to(cut_ref[...], (LANES, waves)).T
+
+    lane = lax.broadcasted_iota(jnp.int32, (ROW_STEP, LANES), 1)
+    sub = lax.broadcasted_iota(jnp.int32, (ROW_STEP, LANES), 0)
+    for part in range(block_rows // ROW_STEP):
+        local = part * ROW_STEP
+        base = pl.multiple_of(step * block_rows + local, ROW_STEP)
+        cut = cut_rows[pl.ds(base, ROW_STEP), :]
+        wave = place_ref[0] + base + sub
+        kx = east_unit * wave.astype(F32)
+        kx2 = kx * kx
+        weight = jnp.where(wave == 0, 1.0, 2.0).astype(F32)
+        values = []
+        for n1 in range(radix):
+            cols = slice(n1 * fast, (n1 + 1) * fast)
+            index = lane + n1 * fast
+            signed = jnp.where(index < north_cells // 2, index, index - north_cells)
+            ky = north_unit * signed.astype(F32)
+            square = kx2 + ky * ky
+            positive = square > 0
+            keep = (jnp.abs(signed) <= cut) & positive
+            inverse = jnp.where(keep, weight / jnp.where(positive, square, 1.0), 0.0)
+            zr = vort_ref[0, 0, local:local + ROW_STEP, cols]
+            zi = vort_ref[1, 0, local:local + ROW_STEP, cols]
+            dr = div_ref[0, 0, local:local + ROW_STEP, cols]
+            di = div_ref[1, 0, local:local + ROW_STEP, cols]
+            if wind == 0:
+                re, im = kx * di - ky * zi, ky * zr - kx * dr
+            else:
+                re, im = kx * zi + ky * di, -kx * zr - ky * dr
+            values.append((re * inverse, im * inverse))
+        result = small_dft(values)
+        for y1 in range(radix):
+            re, im = result[y1]
+            if y1:
+                c = twiddle_ref[0, y1:y1 + 1, :]
+                s = twiddle_ref[1, y1:y1 + 1, :]
+                re, im = re * c - im * s, re * s + im * c
+            row = pl.multiple_of(y1 * waves + base, ROW_STEP)
+            high, low = split_f32(re)
+            g_high[pl.ds(row, ROW_STEP), 0:fast] = high
+            g_low[pl.ds(row, ROW_STEP), 0:fast] = low
+            high, low = split_f32(im)
+            g_high[pl.ds(row, ROW_STEP), fast:2 * fast] = high
+            g_low[pl.ds(row, ROW_STEP), fast:2 * fast] = low
+
+    @pl.when(step == steps - 1)
+    def _():
+        contract = (((1,), (1,)), ((), ()))
+        dot = functools.partial(lax.dot_general, dimension_numbers=contract, preferred_element_type=F32)
+        height = place_ref[1]
+        planes = len(out_refs) if len(out_refs) > 1 else out_refs[0].shape[1]
+        owners = out_refs[0].shape[0]
+        span = owners * SUBLANES
+
+        def rows_of(kind):
+            return jnp.concatenate(
+                [matrix_ref[kind, pl.ds((height ^ j) * span, span), :] for j in range(planes)], axis=0
+            )
+
+        matrix_high, matrix_low = rows_of(0), rows_of(1)
+        for pair in range(radix // 2):
+            rows = slice(pair * 2 * waves, (pair + 1) * 2 * waves)
+            high = g_high[rows, :]
+            low = g_low[rows, :]
+            product = dot(matrix_high, high) + dot(matrix_high, low) + dot(matrix_low, high)
+            for part in range(2):
+                y1 = 2 * pair + part
+                for j in range(planes):
+                    piece = product[j * span:(j + 1) * span, part * waves:(part + 1) * waves]
+                    piece = piece.reshape(owners, SUBLANES, waves)
+                    if len(out_refs) > 1:
+                        out_refs[j][:, y1] = piece
+                    else:
+                        out_refs[0][:, j, y1] = piece
+
+
+def north_call(place, cut, vort, div, matrix, twiddle, slot, wind, radix, east_cells, planes, owners, apart):
+    waves = vort.shape[2]
+    north_cells = vort.shape[3]
+    steps = 4
+    block_rows = waves // steps
+    fast = north_cells // radix
+    data_spec = pl.BlockSpec((2, 1, block_rows, north_cells), lambda i: (0, slot, i, 0))
+    kernel = functools.partial(north_kernel, wind, radix, east_cells, north_cells, steps)
+    flops = 6 * (2 * fast) ** 2 * radix * waves
+    tile = (radix, SUBLANES, waves)
+    shape = (owners,) + tile if apart else (owners, planes) + tile
+    whole = pl.BlockSpec(shape, lambda i: (0,) * len(shape))
+    out_specs = [whole] * (planes if apart else 1)
+    return pl.pallas_call(
+        kernel,
+        grid=(steps,),
+        in_specs=[
+            pl.BlockSpec(memory_space=pltpu.SMEM),
+            pl.BlockSpec((1, waves), lambda i: (0, 0)),
+            data_spec,
+            data_spec,
+            pl.BlockSpec(matrix.shape, lambda i: (0, 0, 0)),
+            pl.BlockSpec(twiddle.shape, lambda i: (0, 0, 0)),
+        ],
+        out_specs=out_specs,
+        out_shape=[jax.ShapeDtypeStruct(shape, F32)] * len(out_specs),
+        scratch_shapes=[
+            pltpu.VMEM((waves, LANES), jnp.int32),
+            pltpu.VMEM((radix * waves, 2 * fast), BF16),
+            pltpu.VMEM((radix * waves, 2 * fast), BF16),
+        ],
+        compiler_params=pltpu.CompilerParams(dimension_semantics=("arbitrary",)),
+        cost_estimate=pl.CostEstimate(flops=flops, bytes_accessed=6 << 20, transcendentals=0),
+    )(place, cut, vort, div, matrix, twiddle)
+
+
+def east_tables(columns, local_waves, east_cells, height, width):
+    radix = EAST_RADIX
+    span = east_cells // radix
+    lane = jnp.arange(LANES, dtype=jnp.int32)
+    column = (lane % columns) ^ (height * width)
+    base = column * local_waves + (lane // columns) * radix
+    wave = jnp.arange(radix, dtype=jnp.int32)[:, None] + base[None, :]
+    steps = wave[:, :, None] * jnp.arange(span, dtype=jnp.int32)[None, None, :] % east_cells
+    angle = 2.0 * math.pi / east_cells * steps.astype(F32)
+    kx = (2.0 * math.pi / east_cells * wave.astype(F32))[:, :, None]
+    c, s = jnp.cos(angle), jnp.sin(angle)
+    kc, ks = kx * c, kx * s
+    real_rows = jnp.concatenate([c, s, -ks, kc], axis=2)
+    imag_rows = jnp.concatenate([-s, c, -kc, -ks], axis=2)
+    table = jnp.concatenate([real_rows, imag_rows], axis=1)
+    high = lax.reduce_precision(table, 8, 7)
+    low = (table - high).astype(BF16)
+    return high.astype(BF16), low
+
+
+def east_kernel(slot, slots_local, planes, *refs):
+    level_ref, high_ref, low_ref = refs[:3]
+    got_refs = refs[3:3 + planes]
+    value_ref, slope_ref, h_high, h_low, spectra, grid_out, sems = refs[-7:]
+    step = pl.program_id(0)
+    radix = EAST_RADIX
+    width, groups, packed, lanes = got_refs[0].shape
+    columns = planes * width
+    north_radix = packed // SUBLANES
+    per_owner = SUBLANES // 2
+    rows_out = north_radix * per_owner
+    span = spectra.shape[2] // 4
+
+    @pl.when(step == 0)
+    def _():
+        lane = lax.broadcasted_iota(jnp.int32, (north_radix, lanes), 1)
+
+        def shuffle(group, carry):
+            for y2 in range(per_owner):
+                for ri in range(2):
+                    slabs = [
+                        got_refs[c // width][c % width, group, pl.ds(ri * per_owner + y2, north_radix, stride=SUBLANES), :]
+                        for c in range(columns)
+                    ]
+                    bit = 1
+                    while bit < columns:
+                        mask = (lane & bit) == 0
+                        for c in range(columns):
+                            if c & bit == 0:
+                                a, b = slabs[c], slabs[c | bit]
+                                slabs[c] = jnp.where(mask, a, pltpu.roll(b, bit, 1))
+                                slabs[c | bit] = jnp.where(mask, pltpu.roll(a, lanes - bit, 1), b)
+                        bit *= 2
+                    row = pl.multiple_of(group * rows_out + y2 * north_radix, north_radix)
+                    for a in range(radix):
+                        high, low = split_f32(slabs[a])
+                        h_high[a, pl.ds(row, north_radix), ri * lanes:(ri + 1) * lanes] = high
+                        h_low[a, pl.ds(row, north_radix), ri * lanes:(ri + 1) * lanes] = low
+            return carry
+
+        lax.fori_loop(0, groups, shuffle, 0)
+
+    dot = functools.partial(jnp.dot, preferred_element_type=F32)
+    left, left_low = h_high[step], h_low[step]
+    spectra[step] = dot(left, high_ref[0]) + dot(left_low, high_ref[0]) + dot(left, low_ref[0])
+
+    @pl.when(step == radix - 1)
+    def _():
+        copies = []
+        for group in range(groups):
+            level = level_ref[group * slots_local + slot]
+            for kind in range(2):
+
+                def combine(block, carry, group=group, kind=kind):
+                    row = pl.multiple_of(group * rows_out + block * SUBLANES, SUBLANES)
+                    for tile in range(span // LANES):
+                        first = 2 * kind * span + tile * LANES
+                        values = [
+                            (
+                                spectra[a, pl.ds(row, SUBLANES), first:first + LANES],
+                                spectra[a, pl.ds(row, SUBLANES), first + span:first + span + LANES],
+                            )
+                            for a in range(radix)
+                        ]
+                        outs = small_dft_real(values)
+                        for x1 in range(radix):
+                            at = x1 * span + tile * LANES
+                            grid_out[kind, pl.ds(row, SUBLANES), at:at + LANES] = outs[x1]
+                    return carry
+
+                lax.fori_loop(0, rows_out // SUBLANES, combine, 0, unroll=2)
+                target = value_ref if kind == 0 else slope_ref
+                copy = pltpu.make_async_copy(
+                    grid_out.at[kind, pl.ds(group * rows_out, rows_out), :],
+                    target.at[level],
+                    sems.at[2 * group + kind],
+                )
+                copy.start()
+                copies.append(copy)
+        for copy in copies:
+            copy.wait()
+
+
+def east_call(levels, got, high, low, slot, slots_local, east_cells, previous):
+    planes = len(got)
+    width, groups, packed, lanes = got[0][0].shape[0], got[0][0].shape[1], *got[0][0].shape[-2:]
+    rows_out = packed // 2
+    radix = EAST_RADIX
+    level_count = levels.shape[0]
+    out = jax.ShapeDtypeStruct((level_count, rows_out, east_cells), F32)
+    in_specs = [
+        pl.BlockSpec(memory_space=pltpu.SMEM),
+        pl.BlockSpec((1,) + high.shape[1:], lambda i: (i, 0, 0)),
+        pl.BlockSpec((1,) + low.shape[1:], lambda i: (i, 0, 0)),
+    ]
+    operands = [levels, high, low]
+    for array, plane in got:
+        if plane is None:
+            in_specs.append(pl.BlockSpec(array.shape, lambda i: (0, 0, 0, 0)))
+        else:
+            in_specs.append(
+                pl.BlockSpec((width, groups, None, packed, lanes), lambda i, plane=plane: (0, 0, plane, 0, 0))
+            )
+        operands.append(array)
+    aliases = {}
+    if previous is not None:
+        aliases = {len(operands): 0, len(operands) + 1: 1}
+        in_specs += [pl.BlockSpec(memory_space=ANY)] * 2
+        operands += list(previous)
+    rows = groups * rows_out
+    return pl.pallas_call(
+        functools.partial(east_kernel, slot, slots_local, planes),
+        grid=(radix,),
+        in_specs=in_specs,
+        out_specs=[pl.BlockSpec(memory_space=ANY)] * 2,
+        out_shape=[out, out],
+        scratch_shapes=[
+            pltpu.VMEM((radix, rows, 2 * lanes), BF16),
+            pltpu.VMEM((radix, rows, 2 * lanes), BF16),
+            pltpu.VMEM((radix, rows, high.shape[2]), F32),
+            pltpu.VMEM((2, rows, east_cells), F32),
+            pltpu.SemaphoreType.DMA((2 * groups,)),
+        ],
+        input_output_aliases=aliases,
+        compiler_params=pltpu.CompilerParams(dimension_semantics=("arbitrary",)),
+        cost_estimate=pl.CostEstimate(
+            flops=6 * radix * rows * high.shape[1] * high.shape[2], bytes_accessed=14 << 20, transcendentals=0
+        ),
+    )(*operands)
+
+
+def fast_shapes(mesh, vorticity):
+    columns = mesh.shape["height"] * mesh.shape["width"]
+    groups = mesh.shape["row"]
+    waves = vorticity.shape[2]
+    north_cells = vorticity.shape[3]
+    rows_out = north_cells // (columns * groups)
+    radix = rows_out // (SUBLANES // 2)
+    return (
+        waves == LANES
+        and columns == EAST_RADIX
+        and radix >= 2
+        and radix & (radix - 1) == 0
+        and north_cells == radix * LANES
+    )
+
+
+def fast_on_device(*args):
+    return fast_body(*args)
+
+
+def fast_body(vorticity, divergence, trunc_cut, level_slot):
+    planes = lax.axis_size("height")
+    width = lax.axis_size("width")
+    groups = lax.axis_size("row")
+    columns = planes * width
+    slots_local = vorticity.shape[1]
+    waves = vorticity.shape[2]
+    north_cells = vorticity.shape[3]
+    east_cells = 2 * waves * columns
+    rows_out = north_cells // (columns * groups)
+    radix = rows_out // (SUBLANES // 2)
+    height = lax.axis_index("height").astype(jnp.int32)
+    column = height * width + lax.axis_index("width")
+    place = jnp.stack([column * waves, height]).astype(jnp.int32)
+    matrix, twiddle = north_tables(north_cells, radix, rows_out, columns * groups)
+    cut = trunc_cut.reshape(1, waves)
+    packed = radix * SUBLANES
+    swaps = [[(z, z ^ j) for z in range(planes)] for j in range(planes)]
+    order = list(range(planes - 1, 0, -1))
+
+    def north(slot, wind, apart):
+        return north_call(
+            place, cut, vorticity, divergence, matrix, twiddle, slot, wind, radix, east_cells,
+            planes, width * groups, apart,
+        )
+
+    def swap(parts):
+        got = {0: parts[0]}
+        for j in order:
+            got[j] = lax.ppermute(parts[j], "height", swaps[j])
+        return got
+
+    def around(block):
+        return lax.all_to_all(block, ("width", "row"), split_axis=0, concat_axis=0, tiled=True)
+
+    chunks = [(slot, wind) for slot in range(slots_local) for wind in range(2)]
+    high, low = east_tables(columns, waves, east_cells, height, width)
+    outputs = [None, None]
+    ready = []
+    for at, (slot, wind) in enumerate(chunks):
+        if at == 0:
+            swapped = swap(north(slot, wind, True))
+            block = jnp.stack([swapped[j] for j in range(planes)], axis=1)
+            block = around(block).reshape(width, groups, planes, packed, waves)
+            ready.append([(block, j) for j in range(planes)])
+        else:
+            block = around(north(slot, wind, False)[0])
+            swapped = swap([block[:, j] for j in range(planes)])
+            ready.append([(swapped[j].reshape(width, groups, packed, waves), None) for j in range(planes)])
+    for at in [1, 0] + list(range(2, len(chunks))):
+        slot, wind = chunks[at]
+        outputs[wind] = east_call(
+            level_slot, ready[at], high, low, slot, slots_local, east_cells, outputs[wind]
+        )
+    return (outputs[0][0], outputs[1][0], outputs[0][1], outputs[1][1])
 
 
 def spectral_winds(vorticity, divergence, trunc_cut, first_wave, east_cells):
@@ -102,7 +545,7 @@
     return jnp.einsum("ls,fasyx->falyx", selector, grid_all, precision=HIGHEST)
 
 
-def on_device(vorticity, divergence, trunc_cut, level_slot):
+def plain_on_device(vorticity, divergence, trunc_cut, level_slot):
     columns = lax.axis_size("col")
     row_count = lax.axis_size("row")
     local_waves = vorticity.shape[2]
@@ -128,15 +571,24 @@
 
 
 def solution(mesh):
-    return jax.shard_map(
-        on_device,
-        mesh=mesh,
-        in_specs=(P(None, "row", "col", None), P(None, "row", "col", None), P("col"), P()),
-        out_specs=(
-            P(None, ("col", "row"), None),
-            P(None, ("col", "row"), None),
-            P(None, ("col", "row"), None),
-            P(None, ("col", "row"), None),
-        ),
-        check_vma=False,
-    )
+    columns = mesh.shape["col"]
+    groups = mesh.shape["row"]
+    width = 2 if columns % 2 == 0 else 1
+    fine = Mesh(mesh.devices.reshape(columns // width, width, groups), ("height", "width", "row"))
+
+    def whole(vorticity, divergence, trunc_cut, level_slot):
+        waves = vorticity.shape[2] // columns
+        local = jax.ShapeDtypeStruct((2, vorticity.shape[1] // groups, waves, vorticity.shape[3]), F32)
+        fast = fast_shapes(fine, local)
+        column = ("height", "width") if fast else "col"
+        grid = P(None, ("height", "width", "row") if fast else ("col", "row"), None)
+        spectral = P(None, "row", column, None)
+        return jax.shard_map(
+            fast_on_device if fast else plain_on_device,
+            mesh=fine if fast else mesh,
+            in_specs=(spectral, spectral, P(column), P()),
+            out_specs=(grid, grid, grid, grid),
+            check_vma=False,
+        )(vorticity, divergence, trunc_cut, level_slot)
+
+    return whole

time: 824 us -> 296 us (0.36)
  matrix products: 417 us -> 0 us
  local copies, waits for them, and re-layouts: 119 us -> 13.2 us
  waiting for transfers between devices: 188 us -> 89.4 us
  starting transfers between devices: 6.13 us -> 93.7 us
  Pallas kernels: 0 us -> 85.1 us
  other arithmetic: 61.3 us -> 10.6 us
  loops' own time: 27.3 us -> 0 us
    dot_general x25 -> x0, matrix products: 417 us -> none  [the longest x8 145 us: north_one_block(): jnp.einsum('yn,lkn->lyk', sine_table, flattened, precision=HIGHEST)]
    all_to_all x1 -> x4, waiting for transfers between devices: 188 us -> 35.7 us  [around(): lax.all_to_all(block, ('width', 'row'), split_axis=0, concat_axis=0, tile...]
    pallas_call x0 -> x8, Pallas kernels: none -> 85.1 us  [the longest x4 59.5 us: east_call(): pl.pallas_call(functools.partial(east_kernel, slot, slots_local, planes),...]
    ppermute x0 -> x12, starting transfers between devices: none -> 75.3 us  [swap(): got[j] = lax.ppermute(parts[j], 'height', swaps[j])]
    ppermute x0 -> x12, waiting for transfers between devices: none -> 53.7 us  [swap(): got[j] = lax.ppermute(parts[j], 'height', swaps[j])]
    mul x22 -> x2, other arithmetic: 39.3 us -> 4.47 us  [the longest x1 4.46 us: east_tables(): kc, ks = (kx * c, kx * s)]
    another operation x2 -> x0, loops' own time: 27.3 us -> none  [the longest x1 26.5 us: north_transform(): return lax.fori_loop(0, block_count, north_one_block, initial)]
    while x16 -> x0, local copies, waits for them, and re-layouts: 23.4 us -> none
  transfers between devices with their start and end apart: 1 -> 16, of which waited for: 1 -> 6; matrix products, arithmetic and copies ran while one was open for 0% -> 5% of each run, Pallas kernels for 0% -> 22%
where the time goes in v1:
time: 296 us; the launch traced here: 293 us
  starting transfers between devices  93.7 us (32%)
  waiting for transfers between devices  89.4 us (30%)
  Pallas kernels  85.1 us (29%)
  local copies, waits for them, and re-layouts  13.2 us (4%)
  other arithmetic  10.6 us (4%)
    ppermute x12, starting transfers between devices, swap(): got[j] = lax.ppermute(parts[j], 'height', swaps[j])  75.3 us
    pallas_call x4, Pallas kernels, east_call(): pl.pallas_call(functools.partial(east_kernel, slot, slots_local, planes),...  59.5 us
    ppermute x12, waiting for transfers between devices, swap(): got[j] = lax.ppermute(parts[j], 'height', swaps[j])  53.7 us
    all_to_all x4, waiting for transfers between devices, around(): lax.all_to_all(block, ('width', 'row'), split_axis=0, concat_axis=0, tile...  35.7 us
    pallas_call x4, Pallas kernels, north_call(): pl.pallas_call(kernel, grid=(steps,), in_specs=[pl.BlockSpec(memory_space...  25.6 us
    all_to_all x4, starting transfers between devices, around(): lax.all_to_all(block, ('width', 'row'), split_axis=0, concat_axis=0, tile...  18.4 us
    unnamed x26, local copies, waits for them, and re-layouts  7.84 us
  transfers between devices with their start and end apart: 16, of which 6 were waited for; matrix products, arithmetic and copies ran while one was open for 5% of the time, Pallas kernels for 22%

profile of v1, /device:TPU:6, one launch (start us, length us, event | category | flops | bytes accessed | tf_op | source)
XLA Modules:
  0.0 293.0 jit_solution(12518806752254899787)
XLA Ops:
  0.6 0.7 pad_add_fusion.place_ref
  1.3 6.4 %shard_map.98 = f32[8,4,16,8,128]{4,3,2,1,0:T(8,128)} custom-call(s32[2]{0:T(128)} %pad_add_fusion.place_ref, s32[1,128]{1,0:T(1,128)} %bitcast.54, f32[2,2,128,2048]{3,2,1,0:T(8,128)} %vort_ref.7, f32[2,2,128,2048]{3,2,1,0:T(8,128)} %div_ref.7, bf16[2,256,256]{2,1,0:T(8,128)(2,1)} %constant.68.clone.matrix_ref, f32[2,16,128]{2,1,0:T(8,128)} %constant.69.clone.twiddle_ref), custom_call_target="tpu_custom_call" | custom-call | flops 805306368 | bytes 6291456 | tf_op jit(solution)/shard_map/pallas_call | solution.py:203
  7.7 4.2 %all-to-all-start.3 = ((f32[8,4,16,8,128]{4,3,2,1,0:T(8,128)}), f32[8,4,16,8,128]{4,3,2,1,0:T(8,128)S(1)}, u32[]{:S(2)}, u32[]{:S(2)}) async-start(f32[8,4,16,8,128]{4,3,2,1,0:T(8,128)} %shard_map.98), calls=%async_computation.3 | async-start | bytes 4194304 | tf_op jit(solution)/shard_map/all_to_all | solution.py:430
  11.9 6.4 %shard_map.97 = f32[8,4,16,8,128]{4,3,2,1,0:T(8,128)} custom-call(s32[2]{0:T(128)} %pad_add_fusion.place_ref, s32[1,128]{1,0:T(1,128)} %bitcast.55, f32[2,2,128,2048]{3,2,1,0:T(8,128)} %vort_ref.7, f32[2,2,128,2048]{3,2,1,0:T(8,128)} %div_ref.7, bf16[2,256,256]{2,1,0:T(8,128)(2,1)} %constant.68.clone.matrix_ref, f32[2,16,128]{2,1,0:T(8,128)} %constant.69.clone.twiddle_ref), custom_call_target="tpu_custom_call" | custom-call | flops 805306368 | bytes 6291456 | tf_op jit(solution)/shard_map/pallas_call | solution.py:203
  18.3 17.9 %all-to-all-done.3 = f32[8,4,16,8,128]{4,3,2,1,0:T(8,128)S(1)} async-done(((f32[8,4,16,8,128]{4,3,2,1,0:T(8,128)}), f32[8,4,16,8,128]{4,3,2,1,0:T(8,128)S(1)}, u32[]{:S(2)}, u32[]{:S(2)}) %all-to-all-start.3) | async-done | bytes 2097184 | tf_op jit(solution)/shard_map/all_to_all | solution.py:430
  36.1 1.3 copy-done.5
  37.4 5.0 %all-to-all-start.2 = ((f32[8,4,16,8,128]{4,3,2,1,0:T(8,128)}), f32[8,4,16,8,128]{4,3,2,1,0:T(8,128)S(1)}, u32[]{:S(2)}, u32[]{:S(2)}) async-start(f32[8,4,16,8,128]{4,3,2,1,0:T(8,128)} %shard_map.97), calls=%async_computation.2 | async-start | bytes 4194304 | tf_op jit(solution)/shard_map/all_to_all | solution.py:430
  42.4 6.4 %shard_map.93 = f32[8,4,16,8,128]{4,3,2,1,0:T(8,128)} custom-call(s32[2]{0:T(128)} %pad_add_fusion.place_ref, s32[1,128]{1,0:T(1,128)} %bitcast.56, f32[2,2,128,2048]{3,2,1,0:T(8,128)} %vort_ref.7, f32[2,2,128,2048]{3,2,1,0:T(8,128)} %div_ref.7, bf16[2,256,256]{2,1,0:T(8,128)(2,1)} %constant.68.clone.matrix_ref, f32[2,16,128]{2,1,0:T(8,128)} %constant.69.clone.twiddle_ref), custom_call_target="tpu_custom_call" | custom-call | flops 805306368 | bytes 6291456 | tf_op jit(solution)/shard_map/pallas_call | solution.py:203
  48.8 17.8 %all-to-all-done.2 = f32[8,4,16,8,128]{4,3,2,1,0:T(8,128)S(1)} async-done(((f32[8,4,16,8,128]{4,3,2,1,0:T(8,128)}), f32[8,4,16,8,128]{4,3,2,1,0:T(8,128)S(1)}, u32[]{:S(2)}, u32[]{:S(2)}) %all-to-all-start.2) | async-done | bytes 2097184 | tf_op jit(solution)/shard_map/all_to_all | solution.py:430
  66.7 1.3 copy-done.3
  68.0 5.0 %all-to-all-start = ((f32[8,4,16,8,128]{4,3,2,1,0:T(8,128)}), f32[8,4,16,8,128]{4,3,2,1,0:T(8,128)S(1)}, u32[]{:S(2)}, u32[]{:S(2)}) async-start(f32[8,4,16,8,128]{4,3,2,1,0:T(8,128)} %shard_map.93), calls=%async_computation | async-start | bytes 4194304 | tf_op jit(solution)/shard_map/all_to_all | solution.py:430
  73.0 6.4 %shard_map.94 = (f32[8,16,8,128]{3,2,1,0:T(8,128)}, f32[8,16,8,128]{3,2,1,0:T(8,128)}, f32[8,16,8,128]{3,2,1,0:T(8,128)}, f32[8,16,8,128]{3,2,1,0:T(8,128)}) custom-call(s32[2]{0:T(128)} %pad_add_fusion.place_ref, s32[1,128]{1,0:T(1,128)} %bitcast.57, f32[2,2,128,2048]{3,2,1,0:T(8,128)} %vort_ref.7, f32[2,2,128,2048]{3,2,1,0:T(8,128)} %div_ref.7, ...), custom_call_target="tpu_custom_call" | custom-call | flops 805306368 | bytes 6291456 | tf_op jit(solution)/shard_map/pallas_call | solution.py:203
  79.4 1.6 collective-permute-start.3
  81.0 2.6 collective-permute-start.4
  83.6 0.2 collective-permute-start.5
  83.9 20.4 %collective-permute-done.3 = f32[8,16,8,128]{3,2,1,0:T(8,128)S(1)} collective-permute-done((f32[8,16,8,128]{3,2,1,0:T(8,128)}, f32[8,16,8,128]{3,2,1,0:T(8,128)S(1)}, u32[]{:S(2)}, u32[]{:S(2)}) %collective-permute-start.3) | collective-permute-done | bytes 524320 | tf_op jit(solution)/shard_map/ppermute | solution.py:426
  104.2 15.2 %collective-permute-done.4 = f32[8,16,8,128]{3,2,1,0:T(8,128)S(1)} collective-permute-done((f32[8,16,8,128]{3,2,1,0:T(8,128)}, f32[8,16,8,128]{3,2,1,0:T(8,128)S(1)}, u32[]{:S(2)}, u32[]{:S(2)}) %collective-permute-start.4) | collective-permute-done | bytes 524320 | tf_op jit(solution)/shard_map/ppermute | solution.py:426
  119.4 0.0 collective-permute-done.5
  119.4 1.2 pad_maximum_fusion
  120.6 1.5 copy.15
  122.1 0.0 all-to-all-done
  122.1 1.3 copy-done.1
  123.4 4.2 %all-to-all-start.1 = ((f32[8,4,16,8,128]{4,3,2,1,0:T(8,128)}), f32[8,4,16,8,128]{4,3,2,1,0:T(8,128)S(1)}, u32[]{:S(2)}, u32[]{:S(2)}) async-start(f32[8,4,16,8,128]{4,3,2,1,0:T(8,128)} %copy.15), calls=%async_computation.1 | async-start | bytes 4194304 | tf_op jit(solution)/shard_map/all_to_all | solution.py:430
  127.6 4.5 %broadcast_multiply_fusion = (f32[8,128,256]{2,1,0:T(8,128)S(1)}, f32[8,128,256]{2,1,0:T(8,128)S(1)}, f32[8,128,256]{2,1,0:T(8,128)S(1)}, f32[8,128,256]{2,1,0:T...) fusion(f32[8,128]{1,0:T(8,128)S(1)} %convert_multiply_fusion, s32[8,128]{1,0:T(8,128)S(1)} %iota_add_fusion), kind=kLoop, calls=%fused_computation.24 | loop fusion | flops 4980736 | bytes 6299648 | tf_op jit(solution)/shard_map/mul | solution.py:237
  132.1 0.0 copy-start.6
  132.1 4.2 %fusion = (bf16[8,256,1024]{2,1,0:T(8,128)(2,1)}, bf16[8,256,1024]{2,1,0:T(8,128)(2,1)}) fusion(f32[8,128,256]{2,1,0:T(8,128)S(1)} %get-tuple-element.44, f32[8,128,256]{2,1,0:T(8,128)S(1)} %get-tuple-element.43, f32[8,128,256]{2,1,0:T(8,128)S(1)} %get-tuple-element.47, f32[8,128,256]{2,1,0:T(8,128)S(1)} %get-tuple-element.46, ...), kind=kLoop, calls=%fused_computation.2 | loop fusion | flops 23068672 | bytes 14680064 | tf_op jit(solution)/shard_map/convert_element_type | solution.py:242
  136.4 1.2 slice_bitcast_fusion
  137.6 2.5 collective-permute-start.11
  140.0 9.7 %collective-permute-start.10 = (f32[8,16,8,128]{3,2,1,0:T(8,128)}, f32[8,16,8,128]{3,2,1,0:T(8,128)}, u32[]{:S(2)}, u32[]{:S(2)}) collective-permute-start(f32[8,16,8,128]{3,2,1,0:T(8,128)} %get-tuple-element.31), channel_id=1, source_target_pairs={{0,16},{8,24},{16,0},{24,8},{1,17},{9,25},{17,1},{25,9},{2,18},{10... | collective-permute-start | bytes 1572872 | tf_op jit(solution)/shard_map/ppermute | solution.py:426
  149.7 0.1 collective-permute-start.9
  149.9 1.3 slice_bitcast_fusion.3
  151.2 2.4 collective-permute-start.8
  153.5 1.0 collective-permute-start.7
  154.6 1.4 slice_bitcast_fusion.6
  156.0 0.8 copy-done.12
  156.8 21.1 %collective-permute-start.6 = (f32[8,16,8,128]{3,2,1,0:T(8,128)}, f32[8,16,8,128]{3,2,1,0:T(8,128)}, u32[]{:S(2)}, u32[]{:S(2)}) collective-permute-start(f32[8,16,8,128]{3,2,1,0:T(8,128)} %get-tuple-element.36), channel_id=1, source_target_pairs={{0,8},{8,0},{16,24},{24,16},{1,9},{9,1},{17,25},{25,17},{2,10},{10... | collective-permute-start | bytes 1572872 | tf_op jit(solution)/shard_map/ppermute | solution.py:426
  177.9 1.3 copy-done
  179.2 14.9 %shard_map.95 = (f32[8,64,2048]{2,1,0:T(8,128)}, f32[8,64,2048]{2,1,0:T(8,128)}) custom-call(s32[8]{0:T(128)} %refs_0_.7, bf16[8,256,1024]{2,1,0:T(8,128)(2,1)} %get-tuple-element.29.refs_1_, bf16[8,256,1024]{2,1,0:T(8,128)(2,1)} %get-tuple-element.28.refs_2_, f32[2,4,4,128,128]{4,3,2,1,0:T(8,128)} %bitcast.38, f32[2,4,4,128,128]{4,3,2,1,0:T(8,128)} %bitcast.39, ...), custom_call_target="tpu_custom_call" | custom-call | flops 3221225472 | bytes 14680064 | tf_op jit(solution)/shard_map/pallas_call | solution.py:356
  194.1 15.6 %collective-permute-done.10 = f32[8,16,8,128]{3,2,1,0:T(8,128)} collective-permute-done((f32[8,16,8,128]{3,2,1,0:T(8,128)}, f32[8,16,8,128]{3,2,1,0:T(8,128)}, u32[]{:S(2)}, u32[]{:S(2)}) %collective-permute-start.10) | collective-permute-done | bytes 524320 | tf_op jit(solution)/shard_map/ppermute | solution.py:426
  209.7 2.5 collective-permute-start.2
  212.2 31.7 %collective-permute-start = (f32[8,16,8,128]{3,2,1,0:T(8,128)}, f32[8,16,8,128]{3,2,1,0:T(8,128)S(1)}, u32[]{:S(2)}, u32[]{:S(2)}) collective-permute-start(f32[8,16,8,128]{3,2,1,0:T(8,128)} %get-tuple-element.40), channel_id=1, source_target_pairs={{0,8},{8,0},{16,24},{24,16},{1,9},{9,1},{17,25},{25,17},{2,10},{10... | collective-permute-start | bytes 1572872 | tf_op jit(solution)/shard_map/ppermute | solution.py:426
  243.9 14.9 %shard_map.99 = (f32[8,64,2048]{2,1,0:T(8,128)}, f32[8,64,2048]{2,1,0:T(8,128)}) custom-call(s32[8]{0:T(128)} %refs_0_.7, bf16[8,256,1024]{2,1,0:T(8,128)(2,1)} %get-tuple-element.29.refs_1_, bf16[8,256,1024]{2,1,0:T(8,128)(2,1)} %get-tuple-element.28.refs_2_, f32[2,4,128,128]{3,2,1,0:T(8,128)} %bitcast.49, f32[2,4,128,128]{3,2,1,0:T(8,128)} %bitcast.24.refs_4_, ...), custom_call_target="tpu_custom_call" | custom-call | flops 3221225472 | bytes 14680064 | tf_op jit(solution)/shard_map/pallas_call | solution.py:356
  258.8 0.8 copy-done.8
  259.6 14.9 %shard_map.100 = (f32[8,64,2048]{2,1,0:T(8,128)}, f32[8,64,2048]{2,1,0:T(8,128)}) custom-call(s32[8]{0:T(128)} %refs_0_.7, bf16[8,256,1024]{2,1,0:T(8,128)(2,1)} %get-tuple-element.29.refs_1_, bf16[8,256,1024]{2,1,0:T(8,128)(2,1)} %get-tuple-element.28.refs_2_, f32[2,4,128,128]{3,2,1,0:T(8,128)} %bitcast.43, ...), custom_call_target="tpu_custom_call", output_to_operand_aliasing={{0}: (7, {}), {1}: (8, {})} | custom-call | flops 3221225472 | bytes 14680064 | tf_op jit(solution)/shard_map/pallas_call | solution.py:356
  274.5 2.5 collective-permute-done.1
  277.0 0.8 copy-done.10
  277.8 0.2 copy-done.11
  278.0 14.9 %shard_map.96 = (f32[8,64,2048]{2,1,0:T(8,128)}, f32[8,64,2048]{2,1,0:T(8,128)}) custom-call(s32[8]{0:T(128)} %refs_0_.7, bf16[8,256,1024]{2,1,0:T(8,128)(2,1)} %get-tuple-element.29.refs_1_, bf16[8,256,1024]{2,1,0:T(8,128)(2,1)} %get-tuple-element.28.refs_2_, f32[2,4,128,128]{3,2,1,0:T(8,128)} %bitcast.42, ...), custom_call_target="tpu_custom_call", output_to_operand_aliasing={{0}: (7, {}), {1}: (8, {})} | custom-call | flops 3221225472 | bytes 14680064 | tf_op jit(solution)/shard_map/pallas_call | solution.py:356
  (29 shorter events, 0.1 us)
Async XLA Ops:
  7.7 28.4 %all-to-all-start.3 = ((f32[8,4,16,8,128]{4,3,2,1,0:T(8,128)}), f32[8,4,16,8,128]{4,3,2,1,0:T(8,128)S(1)}, u32[]{:S(2)}, u32[]{:S(2)}) async-start(f32[8,4,16,8,128]{4,3,2,1,0:T(8,128)} %shard_map.98), calls=%async_computation.3 | async-start | bytes 4194304 | tf_op jit(solution)/shard_map/all_to_all | solution.py:430
  36.1 1.3 copy-start.5
  37.4 29.2 %all-to-all-start.2 = ((f32[8,4,16,8,128]{4,3,2,1,0:T(8,128)}), f32[8,4,16,8,128]{4,3,2,1,0:T(8,128)S(1)}, u32[]{:S(2)}, u32[]{:S(2)}) async-start(f32[8,4,16,8,128]{4,3,2,1,0:T(8,128)} %shard_map.97), calls=%async_computation.2 | async-start | bytes 4194304 | tf_op jit(solution)/shard_map/all_to_all | solution.py:430
  66.7 1.3 copy-start.3
  68.0 54.1 %all-to-all-start = ((f32[8,4,16,8,128]{4,3,2,1,0:T(8,128)}), f32[8,4,16,8,128]{4,3,2,1,0:T(8,128)S(1)}, u32[]{:S(2)}, u32[]{:S(2)}) async-start(f32[8,4,16,8,128]{4,3,2,1,0:T(8,128)} %shard_map.93), calls=%async_computation | async-start | bytes 4194304 | tf_op jit(solution)/shard_map/all_to_all | solution.py:430
  79.4 24.8 %collective-permute-start.3 = (f32[8,16,8,128]{3,2,1,0:T(8,128)}, f32[8,16,8,128]{3,2,1,0:T(8,128)S(1)}, u32[]{:S(2)}, u32[]{:S(2)}) collective-permute-start(f32[8,16,8,128]{3,2,1,0:T(8,128)} %get-tuple-element.17), channel_id=1, source_target_pairs={{0,8},{8,0},{16,24},{24,16},{1,9},{9,1},{17,25},{25,17},{2,10},{10... | collective-permute-start | bytes 1572872 | tf_op jit(solution)/shard_map/ppermute | solution.py:426
  81.0 38.4 %collective-permute-start.4 = (f32[8,16,8,128]{3,2,1,0:T(8,128)}, f32[8,16,8,128]{3,2,1,0:T(8,128)S(1)}, u32[]{:S(2)}, u32[]{:S(2)}) collective-permute-start(f32[8,16,8,128]{3,2,1,0:T(8,128)} %get-tuple-element.18), channel_id=1, source_target_pairs={{0,16},{8,24},{16,0},{24,8},{1,17},{9,25},{17,1},{25,9},{2,18},{10... | collective-permute-start | bytes 1572872 | tf_op jit(solution)/shard_map/ppermute | solution.py:426
  83.6 35.8 %collective-permute-start.5 = (f32[8,16,8,128]{3,2,1,0:T(8,128)}, f32[8,16,8,128]{3,2,1,0:T(8,128)S(1)}, u32[]{:S(2)}, u32[]{:S(2)}) collective-permute-start(f32[8,16,8,128]{3,2,1,0:T(8,128)} %get-tuple-element.19), channel_id=1, source_target_pairs={{0,24},{8,16},{16,8},{24,0},{1,25},{9,17},{17,9},{25,1},{2,26},{10... | collective-permute-start | bytes 1572872 | tf_op jit(solution)/shard_map/ppermute | solution.py:426
  122.1 1.3 copy-start.1
  123.4 54.4 %all-to-all-start.1 = ((f32[8,4,16,8,128]{4,3,2,1,0:T(8,128)}), f32[8,4,16,8,128]{4,3,2,1,0:T(8,128)S(1)}, u32[]{:S(2)}, u32[]{:S(2)}) async-start(f32[8,4,16,8,128]{4,3,2,1,0:T(8,128)} %copy.15), calls=%async_computation.1 | async-start | bytes 4194304 | tf_op jit(solution)/shard_map/all_to_all | solution.py:430
  132.1 4.2 %copy-start.6 = (f32[8,4,16,8,128]{4,3,2,1,0:T(8,128)S(1)}, f32[8,4,16,8,128]{4,3,2,1,0:T(8,128)}, u32[]{:S(2)}) copy-start(f32[8,4,16,8,128]{4,3,2,1,0:T(8,128)} %copy-done.5) | copy-start | bytes 6291460
  136.3 13.5 %copy-start.4 = (f32[8,4,16,8,128]{4,3,2,1,0:T(8,128)S(1)}, f32[8,4,16,8,128]{4,3,2,1,0:T(8,128)}, u32[]{:S(2)}) copy-start(f32[8,4,16,8,128]{4,3,2,1,0:T(8,128)} %copy-done.3) | copy-start | bytes 6291460
  136.4 18.2 %copy-start.2 = (f32[8,4,16,8,128]{4,3,2,1,0:T(8,128)S(1)}, f32[8,4,16,8,128]{4,3,2,1,0:T(8,128)}, u32[]{:S(2)}) copy-start(f32[8,4,16,8,128]{4,3,2,1,0:T(8,128)} %copy-done.1) | copy-start | bytes 6291460
  137.6 18.4 %collective-permute-start.11 = (f32[8,16,8,128]{3,2,1,0:T(8,128)S(1)}, f32[8,16,8,128]{3,2,1,0:T(8,128)S(1)}, u32[]{:S(2)}, u32[]{:S(2)}) collective-permute-start(f32[8,16,8,128]{3,2,1,0:T(8,128)S(1)} %get-tuple-element.30), channel_id=1, source_target_pairs={{0,24},{8,16},{16,8},{24,0},{1,25},{9,17},{17,9},{25,1},{2,26},{10... | collective-permute-start | bytes 1572872 | tf_op jit(solution)/shard_map/ppermute | solution.py:426
  140.0 69.7 %collective-permute-start.10 = (f32[8,16,8,128]{3,2,1,0:T(8,128)}, f32[8,16,8,128]{3,2,1,0:T(8,128)}, u32[]{:S(2)}, u32[]{:S(2)}) collective-permute-start(f32[8,16,8,128]{3,2,1,0:T(8,128)} %get-tuple-element.31), channel_id=1, source_target_pairs={{0,16},{8,24},{16,0},{24,8},{1,17},{9,25},{17,1},{25,9},{2,18},{10... | collective-permute-start | bytes 1572872 | tf_op jit(solution)/shard_map/ppermute | solution.py:426
  149.7 62.4 %collective-permute-start.9 = (f32[8,16,8,128]{3,2,1,0:T(8,128)}, f32[8,16,8,128]{3,2,1,0:T(8,128)}, u32[]{:S(2)}, u32[]{:S(2)}) collective-permute-start(f32[8,16,8,128]{3,2,1,0:T(8,128)} %get-tuple-element.32), channel_id=1, source_target_pairs={{0,8},{8,0},{16,24},{24,16},{1,9},{9,1},{17,25},{25,17},{2,10},{10... | collective-permute-start | bytes 1572872 | tf_op jit(solution)/shard_map/ppermute | solution.py:426
  151.2 61.0 %collective-permute-start.8 = (f32[8,16,8,128]{3,2,1,0:T(8,128)}, f32[8,16,8,128]{3,2,1,0:T(8,128)S(1)}, u32[]{:S(2)}, u32[]{:S(2)}) collective-permute-start(f32[8,16,8,128]{3,2,1,0:T(8,128)} %get-tuple-element.34), channel_id=1, source_target_pairs={{0,24},{8,16},{16,8},{24,0},{1,25},{9,17},{17,9},{25,1},{2,26},{10... | collective-permute-start | bytes 1572872 | tf_op jit(solution)/shard_map/ppermute | solution.py:426
  153.5 105.2 %collective-permute-start.7 = (f32[8,16,8,128]{3,2,1,0:T(8,128)}, f32[8,16,8,128]{3,2,1,0:T(8,128)S(1)}, u32[]{:S(2)}, u32[]{:S(2)}) collective-permute-start(f32[8,16,8,128]{3,2,1,0:T(8,128)} %get-tuple-element.35), channel_id=1, source_target_pairs={{0,16},{8,24},{16,0},{24,8},{1,17},{9,25},{17,1},{25,9},{2,18},{10... | collective-permute-start | bytes 1572872 | tf_op jit(solution)/shard_map/ppermute | solution.py:426
  156.0 0.8 copy-start.12
  156.8 102.0 %collective-permute-start.6 = (f32[8,16,8,128]{3,2,1,0:T(8,128)}, f32[8,16,8,128]{3,2,1,0:T(8,128)}, u32[]{:S(2)}, u32[]{:S(2)}) collective-permute-start(f32[8,16,8,128]{3,2,1,0:T(8,128)} %get-tuple-element.36), channel_id=1, source_target_pairs={{0,8},{8,0},{16,24},{24,16},{1,9},{9,1},{17,25},{25,17},{2,10},{10... | collective-permute-start | bytes 1572872 | tf_op jit(solution)/shard_map/ppermute | solution.py:426
  177.9 1.3 copy-start
  209.7 64.7 %collective-permute-start.2 = (f32[8,16,8,128]{3,2,1,0:T(8,128)}, f32[8,16,8,128]{3,2,1,0:T(8,128)S(1)}, u32[]{:S(2)}, u32[]{:S(2)}) collective-permute-start(f32[8,16,8,128]{3,2,1,0:T(8,128)} %get-tuple-element.38), channel_id=1, source_target_pairs={{0,24},{8,16},{16,8},{24,0},{1,25},{9,17},{17,9},{25,1},{2,26},{10... | collective-permute-start | bytes 1572872 | tf_op jit(solution)/shard_map/ppermute | solution.py:426
  212.2 64.8 %collective-permute-start.1 = (f32[8,16,8,128]{3,2,1,0:T(8,128)}, f32[8,16,8,128]{3,2,1,0:T(8,128)S(1)}, u32[]{:S(2)}, u32[]{:S(2)}) collective-permute-start(f32[8,16,8,128]{3,2,1,0:T(8,128)} %get-tuple-element.39), channel_id=1, source_target_pairs={{0,16},{8,24},{16,0},{24,8},{1,17},{9,25},{17,1},{25,9},{2,18},{10... | collective-permute-start | bytes 1572872 | tf_op jit(solution)/shard_map/ppermute | solution.py:426
  212.2 46.6 %copy-start.7 = (f32[8,16,8,128]{3,2,1,0:T(8,128)}, f32[8,16,8,128]{3,2,1,0:T(8,128)S(1)}, u32[]{:S(2)}) copy-start(f32[8,16,8,128]{3,2,1,0:T(8,128)S(1)} %collective-permute-done.8) | copy-start | bytes 1572868
  212.2 64.8 %collective-permute-start = (f32[8,16,8,128]{3,2,1,0:T(8,128)}, f32[8,16,8,128]{3,2,1,0:T(8,128)S(1)}, u32[]{:S(2)}, u32[]{:S(2)}) collective-permute-start(f32[8,16,8,128]{3,2,1,0:T(8,128)} %get-tuple-element.40), channel_id=1, source_target_pairs={{0,8},{8,0},{16,24},{24,16},{1,9},{9,1},{17,25},{25,17},{2,10},{10... | collective-permute-start | bytes 1572872 | tf_op jit(solution)/shard_map/ppermute | solution.py:426
  258.8 0.8 copy-start.8
  274.5 2.5 copy-start.9
  277.0 0.8 copy-start.10
  277.0 1.0 copy-start.11

commit v2 on v1

--- a/solution.py
+++ b/solution.py
@@ -14,7 +14,8 @@
 LANES = 128
 SUBLANES = 8
 EAST_RADIX = 8
-ROW_STEP = 16
+CHUNKS = 4
+LAST_PIECES = 2
 F32 = jnp.float32
 BF16 = jnp.bfloat16
 ANY = pl.ANY
@@ -100,7 +101,7 @@
     wind, radix, east_cells, north_cells, steps,
     place_ref, cut_ref, vort_ref, div_ref, matrix_ref, twiddle_ref, *rest,
 ):
-    *out_refs, cut_rows, g_high, g_low = rest
+    *out_refs, cut_rows, winds, g_high, g_low = rest
     step = pl.program_id(0)
     waves = cut_ref.shape[1]
     fast = north_cells // radix
@@ -112,17 +113,17 @@
     def _():
         cut_rows[...] = jnp.broadcast_to(cut_ref[...], (LANES, waves)).T
 
-    lane = lax.broadcasted_iota(jnp.int32, (ROW_STEP, LANES), 1)
-    sub = lax.broadcasted_iota(jnp.int32, (ROW_STEP, LANES), 0)
-    for part in range(block_rows // ROW_STEP):
-        local = part * ROW_STEP
-        base = pl.multiple_of(step * block_rows + local, ROW_STEP)
-        cut = cut_rows[pl.ds(base, ROW_STEP), :]
+    lane = lax.broadcasted_iota(jnp.int32, (SUBLANES, LANES), 1)
+    sub = lax.broadcasted_iota(jnp.int32, (SUBLANES, LANES), 0)
+
+    def wind_rows(part, carry):
+        local = pl.multiple_of(part * SUBLANES, SUBLANES)
+        base = pl.multiple_of(step * block_rows + local, SUBLANES)
+        cut = cut_rows[pl.ds(base, SUBLANES), :]
         wave = place_ref[0] + base + sub
         kx = east_unit * wave.astype(F32)
         kx2 = kx * kx
         weight = jnp.where(wave == 0, 1.0, 2.0).astype(F32)
-        values = []
         for n1 in range(radix):
             cols = slice(n1 * fast, (n1 + 1) * fast)
             index = lane + n1 * fast
@@ -132,29 +133,50 @@
             positive = square > 0
             keep = (jnp.abs(signed) <= cut) & positive
             inverse = jnp.where(keep, weight / jnp.where(positive, square, 1.0), 0.0)
-            zr = vort_ref[0, 0, local:local + ROW_STEP, cols]
-            zi = vort_ref[1, 0, local:local + ROW_STEP, cols]
-            dr = div_ref[0, 0, local:local + ROW_STEP, cols]
-            di = div_ref[1, 0, local:local + ROW_STEP, cols]
+            zr = vort_ref[0, 0, pl.ds(local, SUBLANES), cols]
+            zi = vort_ref[1, 0, pl.ds(local, SUBLANES), cols]
+            dr = div_ref[0, 0, pl.ds(local, SUBLANES), cols]
+            di = div_ref[1, 0, pl.ds(local, SUBLANES), cols]
             if wind == 0:
                 re, im = kx * di - ky * zi, ky * zr - kx * dr
             else:
                 re, im = kx * zi + ky * di, -kx * zr - ky * dr
-            values.append((re * inverse, im * inverse))
-        result = small_dft(values)
-        for y1 in range(radix):
-            re, im = result[y1]
-            if y1:
-                c = twiddle_ref[0, y1:y1 + 1, :]
-                s = twiddle_ref[1, y1:y1 + 1, :]
-                re, im = re * c - im * s, re * s + im * c
-            row = pl.multiple_of(y1 * waves + base, ROW_STEP)
-            high, low = split_f32(re)
-            g_high[pl.ds(row, ROW_STEP), 0:fast] = high
-            g_low[pl.ds(row, ROW_STEP), 0:fast] = low
-            high, low = split_f32(im)
-            g_high[pl.ds(row, ROW_STEP), fast:2 * fast] = high
-            g_low[pl.ds(row, ROW_STEP), fast:2 * fast] = low
+            winds[0, n1, pl.ds(base, SUBLANES), :] = re * inverse
+            winds[1, n1, pl.ds(base, SUBLANES), :] = im * inverse
+        return carry
+
+    lax.fori_loop(0, block_rows // SUBLANES, wind_rows, 0)
+
+    @pl.when(step == steps - 1)
+    def _():
+        column = place_ref[2]
+        stride = EAST_RADIX
+        count = waves // stride
+
+        def transform(t, carry):
+            residue = t ^ column
+            values = []
+            for n1 in range(radix):
+                values.append(
+                    tuple(winds[ri, n1, pl.ds(residue, count, stride=stride), :] for ri in range(2))
+                )
+            result = small_dft(values)
+            for y1 in range(radix):
+                re, im = result[y1]
+                if y1:
+                    c = twiddle_ref[0, y1:y1 + 1, :]
+                    s = twiddle_ref[1, y1:y1 + 1, :]
+                    re, im = re * c - im * s, re * s + im * c
+                row = pl.multiple_of(y1 * waves + t * count, count)
+                high, low = split_f32(re)
+                g_high[pl.ds(row, count), 0:fast] = high
+                g_low[pl.ds(row, count), 0:fast] = low
+                high, low = split_f32(im)
+                g_high[pl.ds(row, count), fast:2 * fast] = high
+                g_low[pl.ds(row, count), fast:2 * fast] = low
+            return carry
+
+        lax.fori_loop(0, stride, transform, 0)
 
     @pl.when(step == steps - 1)
     def _():
@@ -190,7 +212,7 @@
 def north_call(place, cut, vort, div, matrix, twiddle, slot, wind, radix, east_cells, planes, owners, apart):
     waves = vort.shape[2]
     north_cells = vort.shape[3]
-    steps = 4
+    steps = 2
     block_rows = waves // steps
     fast = north_cells // radix
     data_spec = pl.BlockSpec((2, 1, block_rows, north_cells), lambda i: (0, slot, i, 0))
@@ -215,6 +237,7 @@
         out_shape=[jax.ShapeDtypeStruct(shape, F32)] * len(out_specs),
         scratch_shapes=[
             pltpu.VMEM((waves, LANES), jnp.int32),
+            pltpu.VMEM((2, radix, waves, fast), F32),
             pltpu.VMEM((radix * waves, 2 * fast), BF16),
             pltpu.VMEM((radix * waves, 2 * fast), BF16),
         ],
@@ -223,153 +246,182 @@
     )(place, cut, vort, div, matrix, twiddle)
 
 
-def east_tables(columns, local_waves, east_cells, height, width):
+def east_table(local_waves, east_cells):
     radix = EAST_RADIX
     span = east_cells // radix
-    lane = jnp.arange(LANES, dtype=jnp.int32)
-    column = (lane % columns) ^ (height * width)
-    base = column * local_waves + (lane // columns) * radix
-    wave = jnp.arange(radix, dtype=jnp.int32)[:, None] + base[None, :]
+    count = LANES // radix
+    lane = jnp.arange(LANES, dtype=jnp.int32)[None, :]
+    residue = jnp.arange(radix, dtype=jnp.int32)[:, None]
+    wave = ((lane // count) ^ residue) * local_waves + (lane % count) * radix + residue
     steps = wave[:, :, None] * jnp.arange(span, dtype=jnp.int32)[None, None, :] % east_cells
     angle = 2.0 * math.pi / east_cells * steps.astype(F32)
-    kx = (2.0 * math.pi / east_cells * wave.astype(F32))[:, :, None]
-    c, s = jnp.cos(angle), jnp.sin(angle)
-    kc, ks = kx * c, kx * s
-    real_rows = jnp.concatenate([c, s, -ks, kc], axis=2)
-    imag_rows = jnp.concatenate([-s, c, -kc, -ks], axis=2)
-    table = jnp.concatenate([real_rows, imag_rows], axis=1)
-    high = lax.reduce_precision(table, 8, 7)
-    low = (table - high).astype(BF16)
-    return high.astype(BF16), low
-
-
-def east_kernel(slot, slots_local, planes, *refs):
-    level_ref, high_ref, low_ref = refs[:3]
-    got_refs = refs[3:3 + planes]
-    value_ref, slope_ref, h_high, h_low, spectra, grid_out, sems = refs[-7:]
-    step = pl.program_id(0)
+
+    def parts(x):
+        high = lax.reduce_precision(x, 8, 7)
+        return jnp.stack([high.astype(BF16), (x - high).astype(BF16)], axis=1)
+
+    c, s = parts(jnp.cos(angle)), parts(jnp.sin(angle))
+    rows = [jnp.concatenate([c, s], axis=3), jnp.concatenate([-s, c], axis=3)]
+    return jnp.concatenate(rows, axis=2)
+
+
+def east_kernel(slot, slots_local, sources, first_group, east_cells, local_waves, *refs):
+    planes = len(sources)
+    place_ref, level_ref, table_hbm = refs[:3]
+    got_hbm = refs[3:3 + planes]
+    value_ref, slope_ref, got, table, h_high, h_low, spectra, grid_out, got_sems, table_sems, out_sems = refs[-11:]
     radix = EAST_RADIX
-    width, groups, packed, lanes = got_refs[0].shape
+    _, width, groups, packed, lanes = got.shape
     columns = planes * width
     north_radix = packed // SUBLANES
     per_owner = SUBLANES // 2
     rows_out = north_radix * per_owner
-    span = spectra.shape[2] // 4
-
-    @pl.when(step == 0)
-    def _():
-        lane = lax.broadcasted_iota(jnp.int32, (north_radix, lanes), 1)
-
-        def shuffle(group, carry):
-            for y2 in range(per_owner):
-                for ri in range(2):
-                    slabs = [
-                        got_refs[c // width][c % width, group, pl.ds(ri * per_owner + y2, north_radix, stride=SUBLANES), :]
-                        for c in range(columns)
-                    ]
-                    bit = 1
-                    while bit < columns:
-                        mask = (lane & bit) == 0
-                        for c in range(columns):
-                            if c & bit == 0:
-                                a, b = slabs[c], slabs[c | bit]
-                                slabs[c] = jnp.where(mask, a, pltpu.roll(b, bit, 1))
-                                slabs[c | bit] = jnp.where(mask, pltpu.roll(a, lanes - bit, 1), b)
-                        bit *= 2
-                    row = pl.multiple_of(group * rows_out + y2 * north_radix, north_radix)
-                    for a in range(radix):
-                        high, low = split_f32(slabs[a])
-                        h_high[a, pl.ds(row, north_radix), ri * lanes:(ri + 1) * lanes] = high
-                        h_low[a, pl.ds(row, north_radix), ri * lanes:(ri + 1) * lanes] = low
-            return carry
-
-        lax.fori_loop(0, groups, shuffle, 0)
+    span = spectra.shape[3] // 2
+    height = place_ref[1]
+
+    loads = []
+    for j, plane in enumerate(sources):
+        source = got_hbm[j]
+        if plane is not None:
+            source = source.at[:, pl.ds(first_group, groups), plane]
+        copy = pltpu.make_async_copy(source, got.at[height ^ j], got_sems.at[j])
+        copy.start()
+        loads.append(copy)
+
+    def columns_of(a):
+        return slice(0, span if a % (radix // 2) == 0 else 2 * span)
+
+    tables = []
+    for a in range(radix):
+        cols = columns_of(a)
+        copy = pltpu.make_async_copy(
+            table_hbm.at[a, :, :, cols], table.at[a, :, :, cols], table_sems.at[a]
+        )
+        copy.start()
+        tables.append(copy)
+    for copy in loads:
+        copy.wait()
+
+    lane = lax.broadcasted_iota(jnp.int32, (north_radix, lanes), 1)
+    count = lanes // radix
+    group_of = lane // count
+    east_unit = 2.0 * math.pi / east_cells
+    kx = [
+        east_unit * ((group_of ^ a) * local_waves + (lane % count) * radix + a).astype(F32) for a in range(radix)
+    ]
+
+    def shuffle(group, carry):
+        for y2 in range(per_owner):
+            for ri in range(2):
+                slabs = [
+                    got[c // width, c % width, group, pl.ds(ri * per_owner + y2, north_radix, stride=SUBLANES), :]
+                    for c in range(columns)
+                ]
+                bit = 1
+                while bit < columns:
+                    mask = (group_of & bit) == 0
+                    slabs = [jnp.where(mask, slabs[i], slabs[i ^ bit]) for i in range(columns)]
+                    bit *= 2
+                row = pl.multiple_of(group * rows_out + y2 * north_radix, north_radix)
+                for a in range(radix):
+                    sloped = slabs[a] * kx[a]
+                    for kind, value, part in ((0, slabs[a], ri), (1, -sloped if ri else sloped, 1 - ri)):
+                        high, low = split_f32(value)
+                        h_high[kind, a, pl.ds(row, north_radix), part * lanes:(part + 1) * lanes] = high
+                        h_low[kind, a, pl.ds(row, north_radix), part * lanes:(part + 1) * lanes] = low
+        return carry
+
+    lax.fori_loop(0, groups, shuffle, 0)
 
     dot = functools.partial(jnp.dot, preferred_element_type=F32)
-    left, left_low = h_high[step], h_low[step]
-    spectra[step] = dot(left, high_ref[0]) + dot(left_low, high_ref[0]) + dot(left, low_ref[0])
-
-    @pl.when(step == radix - 1)
-    def _():
-        copies = []
-        for group in range(groups):
-            level = level_ref[group * slots_local + slot]
-            for kind in range(2):
-
-                def combine(block, carry, group=group, kind=kind):
-                    row = pl.multiple_of(group * rows_out + block * SUBLANES, SUBLANES)
-                    for tile in range(span // LANES):
-                        first = 2 * kind * span + tile * LANES
-                        values = [
-                            (
-                                spectra[a, pl.ds(row, SUBLANES), first:first + LANES],
-                                spectra[a, pl.ds(row, SUBLANES), first + span:first + span + LANES],
-                            )
-                            for a in range(radix)
-                        ]
-                        outs = small_dft_real(values)
-                        for x1 in range(radix):
-                            at = x1 * span + tile * LANES
-                            grid_out[kind, pl.ds(row, SUBLANES), at:at + LANES] = outs[x1]
-                    return carry
-
-                lax.fori_loop(0, rows_out // SUBLANES, combine, 0, unroll=2)
-                target = value_ref if kind == 0 else slope_ref
-                copy = pltpu.make_async_copy(
-                    grid_out.at[kind, pl.ds(group * rows_out, rows_out), :],
-                    target.at[level],
-                    sems.at[2 * group + kind],
-                )
-                copy.start()
-                copies.append(copy)
-        for copy in copies:
-            copy.wait()
-
-
-def east_call(levels, got, high, low, slot, slots_local, east_cells, previous):
+
+    def multiply(kind, a):
+        cols = columns_of(a)
+        left, left_low = h_high[kind, a], h_low[kind, a]
+        right, right_low = table[a, 0, :, cols], table[a, 1, :, cols]
+        spectra[kind, a, :, cols] = dot(left, right) + dot(left_low, right) + dot(left, right_low)
+
+    def combine(kind, row):
+        for tile in range(span // LANES):
+            first = tile * LANES
+            values = []
+            for a in range(radix):
+                re = spectra[kind, a, row:row + SUBLANES, first:first + LANES]
+                im = None
+                if a % (radix // 2):
+                    im = spectra[kind, a, row:row + SUBLANES, first + span:first + span + LANES]
+                values.append((re, im))
+            outs = small_dft_real(values)
+            for x1 in range(radix):
+                at = x1 * span + first
+                grid_out[kind, row:row + SUBLANES, at:at + LANES] = outs[x1]
+
+    def finish(kind, group):
+        for row in range(group * rows_out, (group + 1) * rows_out, SUBLANES):
+            combine(kind, row)
+        level = level_ref[(first_group + group) * slots_local + slot]
+        copy = pltpu.make_async_copy(
+            grid_out.at[kind, pl.ds(group * rows_out, rows_out), :],
+            (value_ref, slope_ref)[kind].at[level],
+            out_sems.at[2 * group + kind],
+        )
+        copy.start()
+        return copy
+
+    for copy in tables:
+        copy.wait()
+    for a in range(radix):
+        multiply(0, a)
+    copies = []
+    share = radix // groups
+    for group in range(groups):
+        for a in range(group * share, (group + 1) * share):
+            multiply(1, a)
+        copies.append(finish(0, group))
+    for group in range(groups):
+        copies.append(finish(1, group))
+    for copy in copies:
+        copy.wait()
+
+
+def east_call(
+    place, levels, got, table, slot, slots_local, first_group, groups, width, east_cells, local_waves, previous
+):
     planes = len(got)
-    width, groups, packed, lanes = got[0][0].shape[0], got[0][0].shape[1], *got[0][0].shape[-2:]
+    packed, lanes = got[0][0].shape[-2:]
     rows_out = packed // 2
     radix = EAST_RADIX
     level_count = levels.shape[0]
     out = jax.ShapeDtypeStruct((level_count, rows_out, east_cells), F32)
-    in_specs = [
-        pl.BlockSpec(memory_space=pltpu.SMEM),
-        pl.BlockSpec((1,) + high.shape[1:], lambda i: (i, 0, 0)),
-        pl.BlockSpec((1,) + low.shape[1:], lambda i: (i, 0, 0)),
-    ]
-    operands = [levels, high, low]
-    for array, plane in got:
-        if plane is None:
-            in_specs.append(pl.BlockSpec(array.shape, lambda i: (0, 0, 0, 0)))
-        else:
-            in_specs.append(
-                pl.BlockSpec((width, groups, None, packed, lanes), lambda i, plane=plane: (0, 0, plane, 0, 0))
-            )
-        operands.append(array)
+    in_specs = [pl.BlockSpec(memory_space=pltpu.SMEM)] * 2 + [pl.BlockSpec(memory_space=ANY)] * (1 + planes)
+    operands = [place, levels, table] + [array for array, _ in got]
     aliases = {}
     if previous is not None:
         aliases = {len(operands): 0, len(operands) + 1: 1}
         in_specs += [pl.BlockSpec(memory_space=ANY)] * 2
         operands += list(previous)
     rows = groups * rows_out
+    columns = table.shape[-1]
+    sources = tuple(plane for _, plane in got)
     return pl.pallas_call(
-        functools.partial(east_kernel, slot, slots_local, planes),
-        grid=(radix,),
+        functools.partial(east_kernel, slot, slots_local, sources, first_group, east_cells, local_waves),
         in_specs=in_specs,
         out_specs=[pl.BlockSpec(memory_space=ANY)] * 2,
         out_shape=[out, out],
         scratch_shapes=[
-            pltpu.VMEM((radix, rows, 2 * lanes), BF16),
-            pltpu.VMEM((radix, rows, 2 * lanes), BF16),
-            pltpu.VMEM((radix, rows, high.shape[2]), F32),
+            pltpu.VMEM((planes, width, groups, packed, lanes), F32),
+            pltpu.VMEM(table.shape, BF16),
+            pltpu.VMEM((2, radix, rows, 2 * lanes), BF16),
+            pltpu.VMEM((2, radix, rows, 2 * lanes), BF16),
+            pltpu.VMEM((2, radix, rows, columns), F32),
             pltpu.VMEM((2, rows, east_cells), F32),
+            pltpu.SemaphoreType.DMA((planes,)),
+            pltpu.SemaphoreType.DMA((radix,)),
             pltpu.SemaphoreType.DMA((2 * groups,)),
         ],
         input_output_aliases=aliases,
-        compiler_params=pltpu.CompilerParams(dimension_semantics=("arbitrary",)),
         cost_estimate=pl.CostEstimate(
-            flops=6 * radix * rows * high.shape[1] * high.shape[2], bytes_accessed=14 << 20, transcendentals=0
+            flops=12 * radix * rows * 2 * lanes * columns, bytes_accessed=14 << 20, transcendentals=0
         ),
     )(*operands)
 
@@ -387,6 +439,9 @@
         and radix >= 2
         and radix & (radix - 1) == 0
         and north_cells == radix * LANES
+        and groups % LAST_PIECES == 0
+        and EAST_RADIX % groups == 0
+        and vorticity.shape[1] * 2 == CHUNKS
     )
 
 
@@ -407,7 +462,7 @@
     radix = rows_out // (SUBLANES // 2)
     height = lax.axis_index("height").astype(jnp.int32)
     column = height * width + lax.axis_index("width")
-    place = jnp.stack([column * waves, height]).astype(jnp.int32)
+    place = jnp.stack([column * waves, height, column]).astype(jnp.int32)
     matrix, twiddle = north_tables(north_cells, radix, rows_out, columns * groups)
     cut = trunc_cut.reshape(1, waves)
     packed = radix * SUBLANES
@@ -430,23 +485,30 @@
         return lax.all_to_all(block, ("width", "row"), split_axis=0, concat_axis=0, tiled=True)
 
     chunks = [(slot, wind) for slot in range(slots_local) for wind in range(2)]
-    high, low = east_tables(columns, waves, east_cells, height, width)
+    table = east_table(waves, east_cells)
     outputs = [None, None]
     ready = []
+    last = len(chunks) - 1
     for at, (slot, wind) in enumerate(chunks):
         if at == 0:
             swapped = swap(north(slot, wind, True))
             block = jnp.stack([swapped[j] for j in range(planes)], axis=1)
             block = around(block).reshape(width, groups, planes, packed, waves)
-            ready.append([(block, j) for j in range(planes)])
+            ready.append((at, slot, wind, 0, groups, [(block, j) for j in range(planes)]))
         else:
             block = around(north(slot, wind, False)[0])
-            swapped = swap([block[:, j] for j in range(planes)])
-            ready.append([(swapped[j].reshape(width, groups, packed, waves), None) for j in range(planes)])
-    for at in [1, 0] + list(range(2, len(chunks))):
-        slot, wind = chunks[at]
+            block = block.reshape(width, groups, planes, packed, waves)
+            pieces = LAST_PIECES if at == last else 1
+            share = groups // pieces
+            for piece in range(pieces):
+                near = piece * share
+                swapped = swap([block[:, near:near + share, j] for j in range(planes)])
+                got = [(block, 0)] + [(swapped[j], None) for j in range(1, planes)]
+                ready.append((at + piece, slot, wind, near, share, got))
+    ready[0], ready[1] = ready[1], ready[0]
+    for at, slot, wind, near, share, got in ready:
         outputs[wind] = east_call(
-            level_slot, ready[at], high, low, slot, slots_local, east_cells, outputs[wind]
+            place, level_slot, got, table, slot, slots_local, near, share, width, east_cells, waves, outputs[wind]
         )
     return (outputs[0][0], outputs[1][0], outputs[0][1], outputs[1][1])
 

time: 296 us -> 281 us (0.949)
  waiting for transfers between devices: 89.4 us -> 115 us
  starting transfers between devices: 93.7 us -> 72.9 us
  Pallas kernels: 85.1 us -> 66.3 us
    ppermute x12 -> x15, waiting for transfers between devices: 53.7 us -> 80.1 us  [swap(): got[j] = lax.ppermute(parts[j], 'height', swaps[j])]
    ppermute x12 -> x15, starting transfers between devices: 75.3 us -> 53.7 us  [swap(): got[j] = lax.ppermute(parts[j], 'height', swaps[j])]
    pallas_call x4 -> x5, Pallas kernels: 59.5 us -> 40 us  [east_call(): pl.pallas_call(functools.partial(east_kernel, slot, slots_local, sources,...]
    mul x2 -> x0, other arithmetic: 4.47 us -> none  [the longest x1 4.46 us: east_tables(): kc, ks = (kx * c, kx * s)]
    concatenate x0 -> x1, other arithmetic: none -> 3.86 us  [east_table(): return jnp.concatenate(rows, axis=2)]
    unnamed x26 -> x28, local copies, waits for them, and re-layouts: 7.84 us -> 5.78 us
  transfers between devices with their start and end apart: 16 -> 19, of which waited for: 6 -> 7; matrix products, arithmetic and copies ran while one was open for 5% -> 6% of each run, Pallas kernels for 22% -> 18%
where the time goes in v2:
time: 281 us; the launch traced here: 279 us
  waiting for transfers between devices  115 us (41%)
  starting transfers between devices  72.9 us (26%)
  Pallas kernels  66.3 us (24%)
  other arithmetic  11.6 us (4%)
  local copies, waits for them, and re-layouts  11.6 us (4%)
    ppermute x15, waiting for transfers between devices, swap(): got[j] = lax.ppermute(parts[j], 'height', swaps[j])  80.1 us
    ppermute x15, starting transfers between devices, swap(): got[j] = lax.ppermute(parts[j], 'height', swaps[j])  53.7 us
    pallas_call x5, Pallas kernels, east_call(): pl.pallas_call(functools.partial(east_kernel, slot, slots_local, sources,...  40 us
    all_to_all x4, waiting for transfers between devices, around(): lax.all_to_all(block, ('width', 'row'), split_axis=0, concat_axis=0, tile...  35.3 us
    pallas_call x4, Pallas kernels, north_call(): pl.pallas_call(kernel, grid=(steps,), in_specs=[pl.BlockSpec(memory_space...  26.3 us
    all_to_all x4, starting transfers between devices, around(): lax.all_to_all(block, ('width', 'row'), split_axis=0, concat_axis=0, tile...  19.2 us
    convert_element_type x1, other arithmetic, parts(): return jnp.stack([high.astype(BF16), (x - high).astype(BF16)], axis=1)  5.8 us
    unnamed x28, local copies, waits for them, and re-layouts  5.78 us
  transfers between devices with their start and end apart: 19, of which 7 were waited for; matrix products, arithmetic and copies ran while one was open for 6% of the time, Pallas kernels for 18%

profile of v2, /device:TPU:6, one launch (start us, length us, event | category | flops | bytes accessed | tf_op | source)
XLA Modules:
  0.0 278.9 jit_solution(2662599723931869938)
XLA Ops:
  0.6 0.6 pad_add_fusion.place_ref.refs_0_
  1.3 6.6 %shard_map.98 = f32[8,4,16,8,128]{4,3,2,1,0:T(8,128)} custom-call(s32[3]{0:T(128)} %pad_add_fusion.place_ref.refs_0_, s32[1,128]{1,0:T(1,128)} %bitcast.53, f32[2,2,128,2048]{3,2,1,0:T(8,128)} %vort_ref.7, f32[2,2,128,2048]{3,2,1,0:T(8,128)} %div_ref.7, bf16[2,256,256]{2,1,0:T(8,128)(2,1)} %constant.68.clone.matrix_ref, f32[2,16,128]{2,1,0:T(8,128)} %constant.69.clone.twiddle_ref), custom_call_target="tpu_custom_call" | custom-call | flops 805306368 | bytes 6291456 | tf_op jit(solution)/shard_map/pallas_call | solution.py:225
  7.8 4.2 %all-to-all-start.3 = ((f32[8,4,16,8,128]{4,3,2,1,0:T(8,128)}), f32[8,4,16,8,128]{4,3,2,1,0:T(8,128)S(1)}, u32[]{:S(2)}, u32[]{:S(2)}) async-start(f32[8,4,16,8,128]{4,3,2,1,0:T(8,128)} %shard_map.98), calls=%async_computation.3 | async-start | bytes 4194304 | tf_op jit(solution)/shard_map/all_to_all | solution.py:485
  12.0 6.6 %shard_map.97 = f32[8,4,16,8,128]{4,3,2,1,0:T(8,128)} custom-call(s32[3]{0:T(128)} %pad_add_fusion.place_ref.refs_0_, s32[1,128]{1,0:T(1,128)} %bitcast.54, f32[2,2,128,2048]{3,2,1,0:T(8,128)} %vort_ref.7, f32[2,2,128,2048]{3,2,1,0:T(8,128)} %div_ref.7, bf16[2,256,256]{2,1,0:T(8,128)(2,1)} %constant.68.clone.matrix_ref, f32[2,16,128]{2,1,0:T(8,128)} %constant.69.clone.twiddle_ref), custom_call_target="tpu_custom_call" | custom-call | flops 805306368 | bytes 6291456 | tf_op jit(solution)/shard_map/pallas_call | solution.py:225
  18.6 17.7 %all-to-all-done.3 = f32[8,4,16,8,128]{4,3,2,1,0:T(8,128)S(1)} async-done(((f32[8,4,16,8,128]{4,3,2,1,0:T(8,128)}), f32[8,4,16,8,128]{4,3,2,1,0:T(8,128)S(1)}, u32[]{:S(2)}, u32[]{:S(2)}) %all-to-all-start.3) | async-done | bytes 2097184 | tf_op jit(solution)/shard_map/all_to_all | solution.py:485
  36.3 1.4 copy-done.3
  37.7 5.0 %all-to-all-start.2 = ((f32[8,4,16,8,128]{4,3,2,1,0:T(8,128)}), f32[8,4,16,8,128]{4,3,2,1,0:T(8,128)S(1)}, u32[]{:S(2)}, u32[]{:S(2)}) async-start(f32[8,4,16,8,128]{4,3,2,1,0:T(8,128)} %shard_map.97), calls=%async_computation.2 | async-start | bytes 4194304 | tf_op jit(solution)/shard_map/all_to_all | solution.py:485
  42.7 6.6 %shard_map.93 = f32[8,4,16,8,128]{4,3,2,1,0:T(8,128)} custom-call(s32[3]{0:T(128)} %pad_add_fusion.place_ref.refs_0_, s32[1,128]{1,0:T(1,128)} %bitcast.55, f32[2,2,128,2048]{3,2,1,0:T(8,128)} %vort_ref.7, f32[2,2,128,2048]{3,2,1,0:T(8,128)} %div_ref.7, bf16[2,256,256]{2,1,0:T(8,128)(2,1)} %constant.68.clone.matrix_ref, f32[2,16,128]{2,1,0:T(8,128)} %constant.69.clone.twiddle_ref), custom_call_target="tpu_custom_call" | custom-call | flops 805306368 | bytes 6291456 | tf_op jit(solution)/shard_map/pallas_call | solution.py:225
  49.2 17.7 %all-to-all-done.2 = f32[8,4,16,8,128]{4,3,2,1,0:T(8,128)S(1)} async-done(((f32[8,4,16,8,128]{4,3,2,1,0:T(8,128)}), f32[8,4,16,8,128]{4,3,2,1,0:T(8,128)S(1)}, u32[]{:S(2)}, u32[]{:S(2)}) %all-to-all-start.2) | async-done | bytes 2097184 | tf_op jit(solution)/shard_map/all_to_all | solution.py:485
  66.9 5.8 %all-to-all-start = ((f32[8,4,16,8,128]{4,3,2,1,0:T(8,128)}), f32[8,4,16,8,128]{4,3,2,1,0:T(8,128)}, u32[]{:S(2)}, u32[]{:S(2)}) async-start(f32[8,4,16,8,128]{4,3,2,1,0:T(8,128)} %shard_map.93), calls=%async_computation | async-start | bytes 4194304 | tf_op jit(solution)/shard_map/all_to_all | solution.py:485
  72.7 6.6 %shard_map.94 = (f32[8,16,8,128]{3,2,1,0:T(8,128)}, f32[8,16,8,128]{3,2,1,0:T(8,128)}, f32[8,16,8,128]{3,2,1,0:T(8,128)}, f32[8,16,8,128]{3,2,1,0:T(8,128)}) custom-call(s32[3]{0:T(128)} %pad_add_fusion.place_ref.refs_0_, s32[1,128]{1,0:T(1,128)} %bitcast.56, f32[2,2,128,2048]{3,2,1,0:T(8,128)} %vort_ref.7, f32[2,2,128,2048]{3,2,1,0:T(8,128)} %div_ref.7, ...), custom_call_target="tpu_custom_call" | custom-call | flops 805306368 | bytes 6291456 | tf_op jit(solution)/shard_map/pallas_call | solution.py:225
  79.3 1.6 collective-permute-start.3
  80.9 2.6 collective-permute-start.4
  83.5 0.2 collective-permute-start.5
  83.7 5.8 %reduce-precision_convert_fusion = (bf16[8,1,128,256]{3,2,1,0:T(8,128)(2,1)S(1)}, bf16[8,1,128,256]{3,2,1,0:T(8,128)(2,1)S(1)}, bf16[8,1,128,256]{3,2,1,0:T(8,128)(2,1)}, bf16[8,1,128,256]{3,2,1,0:T(8,128)(2,1)}) fusion(s32[8,128]{1,0:T(8,128)S(1)} %iota_add_fusion), kind=kLoop, calls=%fused_computation.6 | loop fusion | flops 5767168 | bytes 2101248 | tf_op jit(solution)/shard_map/convert_element_type | solution.py:261
  89.5 1.1 maximum_negate_fusion
  90.6 13.5 %collective-permute-done.3 = f32[8,16,8,128]{3,2,1,0:T(8,128)S(1)} collective-permute-done((f32[8,16,8,128]{3,2,1,0:T(8,128)}, f32[8,16,8,128]{3,2,1,0:T(8,128)S(1)}, u32[]{:S(2)}, u32[]{:S(2)}) %collective-permute-start.3) | collective-permute-done | bytes 524320 | tf_op jit(solution)/shard_map/ppermute | solution.py:481
  104.1 15.2 %collective-permute-done.4 = f32[8,16,8,128]{3,2,1,0:T(8,128)S(1)} collective-permute-done((f32[8,16,8,128]{3,2,1,0:T(8,128)}, f32[8,16,8,128]{3,2,1,0:T(8,128)S(1)}, u32[]{:S(2)}, u32[]{:S(2)}) %collective-permute-start.4) | collective-permute-done | bytes 524320 | tf_op jit(solution)/shard_map/ppermute | solution.py:481
  119.3 0.2 pad_maximum_fusion
  119.5 1.5 copy.25
  121.0 4.2 %all-to-all-start.1 = ((f32[8,4,16,8,128]{4,3,2,1,0:T(8,128)}), f32[8,4,16,8,128]{4,3,2,1,0:T(8,128)S(1)}, u32[]{:S(2)}, u32[]{:S(2)}) async-start(f32[8,4,16,8,128]{4,3,2,1,0:T(8,128)} %copy.25), calls=%async_computation.1 | async-start | bytes 4194304 | tf_op jit(solution)/shard_map/all_to_all | solution.py:485
  125.2 3.9 %maximum_maximum_fusion.refs_2_ = bf16[8,2,256,512]{3,2,1,0:T(8,128)(2,1)} fusion(bf16[8,1,128,256]{3,2,1,0:T(8,128)(2,1)} %get-tuple-element.46, bf16[8,1,128,256]{3,2,1,0:T(8,128)(2,1)} %get-tuple-element.47, bf16[8,2,128,256]{3,2,1,0:T(8,128)(2,1)} %maximum_negate_fusion, bf16[8,1,128,256]{3,2,1,0:T(8,128)(2,1)S(1)} %get-tuple-element.45, ...), kind=kLoop, calls=%fused_computation | loop fusion | flops 29360128 | bytes 7340032 | tf_op jit(solution)/shard_map/concatenate | solution.py:265
  129.4 2.5 collective-permute-start.14
  131.9 9.7 %collective-permute-start.13 = (f32[2,4,128,128]{3,2,1,0:T(8,128)S(1)}, f32[2,4,128,128]{3,2,1,0:T(8,128)S(1)}, u32[]{:S(2)}, u32[]{:S(2)}) collective-permute-start(f32[2,4,128,128]{3,2,1,0:T(8,128)S(1)} %get-tuple-element.33), channel_id=1, source_target_pairs={{0,16},{8,24},{16,0},{24,8},{1,17},{9,25},{17,1},{25,9},{2,18},{10... | collective-permute-start | bytes 1572872 | tf_op jit(solution)/shard_map/ppermute | solution.py:481
  141.7 0.2 copy.27
  141.9 1.0 slice_bitcast_fusion.6
  142.9 2.4 collective-permute-start.11
  145.3 1.0 collective-permute-start.10
  146.3 1.7 copy.24
  148.0 1.2 slice_bitcast_fusion.3
  149.2 24.9 %collective-permute-done.11.refs_6_ = f32[2,2,128,128]{3,2,1,0:T(8,128)S(1)} collective-permute-done((f32[2,2,128,128]{3,2,1,0:T(8,128)S(1)}, f32[2,2,128,128]{3,2,1,0:T(8,128)S(1)}, u32[]{:S(2)}, u32[]{:S(2)}) %collective-permute-start.11) | collective-permute-done | bytes 262176 | tf_op jit(solution)/shard_map/ppermute | solution.py:481
  174.1 22.2 %collective-permute-start.9 = (f32[2,2,128,128]{3,2,1,0:T(8,128)S(1)}, f32[2,2,128,128]{3,2,1,0:T(8,128)S(1)}, u32[]{:S(2)}, u32[]{:S(2)}) collective-permute-start(f32[2,2,128,128]{3,2,1,0:T(8,128)S(1)} %get-tuple-element.37), channel_id=1, source_target_pairs={{0,8},{8,0},{16,24},{24,16},{1,9},{9,1},{17,25},{25,17},{2,10},{10... | collective-permute-start | bytes 786440 | tf_op jit(solution)/shard_map/ppermute | solution.py:481
  196.4 2.5 collective-permute-start.8
  198.9 0.8 copy-done.12
  199.7 1.2 collective-permute-start.6
  200.9 9.1 %shard_map.99 = (f32[8,64,2048]{2,1,0:T(8,128)}, f32[8,64,2048]{2,1,0:T(8,128)}) custom-call(s32[3]{0:T(128)} %pad_add_fusion.place_ref.refs_0_, s32[8]{0:T(128)} %refs_1_.9, bf16[8,2,256,512]{3,2,1,0:T(8,128)(2,1)} %maximum_maximum_fusion.refs_2_, f32[2,4,4,128,128]{4,3,2,1,0:T(8,128)} %bitcast.45, f32[2,4,128,128]{3,2,1,0:T(8,128)} %copy-done.13, ...), custom_call_target="tpu_custom_call" | custom-call | flops 3221225472 | bytes 14680064 | tf_op jit(solution)/shard_map/pallas_call | solution.py:406
  210.0 0.7 copy-done.9
  210.7 2.5 collective-permute-start.2
  213.1 0.7 copy-done.10
  213.9 5.1 %collective-permute-start = (f32[2,4,128,128]{3,2,1,0:T(8,128)}, f32[2,4,128,128]{3,2,1,0:T(8,128)}, u32[]{:S(2)}, u32[]{:S(2)}) collective-permute-start(f32[2,4,128,128]{3,2,1,0:T(8,128)} %get-tuple-element.43), channel_id=1, source_target_pairs={{0,8},{8,0},{16,24},{24,16},{1,9},{9,1},{17,25},{25,17},{2,10},{10... | collective-permute-start | bytes 1572872 | tf_op jit(solution)/shard_map/ppermute | solution.py:481
  219.0 6.3 %shard_map.100 = (f32[8,64,2048]{2,1,0:T(8,128)}, f32[8,64,2048]{2,1,0:T(8,128)}) custom-call(s32[3]{0:T(128)} %pad_add_fusion.place_ref.refs_0_, s32[8]{0:T(128)} %refs_1_.9, bf16[8,2,256,512]{3,2,1,0:T(8,128)(2,1)} %maximum_maximum_fusion.refs_2_, f32[2,4,4,128,128]{4,3,2,1,0:T(8,128)} %bitcast.43, ...), custom_call_target="tpu_custom_call", output_to_operand_aliasing={{0}: (7, {}), {1}: (8, {})} | custom-call | flops 1610612736 | bytes 14680064 | tf_op jit(solution)/shard_map/pallas_call | solution.py:406
  225.3 21.3 %collective-permute-done.7.refs_5_ = f32[2,2,128,128]{3,2,1,0:T(8,128)} collective-permute-done((f32[2,2,128,128]{3,2,1,0:T(8,128)}, f32[2,2,128,128]{3,2,1,0:T(8,128)}, u32[]{:S(2)}, u32[]{:S(2)}) %collective-permute-start.7) | collective-permute-done | bytes 262176 | tf_op jit(solution)/shard_map/ppermute | solution.py:481
  246.6 6.3 %shard_map.101 = (f32[8,64,2048]{2,1,0:T(8,128)}, f32[8,64,2048]{2,1,0:T(8,128)}) custom-call(s32[3]{0:T(128)} %pad_add_fusion.place_ref.refs_0_, s32[8]{0:T(128)} %refs_1_.9, bf16[8,2,256,512]{3,2,1,0:T(8,128)(2,1)} %maximum_maximum_fusion.refs_2_, f32[2,4,4,128,128]{4,3,2,1,0:T(8,128)} %bitcast.44, ...), custom_call_target="tpu_custom_call", output_to_operand_aliasing={{0}: (7, {}), {1}: (8, {})} | custom-call | flops 1610612736 | bytes 14680064 | tf_op jit(solution)/shard_map/pallas_call | solution.py:406
  252.9 1.4 copy-done
  254.3 9.3 %shard_map.95 = (f32[8,64,2048]{2,1,0:T(8,128)}, f32[8,64,2048]{2,1,0:T(8,128)}) custom-call(s32[3]{0:T(128)} %pad_add_fusion.place_ref.refs_0_, s32[8]{0:T(128)} %refs_1_.9, bf16[8,2,256,512]{3,2,1,0:T(8,128)(2,1)} %maximum_maximum_fusion.refs_2_, f32[2,4,4,128,128]{4,3,2,1,0:T(8,128)} %bitcast.39, f32[2,4,4,128,128]{4,3,2,1,0:T(8,128)} %bitcast.40, ...), custom_call_target="tpu_custom_call" | custom-call | flops 3221225472 | bytes 14680064 | tf_op jit(solution)/shard_map/pallas_call | solution.py:406
  263.6 5.3 %collective-permute-done.1.refs_5_ = f32[2,4,128,128]{3,2,1,0:T(8,128)S(1)} collective-permute-done((f32[2,4,128,128]{3,2,1,0:T(8,128)}, f32[2,4,128,128]{3,2,1,0:T(8,128)S(1)}, u32[]{:S(2)}, u32[]{:S(2)}) %collective-permute-start.1) | collective-permute-done | bytes 524320 | tf_op jit(solution)/shard_map/ppermute | solution.py:481
  268.9 0.8 copy-done.6
  269.6 9.1 %shard_map.96 = (f32[8,64,2048]{2,1,0:T(8,128)}, f32[8,64,2048]{2,1,0:T(8,128)}) custom-call(s32[3]{0:T(128)} %pad_add_fusion.place_ref.refs_0_, s32[8]{0:T(128)} %refs_1_.9, bf16[8,2,256,512]{3,2,1,0:T(8,128)(2,1)} %maximum_maximum_fusion.refs_2_, f32[2,4,4,128,128]{4,3,2,1,0:T(8,128)} %bitcast.5.refs_3_, ...), custom_call_target="tpu_custom_call", output_to_operand_aliasing={{0}: (7, {}), {1}: (8, {})} | custom-call | flops 3221225472 | bytes 14680064 | tf_op jit(solution)/shard_map/pallas_call | solution.py:406
  (41 shorter events, 0.6 us)
Async XLA Ops:
  7.8 28.4 %all-to-all-start.3 = ((f32[8,4,16,8,128]{4,3,2,1,0:T(8,128)}), f32[8,4,16,8,128]{4,3,2,1,0:T(8,128)S(1)}, u32[]{:S(2)}, u32[]{:S(2)}) async-start(f32[8,4,16,8,128]{4,3,2,1,0:T(8,128)} %shard_map.98), calls=%async_computation.3 | async-start | bytes 4194304 | tf_op jit(solution)/shard_map/all_to_all | solution.py:485
  36.3 1.4 copy-start.3
  37.7 29.2 %all-to-all-start.2 = ((f32[8,4,16,8,128]{4,3,2,1,0:T(8,128)}), f32[8,4,16,8,128]{4,3,2,1,0:T(8,128)S(1)}, u32[]{:S(2)}, u32[]{:S(2)}) async-start(f32[8,4,16,8,128]{4,3,2,1,0:T(8,128)} %shard_map.97), calls=%async_computation.2 | async-start | bytes 4194304 | tf_op jit(solution)/shard_map/all_to_all | solution.py:485
  66.9 12.4 %copy-start.1 = (f32[8,4,16,8,128]{4,3,2,1,0:T(8,128)}, f32[8,4,16,8,128]{4,3,2,1,0:T(8,128)S(1)}, u32[]{:S(2)}) copy-start(f32[8,4,16,8,128]{4,3,2,1,0:T(8,128)S(1)} %all-to-all-done.2) | copy-start | bytes 6291460
  66.9 54.1 %all-to-all-start = ((f32[8,4,16,8,128]{4,3,2,1,0:T(8,128)}), f32[8,4,16,8,128]{4,3,2,1,0:T(8,128)}, u32[]{:S(2)}, u32[]{:S(2)}) async-start(f32[8,4,16,8,128]{4,3,2,1,0:T(8,128)} %shard_map.93), calls=%async_computation | async-start | bytes 4194304 | tf_op jit(solution)/shard_map/all_to_all | solution.py:485
  79.3 40.0 %copy-start.7 = (f32[8,16,8,128]{3,2,1,0:T(8,128)S(1)}, f32[8,16,8,128]{3,2,1,0:T(8,128)}, u32[]{:S(2)}) copy-start(f32[8,16,8,128]{3,2,1,0:T(8,128)} %get-tuple-element.18) | copy-start | bytes 1572868
  79.3 24.9 %collective-permute-start.3 = (f32[8,16,8,128]{3,2,1,0:T(8,128)}, f32[8,16,8,128]{3,2,1,0:T(8,128)S(1)}, u32[]{:S(2)}, u32[]{:S(2)}) collective-permute-start(f32[8,16,8,128]{3,2,1,0:T(8,128)} %get-tuple-element.19), channel_id=1, source_target_pairs={{0,8},{8,0},{16,24},{24,16},{1,9},{9,1},{17,25},{25,17},{2,10},{10... | collective-permute-start | bytes 1572872 | tf_op jit(solution)/shard_map/ppermute | solution.py:481
  80.9 38.4 %collective-permute-start.4 = (f32[8,16,8,128]{3,2,1,0:T(8,128)}, f32[8,16,8,128]{3,2,1,0:T(8,128)S(1)}, u32[]{:S(2)}, u32[]{:S(2)}) collective-permute-start(f32[8,16,8,128]{3,2,1,0:T(8,128)} %get-tuple-element.20), channel_id=1, source_target_pairs={{0,16},{8,24},{16,0},{24,8},{1,17},{9,25},{17,1},{25,9},{2,18},{10... | collective-permute-start | bytes 1572872 | tf_op jit(solution)/shard_map/ppermute | solution.py:481
  83.5 35.8 %collective-permute-start.5 = (f32[8,16,8,128]{3,2,1,0:T(8,128)}, f32[8,16,8,128]{3,2,1,0:T(8,128)S(1)}, u32[]{:S(2)}, u32[]{:S(2)}) collective-permute-start(f32[8,16,8,128]{3,2,1,0:T(8,128)} %get-tuple-element.21), channel_id=1, source_target_pairs={{0,24},{8,16},{16,8},{24,0},{1,25},{9,17},{17,9},{25,1},{2,26},{10... | collective-permute-start | bytes 1572872 | tf_op jit(solution)/shard_map/ppermute | solution.py:481
  121.0 131.8 %all-to-all-start.1 = ((f32[8,4,16,8,128]{4,3,2,1,0:T(8,128)}), f32[8,4,16,8,128]{4,3,2,1,0:T(8,128)S(1)}, u32[]{:S(2)}, u32[]{:S(2)}) async-start(f32[8,4,16,8,128]{4,3,2,1,0:T(8,128)} %copy.25), calls=%async_computation.1 | async-start | bytes 4194304 | tf_op jit(solution)/shard_map/all_to_all | solution.py:485
  125.2 3.9 %copy-start.4 = (f32[8,4,16,8,128]{4,3,2,1,0:T(8,128)S(1)}, f32[8,4,16,8,128]{4,3,2,1,0:T(8,128)}, u32[]{:S(2)}) copy-start(f32[8,4,16,8,128]{4,3,2,1,0:T(8,128)} %copy-done.3) | copy-start | bytes 6291460
  129.1 12.7 %copy-start.2 = (f32[8,4,16,8,128]{4,3,2,1,0:T(8,128)S(1)}, f32[8,4,16,8,128]{4,3,2,1,0:T(8,128)}, u32[]{:S(2)}) copy-start(f32[8,4,16,8,128]{4,3,2,1,0:T(8,128)} %copy-done.1) | copy-start | bytes 6291460
  129.4 67.0 %collective-permute-start.14 = (f32[2,4,128,128]{3,2,1,0:T(8,128)S(1)}, f32[2,4,128,128]{3,2,1,0:T(8,128)S(1)}, u32[]{:S(2)}, u32[]{:S(2)}) collective-permute-start(f32[2,4,128,128]{3,2,1,0:T(8,128)S(1)} %get-tuple-element.32), channel_id=1, source_target_pairs={{0,24},{8,16},{16,8},{24,0},{1,25},{9,17},{17,9},{25,1},{2,26},{10... | collective-permute-start | bytes 1572872 | tf_op jit(solution)/shard_map/ppermute | solution.py:481
  131.9 67.0 %collective-permute-start.13 = (f32[2,4,128,128]{3,2,1,0:T(8,128)S(1)}, f32[2,4,128,128]{3,2,1,0:T(8,128)S(1)}, u32[]{:S(2)}, u32[]{:S(2)}) collective-permute-start(f32[2,4,128,128]{3,2,1,0:T(8,128)S(1)} %get-tuple-element.33), channel_id=1, source_target_pairs={{0,16},{8,24},{16,0},{24,8},{1,17},{9,25},{17,1},{25,9},{2,18},{10... | collective-permute-start | bytes 1572872 | tf_op jit(solution)/shard_map/ppermute | solution.py:481
  141.6 57.3 %collective-permute-start.12 = (f32[2,4,128,128]{3,2,1,0:T(8,128)S(1)}, f32[2,4,128,128]{3,2,1,0:T(8,128)S(1)}, u32[]{:S(2)}, u32[]{:S(2)}) collective-permute-start(f32[2,4,128,128]{3,2,1,0:T(8,128)S(1)} %get-tuple-element.34), channel_id=1, source_target_pairs={{0,8},{8,0},{16,24},{24,16},{1,9},{9,1},{17,25},{25,17},{2,10},{10... | collective-permute-start | bytes 1572872 | tf_op jit(solution)/shard_map/ppermute | solution.py:481
  142.9 31.2 %collective-permute-start.11 = (f32[2,2,128,128]{3,2,1,0:T(8,128)S(1)}, f32[2,2,128,128]{3,2,1,0:T(8,128)S(1)}, u32[]{:S(2)}, u32[]{:S(2)}) collective-permute-start(f32[2,2,128,128]{3,2,1,0:T(8,128)S(1)} %get-tuple-element.35), channel_id=1, source_target_pairs={{0,24},{8,16},{16,8},{24,0},{1,25},{9,17},{17,9},{25,1},{2,26},{10... | collective-permute-start | bytes 786440 | tf_op jit(solution)/shard_map/ppermute | solution.py:481
  145.3 64.7 %collective-permute-start.10 = (f32[2,2,128,128]{3,2,1,0:T(8,128)S(1)}, f32[2,2,128,128]{3,2,1,0:T(8,128)S(1)}, u32[]{:S(2)}, u32[]{:S(2)}) collective-permute-start(f32[2,2,128,128]{3,2,1,0:T(8,128)S(1)} %get-tuple-element.36), channel_id=1, source_target_pairs={{0,16},{8,24},{16,0},{24,8},{1,17},{9,25},{17,1},{25,9},{2,18},{10... | collective-permute-start | bytes 786440 | tf_op jit(solution)/shard_map/ppermute | solution.py:481
  174.1 35.8 %copy-start.8 = (f32[2,2,128,128]{3,2,1,0:T(8,128)}, f32[2,2,128,128]{3,2,1,0:T(8,128)S(1)}, u32[]{:S(2)}) copy-start(f32[2,2,128,128]{3,2,1,0:T(8,128)S(1)} %collective-permute-done.11.refs_6_) | copy-start | bytes 786436
  174.1 39.0 %collective-permute-start.9 = (f32[2,2,128,128]{3,2,1,0:T(8,128)S(1)}, f32[2,2,128,128]{3,2,1,0:T(8,128)S(1)}, u32[]{:S(2)}, u32[]{:S(2)}) collective-permute-start(f32[2,2,128,128]{3,2,1,0:T(8,128)S(1)} %get-tuple-element.37), channel_id=1, source_target_pairs={{0,8},{8,0},{16,24},{24,16},{1,9},{9,1},{17,25},{25,17},{2,10},{10... | collective-permute-start | bytes 786440 | tf_op jit(solution)/shard_map/ppermute | solution.py:481
  196.4 2.5 copy-start.11
  196.4 17.5 %collective-permute-start.8 = (f32[2,2,128,128]{3,2,1,0:T(8,128)}, f32[2,2,128,128]{3,2,1,0:T(8,128)}, u32[]{:S(2)}, u32[]{:S(2)}) collective-permute-start(f32[2,2,128,128]{3,2,1,0:T(8,128)} %get-tuple-element.38), channel_id=1, source_target_pairs={{0,24},{8,16},{16,8},{24,0},{1,25},{9,17},{17,9},{25,1},{2,26},{10... | collective-permute-start | bytes 786440 | tf_op jit(solution)/shard_map/ppermute | solution.py:481
  198.9 0.8 copy-start.12
  198.9 47.7 %collective-permute-start.7 = (f32[2,2,128,128]{3,2,1,0:T(8,128)}, f32[2,2,128,128]{3,2,1,0:T(8,128)}, u32[]{:S(2)}, u32[]{:S(2)}) collective-permute-start(f32[2,2,128,128]{3,2,1,0:T(8,128)} %get-tuple-element.39), channel_id=1, source_target_pairs={{0,16},{8,24},{16,0},{24,8},{1,17},{9,25},{17,1},{25,9},{2,18},{10... | collective-permute-start | bytes 786440 | tf_op jit(solution)/shard_map/ppermute | solution.py:481
  198.9 2.0 copy-start.13
  199.7 46.9 %collective-permute-start.6 = (f32[2,2,128,128]{3,2,1,0:T(8,128)}, f32[2,2,128,128]{3,2,1,0:T(8,128)}, u32[]{:S(2)}, u32[]{:S(2)}) collective-permute-start(f32[2,2,128,128]{3,2,1,0:T(8,128)} %get-tuple-element.40), channel_id=1, source_target_pairs={{0,8},{8,0},{16,24},{24,16},{1,9},{9,1},{17,25},{25,17},{2,10},{10... | collective-permute-start | bytes 786440 | tf_op jit(solution)/shard_map/ppermute | solution.py:481
  210.0 0.7 copy-start.9
  210.7 52.9 %collective-permute-start.2 = (f32[2,4,128,128]{3,2,1,0:T(8,128)}, f32[2,4,128,128]{3,2,1,0:T(8,128)S(1)}, u32[]{:S(2)}, u32[]{:S(2)}) collective-permute-start(f32[2,4,128,128]{3,2,1,0:T(8,128)} %get-tuple-element.41), channel_id=1, source_target_pairs={{0,24},{8,16},{16,8},{24,0},{1,25},{9,17},{17,9},{25,1},{2,26},{10... | collective-permute-start | bytes 1572872 | tf_op jit(solution)/shard_map/ppermute | solution.py:481
  213.1 0.7 copy-start.10
  213.8 55.0 %collective-permute-start.1 = (f32[2,4,128,128]{3,2,1,0:T(8,128)}, f32[2,4,128,128]{3,2,1,0:T(8,128)S(1)}, u32[]{:S(2)}, u32[]{:S(2)}) collective-permute-start(f32[2,4,128,128]{3,2,1,0:T(8,128)} %get-tuple-element.42), channel_id=1, source_target_pairs={{0,16},{8,24},{16,0},{24,8},{1,17},{9,25},{17,1},{25,9},{2,18},{10... | collective-permute-start | bytes 1572872 | tf_op jit(solution)/shard_map/ppermute | solution.py:481
  213.9 54.9 %collective-permute-start = (f32[2,4,128,128]{3,2,1,0:T(8,128)}, f32[2,4,128,128]{3,2,1,0:T(8,128)}, u32[]{:S(2)}, u32[]{:S(2)}) collective-permute-start(f32[2,4,128,128]{3,2,1,0:T(8,128)} %get-tuple-element.43), channel_id=1, source_target_pairs={{0,8},{8,0},{16,24},{24,16},{1,9},{9,1},{17,25},{25,17},{2,10},{10... | collective-permute-start | bytes 1572872 | tf_op jit(solution)/shard_map/ppermute | solution.py:481
  252.8 1.4 copy-start
  263.6 5.3 %copy-start.5 = (f32[2,4,128,128]{3,2,1,0:T(8,128)}, f32[2,4,128,128]{3,2,1,0:T(8,128)S(1)}, u32[]{:S(2)}) copy-start(f32[2,4,128,128]{3,2,1,0:T(8,128)S(1)} %collective-permute-done.2.refs_6_) | copy-start | bytes 1572868
  268.8 0.8 copy-start.6

commit v3 on v2

--- a/solution.py
+++ b/solution.py
@@ -15,7 +15,8 @@
 SUBLANES = 8
 EAST_RADIX = 8
 CHUNKS = 4
-LAST_PIECES = 2
+FIRST_PICKS = 8
+TURNS = (1, 0, 2, 3, 4)
 F32 = jnp.float32
 BF16 = jnp.bfloat16
 ANY = pl.ANY
@@ -97,13 +98,20 @@
     return np.stack([high, low]), twiddle
 
 
+def place():
+    height = lax.axis_index("height")
+    return height, height * lax.axis_size("width") + lax.axis_index("width")
+
+
 def north_kernel(
-    wind, radix, east_cells, north_cells, steps,
-    place_ref, cut_ref, vort_ref, div_ref, matrix_ref, twiddle_ref, *rest,
+    wind, radix, first_pick, east_cells, north_cells, steps,
+    cut_ref, vort_ref, div_ref, matrix_ref, twiddle_ref, *rest,
 ):
     *out_refs, cut_rows, winds, g_high, g_low = rest
     step = pl.program_id(0)
+    height, column = place()
     waves = cut_ref.shape[1]
+    picks = g_high.shape[0] // waves
     fast = north_cells // radix
     block_rows = vort_ref.shape[2]
     east_unit = 2.0 * math.pi / east_cells
@@ -120,7 +128,7 @@
         local = pl.multiple_of(part * SUBLANES, SUBLANES)
         base = pl.multiple_of(step * block_rows + local, SUBLANES)
         cut = cut_rows[pl.ds(base, SUBLANES), :]
-        wave = place_ref[0] + base + sub
+        wave = column * waves + base + sub
         kx = east_unit * wave.astype(F32)
         kx2 = kx * kx
         weight = jnp.where(wave == 0, 1.0, 2.0).astype(F32)
@@ -149,7 +157,6 @@
 
     @pl.when(step == steps - 1)
     def _():
-        column = place_ref[2]
         stride = EAST_RADIX
         count = waves // stride
 
@@ -161,13 +168,14 @@
                     tuple(winds[ri, n1, pl.ds(residue, count, stride=stride), :] for ri in range(2))
                 )
             result = small_dft(values)
-            for y1 in range(radix):
+            for pick in range(picks):
+                y1 = first_pick + pick
                 re, im = result[y1]
                 if y1:
                     c = twiddle_ref[0, y1:y1 + 1, :]
                     s = twiddle_ref[1, y1:y1 + 1, :]
                     re, im = re * c - im * s, re * s + im * c
-                row = pl.multiple_of(y1 * waves + t * count, count)
+                row = pl.multiple_of(pick * waves + t * count, count)
                 high, low = split_f32(re)
                 g_high[pl.ds(row, count), 0:fast] = high
                 g_low[pl.ds(row, count), 0:fast] = low
@@ -182,7 +190,6 @@
     def _():
         contract = (((1,), (1,)), ((), ()))
         dot = functools.partial(lax.dot_general, dimension_numbers=contract, preferred_element_type=F32)
-        height = place_ref[1]
         planes = len(out_refs) if len(out_refs) > 1 else out_refs[0].shape[1]
         owners = out_refs[0].shape[0]
         span = owners * SUBLANES
@@ -193,7 +200,7 @@
             )
 
         matrix_high, matrix_low = rows_of(0), rows_of(1)
-        for pair in range(radix // 2):
+        for pair in range(picks // 2):
             rows = slice(pair * 2 * waves, (pair + 1) * 2 * waves)
             high = g_high[rows, :]
             low = g_low[rows, :]
@@ -209,16 +216,18 @@
                         out_refs[0][:, j, y1] = piece
 
 
-def north_call(place, cut, vort, div, matrix, twiddle, slot, wind, radix, east_cells, planes, owners, apart):
+def north_call(
+    cut, vort, div, matrix, twiddle, slot, wind, radix, first_pick, picks, east_cells, planes, owners, apart
+):
     waves = vort.shape[2]
     north_cells = vort.shape[3]
     steps = 2
     block_rows = waves // steps
     fast = north_cells // radix
     data_spec = pl.BlockSpec((2, 1, block_rows, north_cells), lambda i: (0, slot, i, 0))
-    kernel = functools.partial(north_kernel, wind, radix, east_cells, north_cells, steps)
-    flops = 6 * (2 * fast) ** 2 * radix * waves
-    tile = (radix, SUBLANES, waves)
+    kernel = functools.partial(north_kernel, wind, radix, first_pick, east_cells, north_cells, steps)
+    flops = 6 * (2 * fast) ** 2 * picks * waves
+    tile = (picks, SUBLANES, waves)
     shape = (owners,) + tile if apart else (owners, planes) + tile
     whole = pl.BlockSpec(shape, lambda i: (0,) * len(shape))
     out_specs = [whole] * (planes if apart else 1)
@@ -226,7 +235,6 @@
         kernel,
         grid=(steps,),
         in_specs=[
-            pl.BlockSpec(memory_space=pltpu.SMEM),
             pl.BlockSpec((1, waves), lambda i: (0, 0)),
             data_spec,
             data_spec,
@@ -238,12 +246,12 @@
         scratch_shapes=[
             pltpu.VMEM((waves, LANES), jnp.int32),
             pltpu.VMEM((2, radix, waves, fast), F32),
-            pltpu.VMEM((radix * waves, 2 * fast), BF16),
-            pltpu.VMEM((radix * waves, 2 * fast), BF16),
+            pltpu.VMEM((picks * waves, 2 * fast), BF16),
+            pltpu.VMEM((picks * waves, 2 * fast), BF16),
         ],
         compiler_params=pltpu.CompilerParams(dimension_semantics=("arbitrary",)),
         cost_estimate=pl.CostEstimate(flops=flops, bytes_accessed=6 << 20, transcendentals=0),
-    )(place, cut, vort, div, matrix, twiddle)
+    )(cut, vort, div, matrix, twiddle)
 
 
 def east_table(local_waves, east_cells):
@@ -267,9 +275,9 @@
 
 def east_kernel(slot, slots_local, sources, first_group, east_cells, local_waves, *refs):
     planes = len(sources)
-    place_ref, level_ref, table_hbm = refs[:3]
-    got_hbm = refs[3:3 + planes]
-    value_ref, slope_ref, got, table, h_high, h_low, spectra, grid_out, got_sems, table_sems, out_sems = refs[-11:]
+    level_ref, table = refs[:2]
+    got_hbm = refs[2:2 + planes]
+    value_ref, slope_ref, got, parts, spectra, grid_out, got_sems, out_sems = refs[-8:]
     radix = EAST_RADIX
     _, width, groups, packed, lanes = got.shape
     columns = planes * width
@@ -277,7 +285,7 @@
     per_owner = SUBLANES // 2
     rows_out = north_radix * per_owner
     span = spectra.shape[3] // 2
-    height = place_ref[1]
+    height, _ = place()
 
     loads = []
     for j, plane in enumerate(sources):
@@ -291,14 +299,6 @@
     def columns_of(a):
         return slice(0, span if a % (radix // 2) == 0 else 2 * span)
 
-    tables = []
-    for a in range(radix):
-        cols = columns_of(a)
-        copy = pltpu.make_async_copy(
-            table_hbm.at[a, :, :, cols], table.at[a, :, :, cols], table_sems.at[a]
-        )
-        copy.start()
-        tables.append(copy)
     for copy in loads:
         copy.wait()
 
@@ -327,8 +327,8 @@
                     sloped = slabs[a] * kx[a]
                     for kind, value, part in ((0, slabs[a], ri), (1, -sloped if ri else sloped, 1 - ri)):
                         high, low = split_f32(value)
-                        h_high[kind, a, pl.ds(row, north_radix), part * lanes:(part + 1) * lanes] = high
-                        h_low[kind, a, pl.ds(row, north_radix), part * lanes:(part + 1) * lanes] = low
+                        parts[a, kind, pl.ds(row, north_radix), part * lanes:(part + 1) * lanes] = high
+                        parts[a, 2 + kind, pl.ds(row, north_radix), part * lanes:(part + 1) * lanes] = low
         return carry
 
     lax.fori_loop(0, groups, shuffle, 0)
@@ -337,7 +337,7 @@
 
     def multiply(kind, a):
         cols = columns_of(a)
-        left, left_low = h_high[kind, a], h_low[kind, a]
+        left, left_low = parts[a, kind], parts[a, 2 + kind]
         right, right_low = table[a, 0, :, cols], table[a, 1, :, cols]
         spectra[kind, a, :, cols] = dot(left, right) + dot(left_low, right) + dot(left, right_low)
 
@@ -368,15 +368,23 @@
         copy.start()
         return copy
 
-    for copy in tables:
-        copy.wait()
+    def multiply_both(a):
+        cols = columns_of(a)
+        rows = parts.shape[2]
+        both = dot(parts[a].reshape(4 * rows, 2 * lanes), table[a, 0, :, cols])
+        rest = dot(parts[a, 0:2].reshape(2 * rows, 2 * lanes), table[a, 1, :, cols])
+        for kind in range(2):
+            at, low = kind * rows, (2 + kind) * rows
+            spectra[kind, a, :, cols] = both[at:at + rows] + both[low:low + rows] + rest[at:at + rows]
+
+    together = groups == 1
     for a in range(radix):
-        multiply(0, a)
+        multiply_both(a) if together else multiply(0, a)
     copies = []
-    share = radix // groups
     for group in range(groups):
-        for a in range(group * share, (group + 1) * share):
-            multiply(1, a)
+        if not together:
+            for a in range(group * radix // groups, (group + 1) * radix // groups):
+                multiply(1, a)
         copies.append(finish(0, group))
     for group in range(groups):
         copies.append(finish(1, group))
@@ -385,7 +393,7 @@
 
 
 def east_call(
-    place, levels, got, table, slot, slots_local, first_group, groups, width, east_cells, local_waves, previous
+    levels, got, table, slot, slots_local, first_group, groups, width, east_cells, local_waves, previous
 ):
     planes = len(got)
     packed, lanes = got[0][0].shape[-2:]
@@ -393,8 +401,9 @@
     radix = EAST_RADIX
     level_count = levels.shape[0]
     out = jax.ShapeDtypeStruct((level_count, rows_out, east_cells), F32)
-    in_specs = [pl.BlockSpec(memory_space=pltpu.SMEM)] * 2 + [pl.BlockSpec(memory_space=ANY)] * (1 + planes)
-    operands = [place, levels, table] + [array for array, _ in got]
+    in_specs = [pl.BlockSpec(memory_space=pltpu.SMEM), pl.BlockSpec(memory_space=pltpu.VMEM)]
+    in_specs += [pl.BlockSpec(memory_space=ANY)] * planes
+    operands = [levels, table] + [array for array, _ in got]
     aliases = {}
     if previous is not None:
         aliases = {len(operands): 0, len(operands) + 1: 1}
@@ -410,16 +419,14 @@
         out_shape=[out, out],
         scratch_shapes=[
             pltpu.VMEM((planes, width, groups, packed, lanes), F32),
-            pltpu.VMEM(table.shape, BF16),
-            pltpu.VMEM((2, radix, rows, 2 * lanes), BF16),
-            pltpu.VMEM((2, radix, rows, 2 * lanes), BF16),
+            pltpu.VMEM((radix, 4, rows, 2 * lanes), BF16),
             pltpu.VMEM((2, radix, rows, columns), F32),
             pltpu.VMEM((2, rows, east_cells), F32),
             pltpu.SemaphoreType.DMA((planes,)),
-            pltpu.SemaphoreType.DMA((radix,)),
             pltpu.SemaphoreType.DMA((2 * groups,)),
         ],
         input_output_aliases=aliases,
+        compiler_params=pltpu.CompilerParams(vmem_limit_bytes=40 << 20),
         cost_estimate=pl.CostEstimate(
             flops=12 * radix * rows * 2 * lanes * columns, bytes_accessed=14 << 20, transcendentals=0
         ),
@@ -439,8 +446,8 @@
         and radix >= 2
         and radix & (radix - 1) == 0
         and north_cells == radix * LANES
-        and groups % LAST_PIECES == 0
-        and EAST_RADIX % groups == 0
+        and radix > FIRST_PICKS
+        and groups % 2 == 0
         and vorticity.shape[1] * 2 == CHUNKS
     )
 
@@ -460,18 +467,15 @@
     east_cells = 2 * waves * columns
     rows_out = north_cells // (columns * groups)
     radix = rows_out // (SUBLANES // 2)
-    height = lax.axis_index("height").astype(jnp.int32)
-    column = height * width + lax.axis_index("width")
-    place = jnp.stack([column * waves, height, column]).astype(jnp.int32)
     matrix, twiddle = north_tables(north_cells, radix, rows_out, columns * groups)
     cut = trunc_cut.reshape(1, waves)
     packed = radix * SUBLANES
     swaps = [[(z, z ^ j) for z in range(planes)] for j in range(planes)]
     order = list(range(planes - 1, 0, -1))
 
-    def north(slot, wind, apart):
+    def north(slot, wind, first_pick, picks, apart):
         return north_call(
-            place, cut, vorticity, divergence, matrix, twiddle, slot, wind, radix, east_cells,
+            cut, vorticity, divergence, matrix, twiddle, slot, wind, radix, first_pick, picks, east_cells,
             planes, width * groups, apart,
         )
 
@@ -491,24 +495,23 @@
     last = len(chunks) - 1
     for at, (slot, wind) in enumerate(chunks):
         if at == 0:
-            swapped = swap(north(slot, wind, True))
-            block = jnp.stack([swapped[j] for j in range(planes)], axis=1)
-            block = around(block).reshape(width, groups, planes, packed, waves)
+            head = swap(north(slot, wind, 0, FIRST_PICKS, True))
+            tail = swap(north(slot, wind, FIRST_PICKS, radix - FIRST_PICKS, True))
+            joined = [jnp.concatenate([head[j], tail[j]], axis=1) for j in range(planes)]
+            block = around(jnp.stack(joined, axis=1)).reshape(width, groups, planes, packed, waves)
             ready.append((at, slot, wind, 0, groups, [(block, j) for j in range(planes)]))
         else:
-            block = around(north(slot, wind, False)[0])
+            block = around(north(slot, wind, 0, radix, False)[0])
             block = block.reshape(width, groups, planes, packed, waves)
-            pieces = LAST_PIECES if at == last else 1
-            share = groups // pieces
-            for piece in range(pieces):
-                near = piece * share
+            near = 0
+            for piece, share in enumerate((groups // 2,) * 2 if at == last else (groups,)):
                 swapped = swap([block[:, near:near + share, j] for j in range(planes)])
                 got = [(block, 0)] + [(swapped[j], None) for j in range(1, planes)]
                 ready.append((at + piece, slot, wind, near, share, got))
-    ready[0], ready[1] = ready[1], ready[0]
-    for at, slot, wind, near, share, got in ready:
+                near += share
+    for at, slot, wind, near, share, got in (ready[turn] for turn in TURNS):
         outputs[wind] = east_call(
-            place, level_slot, got, table, slot, slots_local, near, share, width, east_cells, waves, outputs[wind]
+            level_slot, got, table, slot, slots_local, near, share, width, east_cells, waves, outputs[wind]
         )
     return (outputs[0][0], outputs[1][0], outputs[0][1], outputs[1][1])
 

time: 281 us -> 291 us (1.036)
  waiting for transfers between devices: 115 us -> 135 us
  Pallas kernels: 66.3 us -> 60.6 us
    ppermute x15 -> x18, waiting for transfers between devices: 80.1 us -> 99.2 us  [swap(): got[j] = lax.ppermute(parts[j], 'height', swaps[j])]
    pallas_call x5, Pallas kernels: 40 us -> 30.1 us  [east_call(): pl.pallas_call(functools.partial(east_kernel, slot, slots_local, sources,...]
    pallas_call x4 -> x5, Pallas kernels: 26.3 us -> 30.5 us  [north_call(): pl.pallas_call(kernel, grid=(steps,), in_specs=[pl.BlockSpec((1, waves),...]
    ppermute x15 -> x18, starting transfers between devices: 53.7 us -> 53.9 us  [swap(): got[j] = lax.ppermute(parts[j], 'height', swaps[j])]
  transfers between devices with their start and end apart: 19 -> 22, of which waited for: 7 -> 9; matrix products, arithmetic and copies ran while one was open for 6% -> 5% of each run, Pallas kernels for 18% -> 16%
where the time goes in v3:
time: 291 us; the launch traced here: 289 us
  waiting for transfers between devices  135 us (46%)
  starting transfers between devices  73 us (25%)
  Pallas kernels  60.6 us (21%)
  local copies, waits for them, and re-layouts  10.8 us (4%)
  other arithmetic  8.75 us (3%)
    ppermute x18, waiting for transfers between devices, swap(): got[j] = lax.ppermute(parts[j], 'height', swaps[j])  99.2 us
    ppermute x18, starting transfers between devices, swap(): got[j] = lax.ppermute(parts[j], 'height', swaps[j])  53.9 us
    all_to_all x4, waiting for transfers between devices, around(): lax.all_to_all(block, ('width', 'row'), split_axis=0, concat_axis=0, tile...  35.4 us
    pallas_call x5, Pallas kernels, north_call(): pl.pallas_call(kernel, grid=(steps,), in_specs=[pl.BlockSpec((1, waves),...  30.5 us
    pallas_call x5, Pallas kernels, east_call(): pl.pallas_call(functools.partial(east_kernel, slot, slots_local, sources,...  30.1 us
    all_to_all x4, starting transfers between devices, around(): lax.all_to_all(block, ('width', 'row'), split_axis=0, concat_axis=0, tile...  19.1 us
  transfers between devices with their start and end apart: 22, of which 9 were waited for; matrix products, arithmetic and copies ran while one was open for 5% of the time, Pallas kernels for 16%

profile of v3, /device:TPU:6, one launch (start us, length us, event | category | flops | bytes accessed | tf_op | source)
XLA Modules:
  0.0 288.8 jit_solution(1202688840881628454)
XLA Ops:
  0.6 6.6 %shard_map.99 = f32[8,4,16,8,128]{4,3,2,1,0:T(8,128)} custom-call(s32[1,128]{1,0:T(1,128)} %bitcast.50, f32[2,2,128,2048]{3,2,1,0:T(8,128)} %vort_ref.9, f32[2,2,128,2048]{3,2,1,0:T(8,128)} %div_ref.9, bf16[2,256,256]{2,1,0:T(8,128)(2,1)} %constant.55.clone.matrix_ref, f32[2,16,128]{2,1,0:T(8,128)} %constant.56.clone.twiddle_ref), custom_call_target="tpu_custom_call" | custom-call | flops 805306368 | bytes 6291456 | tf_op jit(solution)/shard_map/pallas_call | solution.py:234
  7.2 4.2 %all-to-all-start.3 = ((f32[8,4,16,8,128]{4,3,2,1,0:T(8,128)}), f32[8,4,16,8,128]{4,3,2,1,0:T(8,128)S(1)}, u32[]{:S(2)}, u32[]{:S(2)}) async-start(f32[8,4,16,8,128]{4,3,2,1,0:T(8,128)} %shard_map.99), calls=%async_computation.3 | async-start | bytes 4194304 | tf_op jit(solution)/shard_map/all_to_all | solution.py:489
  11.4 6.6 %shard_map.98 = f32[8,4,16,8,128]{4,3,2,1,0:T(8,128)} custom-call(s32[1,128]{1,0:T(1,128)} %bitcast.51, f32[2,2,128,2048]{3,2,1,0:T(8,128)} %vort_ref.9, f32[2,2,128,2048]{3,2,1,0:T(8,128)} %div_ref.9, bf16[2,256,256]{2,1,0:T(8,128)(2,1)} %constant.55.clone.matrix_ref, f32[2,16,128]{2,1,0:T(8,128)} %constant.56.clone.twiddle_ref), custom_call_target="tpu_custom_call" | custom-call | flops 805306368 | bytes 6291456 | tf_op jit(solution)/shard_map/pallas_call | solution.py:234
  18.0 17.7 %all-to-all-done.3 = f32[8,4,16,8,128]{4,3,2,1,0:T(8,128)S(1)} async-done(((f32[8,4,16,8,128]{4,3,2,1,0:T(8,128)}), f32[8,4,16,8,128]{4,3,2,1,0:T(8,128)S(1)}, u32[]{:S(2)}, u32[]{:S(2)}) %all-to-all-start.3) | async-done | bytes 2097184 | tf_op jit(solution)/shard_map/all_to_all | solution.py:489
  35.7 1.4 copy-done.4
  37.0 5.0 %all-to-all-start.2 = ((f32[8,4,16,8,128]{4,3,2,1,0:T(8,128)}), f32[8,4,16,8,128]{4,3,2,1,0:T(8,128)S(1)}, u32[]{:S(2)}, u32[]{:S(2)}) async-start(f32[8,4,16,8,128]{4,3,2,1,0:T(8,128)} %shard_map.98), calls=%async_computation.2 | async-start | bytes 4194304 | tf_op jit(solution)/shard_map/all_to_all | solution.py:489
  42.0 6.6 %shard_map.93 = f32[8,4,16,8,128]{4,3,2,1,0:T(8,128)} custom-call(s32[1,128]{1,0:T(1,128)} %bitcast.52, f32[2,2,128,2048]{3,2,1,0:T(8,128)} %vort_ref.9, f32[2,2,128,2048]{3,2,1,0:T(8,128)} %div_ref.9, bf16[2,256,256]{2,1,0:T(8,128)(2,1)} %constant.55.clone.matrix_ref, f32[2,16,128]{2,1,0:T(8,128)} %constant.56.clone.twiddle_ref), custom_call_target="tpu_custom_call" | custom-call | flops 805306368 | bytes 6291456 | tf_op jit(solution)/shard_map/pallas_call | solution.py:234
  48.6 17.7 %all-to-all-done.2 = f32[8,4,16,8,128]{4,3,2,1,0:T(8,128)S(1)} async-done(((f32[8,4,16,8,128]{4,3,2,1,0:T(8,128)}), f32[8,4,16,8,128]{4,3,2,1,0:T(8,128)S(1)}, u32[]{:S(2)}, u32[]{:S(2)}) %all-to-all-start.2) | async-done | bytes 2097184 | tf_op jit(solution)/shard_map/all_to_all | solution.py:489
  66.2 5.7 %all-to-all-start = ((f32[8,4,16,8,128]{4,3,2,1,0:T(8,128)}), f32[8,4,16,8,128]{4,3,2,1,0:T(8,128)}, u32[]{:S(2)}, u32[]{:S(2)}) async-start(f32[8,4,16,8,128]{4,3,2,1,0:T(8,128)} %shard_map.93), calls=%async_computation | async-start | bytes 4194304 | tf_op jit(solution)/shard_map/all_to_all | solution.py:489
  72.0 5.4 %shard_map.95 = (f32[8,8,8,128]{3,2,1,0:T(8,128)}, f32[8,8,8,128]{3,2,1,0:T(8,128)}, f32[8,8,8,128]{3,2,1,0:T(8,128)}, f32[8,8,8,128]{3,2,1,0:T(8,128)}) custom-call(s32[1,128]{1,0:T(1,128)} %bitcast.53, f32[2,2,128,2048]{3,2,1,0:T(8,128)} %vort_ref.9, f32[2,2,128,2048]{3,2,1,0:T(8,128)} %div_ref.9, bf16[2,256,256]{2,1,0:T(8,128)(2,1)} %constant.55.clone.matrix_ref, ...), custom_call_target="tpu_custom_call" | custom-call | flops 402653184 | bytes 6291456 | tf_op jit(solution)/shard_map/pallas_call | solution.py:234
  77.4 1.6 collective-permute-start.4
  79.0 2.6 collective-permute-start.6
  81.8 5.4 %shard_map.94 = (f32[8,8,8,128]{3,2,1,0:T(8,128)}, f32[8,8,8,128]{3,2,1,0:T(8,128)}, f32[8,8,8,128]{3,2,1,0:T(8,128)}, f32[8,8,8,128]{3,2,1,0:T(8,128)}) custom-call(s32[1,128]{1,0:T(1,128)} %bitcast.54, f32[2,2,128,2048]{3,2,1,0:T(8,128)} %vort_ref.9, f32[2,2,128,2048]{3,2,1,0:T(8,128)} %div_ref.9, bf16[2,256,256]{2,1,0:T(8,128)(2,1)} %constant.55.clone.matrix_ref, ...), custom_call_target="tpu_custom_call" | custom-call | flops 402653184 | bytes 6291456 | tf_op jit(solution)/shard_map/pallas_call | solution.py:234
  87.2 0.7 collective-permute-start.3
  87.9 3.5 %collective-permute-start.5 = (f32[8,8,8,128]{3,2,1,0:T(8,128)}, f32[8,8,8,128]{3,2,1,0:T(8,128)S(1)}, u32[]{:S(2)}, u32[]{:S(2)}) collective-permute-start(f32[8,8,8,128]{3,2,1,0:T(8,128)} %get-tuple-element.26), channel_id=1, source_target_pairs={{0,16},{8,24},{16,0},{24,8},{1,17},{9,25},{17,1},{25,9},{2,18},{10... | collective-permute-start | bytes 786440 | tf_op jit(solution)/shard_map/ppermute | solution.py:485
  91.4 0.4 collective-permute-done.4
  91.8 3.5 %collective-permute-start.7 = (f32[8,8,8,128]{3,2,1,0:T(8,128)}, f32[8,8,8,128]{3,2,1,0:T(8,128)S(1)}, u32[]{:S(2)}, u32[]{:S(2)}) collective-permute-start(f32[8,8,8,128]{3,2,1,0:T(8,128)} %get-tuple-element.28), channel_id=1, source_target_pairs={{0,24},{8,16},{16,8},{24,0},{1,25},{9,17},{17,9},{25,1},{2,26},{10... | collective-permute-start | bytes 786440 | tf_op jit(solution)/shard_map/ppermute | solution.py:485
  95.4 1.0 maximum_bitcast_fusion
  96.3 6.6 %collective-permute-done.3 = f32[8,8,8,128]{3,2,1,0:T(8,128)S(1)} collective-permute-done((f32[8,8,8,128]{3,2,1,0:T(8,128)}, f32[8,8,8,128]{3,2,1,0:T(8,128)S(1)}, u32[]{:S(2)}, u32[]{:S(2)}) %collective-permute-start.3) | collective-permute-done | bytes 262176 | tf_op jit(solution)/shard_map/ppermute | solution.py:485
  103.0 20.0 %collective-permute-done.5 = f32[8,8,8,128]{3,2,1,0:T(8,128)S(1)} collective-permute-done((f32[8,8,8,128]{3,2,1,0:T(8,128)}, f32[8,8,8,128]{3,2,1,0:T(8,128)S(1)}, u32[]{:S(2)}, u32[]{:S(2)}) %collective-permute-start.5) | collective-permute-done | bytes 262176 | tf_op jit(solution)/shard_map/ppermute | solution.py:485
  123.3 1.5 copy.25
  124.8 4.2 %all-to-all-start.1 = ((f32[8,4,16,8,128]{4,3,2,1,0:T(8,128)}), f32[8,4,16,8,128]{4,3,2,1,0:T(8,128)S(1)}, u32[]{:S(2)}, u32[]{:S(2)}) async-start(f32[8,4,16,8,128]{4,3,2,1,0:T(8,128)} %copy.25), calls=%async_computation.1 | async-start | bytes 4194304 | tf_op jit(solution)/shard_map/all_to_all | solution.py:489
  129.0 5.1 %reduce-precision_convert_fusion = (bf16[8,1,128,256]{3,2,1,0:T(8,128)(2,1)S(1)}, bf16[8,1,128,256]{3,2,1,0:T(8,128)(2,1)S(1)}, bf16[8,1,128,256]{3,2,1,0:T(8,128)(2,1)S(1)}, bf16[8,1,128,256]{3,2,1,0:T(8,128)(2,1)S(1)}) fusion(s32[8,128]{1,0:T(8,128)S(1)} %iota_add_fusion), kind=kLoop, calls=%fused_computation.6 | loop fusion | flops 5767168 | bytes 2101248 | tf_op jit(solution)/shard_map/convert_element_type | solution.py:269
  134.3 2.2 maximum_maximum_fusion.refs_1_
  137.0 1.2 slice_bitcast_fusion
  138.2 2.5 collective-permute-start.17
  140.7 4.0 %collective-permute-start.16 = (f32[2,4,128,128]{3,2,1,0:T(8,128)}, f32[2,4,128,128]{3,2,1,0:T(8,128)}, u32[]{:S(2)}, u32[]{:S(2)}) collective-permute-start(f32[2,4,128,128]{3,2,1,0:T(8,128)} %get-tuple-element.41), channel_id=1, source_target_pairs={{0,16},{8,24},{16,0},{24,8},{1,17},{9,25},{17,1},{25,9},{2,18},{10... | collective-permute-start | bytes 1572872 | tf_op jit(solution)/shard_map/ppermute | solution.py:485
  145.1 0.9 slice_bitcast_fusion.6
  146.0 2.4 collective-permute-start.14
  148.4 1.0 collective-permute-start.13
  149.4 1.7 copy.24
  151.1 1.2 slice_bitcast_fusion.3
  152.3 31.0 %collective-permute-done.14.refs_5_ = f32[2,2,128,128]{3,2,1,0:T(8,128)S(1)} collective-permute-done((f32[2,2,128,128]{3,2,1,0:T(8,128)S(1)}, f32[2,2,128,128]{3,2,1,0:T(8,128)S(1)}, u32[]{:S(2)}, u32[]{:S(2)}) %collective-permute-start.14) | collective-permute-done | bytes 262176 | tf_op jit(solution)/shard_map/ppermute | solution.py:485
  183.3 22.1 %collective-permute-start.12 = (f32[2,2,128,128]{3,2,1,0:T(8,128)}, f32[2,2,128,128]{3,2,1,0:T(8,128)S(1)}, u32[]{:S(2)}, u32[]{:S(2)}) collective-permute-start(f32[2,2,128,128]{3,2,1,0:T(8,128)} %get-tuple-element.45), channel_id=1, source_target_pairs={{0,8},{8,0},{16,24},{24,16},{1,9},{9,1},{17,25},{25,17},{2,10},{10... | collective-permute-start | bytes 786440 | tf_op jit(solution)/shard_map/ppermute | solution.py:485
  205.4 5.1 %collective-permute-done.13.refs_4_ = f32[2,2,128,128]{3,2,1,0:T(8,128)S(1)} collective-permute-done((f32[2,2,128,128]{3,2,1,0:T(8,128)S(1)}, f32[2,2,128,128]{3,2,1,0:T(8,128)S(1)}, u32[]{:S(2)}, u32[]{:S(2)}) %collective-permute-start.13) | collective-permute-done | bytes 262176 | tf_op jit(solution)/shard_map/ppermute | solution.py:485
  210.5 2.5 collective-permute-start.11
  212.9 2.2 copy-done
  215.1 6.6 %shard_map.96 = (f32[8,64,2048]{2,1,0:T(8,128)}, f32[8,64,2048]{2,1,0:T(8,128)}) custom-call(s32[8]{0:T(128)S(1)} %copy-done.7, bf16[8,2,256,512]{3,2,1,0:T(8,128)(2,1)S(1)} %copy-done, f32[2,4,4,128,128]{4,3,2,1,0:T(8,128)S(1)} %bitcast.40, f32[2,4,4,128,128]{4,3,2,1,0:T(8,128)S(1)} %bitcast.41, f32[2,4,4,128,128]{4,3,2,1,0:T(8,128)S(1)} %bitcast.42, ...), custom_call_target="tpu_custom_call" | custom-call | flops 3221225472 | bytes 14680064 | tf_op jit(solution)/shard_map/pallas_call | solution.py:415
  221.7 0.5 collective-permute-start.10
  222.3 2.4 collective-permute-start.9
  224.6 1.6 collective-permute-start.2
  226.2 2.8 collective-permute-start
  229.1 7.8 %shard_map.100 = (f32[8,64,2048]{2,1,0:T(8,128)}, f32[8,64,2048]{2,1,0:T(8,128)}) custom-call(s32[8]{0:T(128)S(1)} %copy-done.7, bf16[8,2,256,512]{3,2,1,0:T(8,128)(2,1)S(1)} %copy-done, f32[2,4,4,128,128]{4,3,2,1,0:T(8,128)S(1)} %bitcast.46, f32[2,4,128,128]{3,2,1,0:T(8,128)} %collective-permute-done.15.refs_3_, ...), custom_call_target="tpu_custom_call" | custom-call | flops 3221225472 | bytes 14680064 | tf_op jit(solution)/shard_map/pallas_call | solution.py:415
  236.9 4.0 %shard_map.101 = (f32[8,64,2048]{2,1,0:T(8,128)}, f32[8,64,2048]{2,1,0:T(8,128)}) custom-call(s32[8]{0:T(128)S(1)} %copy-done.7, bf16[8,2,256,512]{3,2,1,0:T(8,128)(2,1)S(1)} %copy-done, f32[2,4,4,128,128]{4,3,2,1,0:T(8,128)S(1)} %bitcast.44, f32[2,2,128,128]{3,2,1,0:T(8,128)S(1)} %collective-permute-done.12.refs_3_, ...), custom_call_target="tpu_custom_call", output_to_operand_aliasing={{0}: (6, {}), {1}: (7, {})} | custom-call | flops 1610612736 | bytes 14680064 | tf_op jit(solution)/shard_map/pallas_call | solution.py:415
  241.0 7.6 %collective-permute-done.9.refs_3_ = f32[2,2,128,128]{3,2,1,0:T(8,128)S(1)} collective-permute-done((f32[2,2,128,128]{3,2,1,0:T(8,128)S(1)}, f32[2,2,128,128]{3,2,1,0:T(8,128)S(1)}, u32[]{:S(2)}, u32[]{:S(2)}) %collective-permute-start.9) | collective-permute-done | bytes 262176 | tf_op jit(solution)/shard_map/ppermute | solution.py:485
  248.5 4.2 %shard_map.102 = (f32[8,64,2048]{2,1,0:T(8,128)}, f32[8,64,2048]{2,1,0:T(8,128)}) custom-call(s32[8]{0:T(128)S(1)} %copy-done.7, bf16[8,2,256,512]{3,2,1,0:T(8,128)(2,1)S(1)} %copy-done, f32[2,4,4,128,128]{4,3,2,1,0:T(8,128)S(1)} %bitcast.45, f32[2,2,128,128]{3,2,1,0:T(8,128)S(1)} %collective-permute-done.9.refs_3_, ...), custom_call_target="tpu_custom_call", output_to_operand_aliasing={{0}: (6, {}), {1}: (7, {})} | custom-call | flops 1610612736 | bytes 14680064 | tf_op jit(solution)/shard_map/pallas_call | solution.py:415
  252.8 28.4 %collective-permute-done.1.refs_4_ = f32[2,4,128,128]{3,2,1,0:T(8,128)S(1)} collective-permute-done((f32[2,4,128,128]{3,2,1,0:T(8,128)S(1)}, f32[2,4,128,128]{3,2,1,0:T(8,128)S(1)}, u32[]{:S(2)}, u32[]{:S(2)}) %collective-permute-start.1) | collective-permute-done | bytes 524320 | tf_op jit(solution)/shard_map/ppermute | solution.py:485
  281.2 7.5 %shard_map.97 = (f32[8,64,2048]{2,1,0:T(8,128)}, f32[8,64,2048]{2,1,0:T(8,128)}) custom-call(s32[8]{0:T(128)S(1)} %copy-done.7, bf16[8,2,256,512]{3,2,1,0:T(8,128)(2,1)S(1)} %copy-done, f32[2,4,4,128,128]{4,3,2,1,0:T(8,128)} %bitcast.2.refs_2_, f32[2,4,128,128]{3,2,1,0:T(8,128)S(1)} %collective-permute-done.refs_3_, ...), custom_call_target="tpu_custom_call", output_to_operand_aliasing={{0}: (6, {}), {1}: (7, {})} | custom-call | flops 3221225472 | bytes 14680064 | tf_op jit(solution)/shard_map/pallas_call | solution.py:415
  (49 shorter events, 1.6 us)
Async XLA Ops:
  7.2 28.4 %all-to-all-start.3 = ((f32[8,4,16,8,128]{4,3,2,1,0:T(8,128)}), f32[8,4,16,8,128]{4,3,2,1,0:T(8,128)S(1)}, u32[]{:S(2)}, u32[]{:S(2)}) async-start(f32[8,4,16,8,128]{4,3,2,1,0:T(8,128)} %shard_map.99), calls=%async_computation.3 | async-start | bytes 4194304 | tf_op jit(solution)/shard_map/all_to_all | solution.py:489
  35.7 1.4 copy-start.4
  37.0 29.2 %all-to-all-start.2 = ((f32[8,4,16,8,128]{4,3,2,1,0:T(8,128)}), f32[8,4,16,8,128]{4,3,2,1,0:T(8,128)S(1)}, u32[]{:S(2)}, u32[]{:S(2)}) async-start(f32[8,4,16,8,128]{4,3,2,1,0:T(8,128)} %shard_map.98), calls=%async_computation.2 | async-start | bytes 4194304 | tf_op jit(solution)/shard_map/all_to_all | solution.py:489
  66.2 11.2 %copy-start.1 = (f32[8,4,16,8,128]{4,3,2,1,0:T(8,128)}, f32[8,4,16,8,128]{4,3,2,1,0:T(8,128)S(1)}, u32[]{:S(2)}) copy-start(f32[8,4,16,8,128]{4,3,2,1,0:T(8,128)S(1)} %all-to-all-done.2) | copy-start | bytes 6291460
  66.2 58.6 %all-to-all-start = ((f32[8,4,16,8,128]{4,3,2,1,0:T(8,128)}), f32[8,4,16,8,128]{4,3,2,1,0:T(8,128)}, u32[]{:S(2)}, u32[]{:S(2)}) async-start(f32[8,4,16,8,128]{4,3,2,1,0:T(8,128)} %shard_map.93), calls=%async_computation | async-start | bytes 4194304 | tf_op jit(solution)/shard_map/all_to_all | solution.py:489
  77.4 14.4 %collective-permute-start.4 = (f32[8,8,8,128]{3,2,1,0:T(8,128)}, f32[8,8,8,128]{3,2,1,0:T(8,128)S(1)}, u32[]{:S(2)}, u32[]{:S(2)}) collective-permute-start(f32[8,8,8,128]{3,2,1,0:T(8,128)} %get-tuple-element.25), channel_id=1, source_target_pairs={{0,8},{8,0},{16,24},{24,16},{1,9},{9,1},{17,25},{25,17},{2,10},{10... | collective-permute-start | bytes 786440 | tf_op jit(solution)/shard_map/ppermute | solution.py:485
  79.0 24.0 %collective-permute-start.6 = (f32[8,8,8,128]{3,2,1,0:T(8,128)}, f32[8,8,8,128]{3,2,1,0:T(8,128)S(1)}, u32[]{:S(2)}, u32[]{:S(2)}) collective-permute-start(f32[8,8,8,128]{3,2,1,0:T(8,128)} %get-tuple-element.27), channel_id=1, source_target_pairs={{0,16},{8,24},{16,0},{24,8},{1,17},{9,25},{17,1},{25,9},{2,18},{10... | collective-permute-start | bytes 786440 | tf_op jit(solution)/shard_map/ppermute | solution.py:485
  81.6 13.8 %copy-start.12 = (f32[8,8,8,128]{3,2,1,0:T(8,128)S(1)}, f32[8,8,8,128]{3,2,1,0:T(8,128)}, u32[]{:S(2)}) copy-start(f32[8,8,8,128]{3,2,1,0:T(8,128)} %get-tuple-element.23) | copy-start | bytes 786436
  81.6 41.5 %collective-permute-start.8 = (f32[8,8,8,128]{3,2,1,0:T(8,128)}, f32[8,8,8,128]{3,2,1,0:T(8,128)S(1)}, u32[]{:S(2)}, u32[]{:S(2)}) collective-permute-start(f32[8,8,8,128]{3,2,1,0:T(8,128)} %get-tuple-element.29), channel_id=1, source_target_pairs={{0,24},{8,16},{16,8},{24,0},{1,25},{9,17},{17,9},{25,1},{2,26},{10... | collective-permute-start | bytes 786440 | tf_op jit(solution)/shard_map/ppermute | solution.py:485
  87.2 15.8 %collective-permute-start.3 = (f32[8,8,8,128]{3,2,1,0:T(8,128)}, f32[8,8,8,128]{3,2,1,0:T(8,128)S(1)}, u32[]{:S(2)}, u32[]{:S(2)}) collective-permute-start(f32[8,8,8,128]{3,2,1,0:T(8,128)} %get-tuple-element.24), channel_id=1, source_target_pairs={{0,8},{8,0},{16,24},{24,16},{1,9},{9,1},{17,25},{25,17},{2,10},{10... | collective-permute-start | bytes 786440 | tf_op jit(solution)/shard_map/ppermute | solution.py:485
  87.9 35.2 %collective-permute-start.5 = (f32[8,8,8,128]{3,2,1,0:T(8,128)}, f32[8,8,8,128]{3,2,1,0:T(8,128)S(1)}, u32[]{:S(2)}, u32[]{:S(2)}) collective-permute-start(f32[8,8,8,128]{3,2,1,0:T(8,128)} %get-tuple-element.26), channel_id=1, source_target_pairs={{0,16},{8,24},{16,0},{24,8},{1,17},{9,25},{17,1},{25,9},{2,18},{10... | collective-permute-start | bytes 786440 | tf_op jit(solution)/shard_map/ppermute | solution.py:485
  91.8 31.3 %collective-permute-start.7 = (f32[8,8,8,128]{3,2,1,0:T(8,128)}, f32[8,8,8,128]{3,2,1,0:T(8,128)S(1)}, u32[]{:S(2)}, u32[]{:S(2)}) collective-permute-start(f32[8,8,8,128]{3,2,1,0:T(8,128)} %get-tuple-element.28), channel_id=1, source_target_pairs={{0,24},{8,16},{16,8},{24,0},{1,25},{9,17},{17,9},{25,1},{2,26},{10... | collective-permute-start | bytes 786440 | tf_op jit(solution)/shard_map/ppermute | solution.py:485
  124.8 88.1 %all-to-all-start.1 = ((f32[8,4,16,8,128]{4,3,2,1,0:T(8,128)}), f32[8,4,16,8,128]{4,3,2,1,0:T(8,128)S(1)}, u32[]{:S(2)}, u32[]{:S(2)}) async-start(f32[8,4,16,8,128]{4,3,2,1,0:T(8,128)} %copy.25), calls=%async_computation.1 | async-start | bytes 4194304 | tf_op jit(solution)/shard_map/all_to_all | solution.py:489
  134.3 2.6 copy-start.5
  136.8 8.0 %copy-start.2 = (f32[8,4,16,8,128]{4,3,2,1,0:T(8,128)S(1)}, f32[8,4,16,8,128]{4,3,2,1,0:T(8,128)}, u32[]{:S(2)}) copy-start(f32[8,4,16,8,128]{4,3,2,1,0:T(8,128)} %copy-done.1) | copy-start | bytes 6291460
  138.2 86.4 %collective-permute-start.17 = (f32[2,4,128,128]{3,2,1,0:T(8,128)}, f32[2,4,128,128]{3,2,1,0:T(8,128)}, u32[]{:S(2)}, u32[]{:S(2)}) collective-permute-start(f32[2,4,128,128]{3,2,1,0:T(8,128)} %get-tuple-element.40), channel_id=1, source_target_pairs={{0,24},{8,16},{16,8},{24,0},{1,25},{9,17},{17,9},{25,1},{2,26},{10... | collective-permute-start | bytes 1572872 | tf_op jit(solution)/shard_map/ppermute | solution.py:485
  140.7 85.5 %collective-permute-start.16 = (f32[2,4,128,128]{3,2,1,0:T(8,128)}, f32[2,4,128,128]{3,2,1,0:T(8,128)}, u32[]{:S(2)}, u32[]{:S(2)}) collective-permute-start(f32[2,4,128,128]{3,2,1,0:T(8,128)} %get-tuple-element.41), channel_id=1, source_target_pairs={{0,16},{8,24},{16,0},{24,8},{1,17},{9,25},{17,1},{25,9},{2,18},{10... | collective-permute-start | bytes 1572872 | tf_op jit(solution)/shard_map/ppermute | solution.py:485
  144.7 81.5 %collective-permute-start.15 = (f32[2,4,128,128]{3,2,1,0:T(8,128)}, f32[2,4,128,128]{3,2,1,0:T(8,128)}, u32[]{:S(2)}, u32[]{:S(2)}) collective-permute-start(f32[2,4,128,128]{3,2,1,0:T(8,128)} %get-tuple-element.42), channel_id=1, source_target_pairs={{0,8},{8,0},{16,24},{24,16},{1,9},{9,1},{17,25},{25,17},{2,10},{10... | collective-permute-start | bytes 1572872 | tf_op jit(solution)/shard_map/ppermute | solution.py:485
  146.0 66.9 %copy-start.7 = (s32[8]{0:T(128)S(1)}, s32[8]{0:T(128)}, u32[]{:S(2)}) copy-start(s32[8]{0:T(128)} %refs_0_.9) | copy-start | bytes 100
  146.0 37.3 %collective-permute-start.14 = (f32[2,2,128,128]{3,2,1,0:T(8,128)S(1)}, f32[2,2,128,128]{3,2,1,0:T(8,128)S(1)}, u32[]{:S(2)}, u32[]{:S(2)}) collective-permute-start(f32[2,2,128,128]{3,2,1,0:T(8,128)S(1)} %get-tuple-element.43), channel_id=1, source_target_pairs={{0,24},{8,16},{16,8},{24,0},{1,25},{9,17},{17,9},{25,1},{2,26},{10... | collective-permute-start | bytes 786440 | tf_op jit(solution)/shard_map/ppermute | solution.py:485
  148.4 62.1 %collective-permute-start.13 = (f32[2,2,128,128]{3,2,1,0:T(8,128)S(1)}, f32[2,2,128,128]{3,2,1,0:T(8,128)S(1)}, u32[]{:S(2)}, u32[]{:S(2)}) collective-permute-start(f32[2,2,128,128]{3,2,1,0:T(8,128)S(1)} %get-tuple-element.44), channel_id=1, source_target_pairs={{0,16},{8,24},{16,0},{24,8},{1,17},{9,25},{17,1},{25,9},{2,18},{10... | collective-permute-start | bytes 786440 | tf_op jit(solution)/shard_map/ppermute | solution.py:485
  183.3 38.4 %collective-permute-start.12 = (f32[2,2,128,128]{3,2,1,0:T(8,128)}, f32[2,2,128,128]{3,2,1,0:T(8,128)S(1)}, u32[]{:S(2)}, u32[]{:S(2)}) collective-permute-start(f32[2,2,128,128]{3,2,1,0:T(8,128)} %get-tuple-element.45), channel_id=1, source_target_pairs={{0,8},{8,0},{16,24},{24,16},{1,9},{9,1},{17,25},{25,17},{2,10},{10... | collective-permute-start | bytes 786440 | tf_op jit(solution)/shard_map/ppermute | solution.py:485
  210.5 11.8 %collective-permute-start.11 = (f32[2,2,128,128]{3,2,1,0:T(8,128)}, f32[2,2,128,128]{3,2,1,0:T(8,128)S(1)}, u32[]{:S(2)}, u32[]{:S(2)}) collective-permute-start(f32[2,2,128,128]{3,2,1,0:T(8,128)} %get-tuple-element.46), channel_id=1, source_target_pairs={{0,24},{8,16},{16,8},{24,0},{1,25},{9,17},{17,9},{25,1},{2,26},{10... | collective-permute-start | bytes 786440 | tf_op jit(solution)/shard_map/ppermute | solution.py:485
  212.9 2.2 copy-start
  215.1 6.6 %copy-start.11 = (f32[2,2,128,128]{3,2,1,0:T(8,128)S(1)}, f32[2,2,128,128]{3,2,1,0:T(8,128)}, u32[]{:S(2)}) copy-start(f32[2,2,128,128]{3,2,1,0:T(8,128)} %get-tuple-element.47) | copy-start | bytes 786436
  215.1 9.5 %copy-start.10 = (f32[2,4,128,128]{3,2,1,0:T(8,128)S(1)}, f32[2,4,128,128]{3,2,1,0:T(8,128)}, u32[]{:S(2)}) copy-start(f32[2,4,128,128]{3,2,1,0:T(8,128)} %get-tuple-element.49) | copy-start | bytes 1572868
  215.1 11.1 %copy-start.9 = (f32[2,4,128,128]{3,2,1,0:T(8,128)S(1)}, f32[2,4,128,128]{3,2,1,0:T(8,128)}, u32[]{:S(2)}) copy-start(f32[2,4,128,128]{3,2,1,0:T(8,128)} %get-tuple-element.50) | copy-start | bytes 1572868
  215.1 11.1 %copy-start.8 = (f32[2,4,128,128]{3,2,1,0:T(8,128)S(1)}, f32[2,4,128,128]{3,2,1,0:T(8,128)}, u32[]{:S(2)}) copy-start(f32[2,4,128,128]{3,2,1,0:T(8,128)} %get-tuple-element.51) | copy-start | bytes 1572868
  215.1 13.9 %copy-start.6 = (f32[8,4,16,8,128]{4,3,2,1,0:T(8,128)S(1)}, f32[8,4,16,8,128]{4,3,2,1,0:T(8,128)}, u32[]{:S(2)}) copy-start(f32[8,4,16,8,128]{4,3,2,1,0:T(8,128)} %copy-done.4) | copy-start | bytes 6291460
  221.7 19.2 %collective-permute-start.10 = (f32[2,2,128,128]{3,2,1,0:T(8,128)S(1)}, f32[2,2,128,128]{3,2,1,0:T(8,128)S(1)}, u32[]{:S(2)}, u32[]{:S(2)}) collective-permute-start(f32[2,2,128,128]{3,2,1,0:T(8,128)S(1)} %copy-done.11), channel_id=1, source_target_pairs={{0,16},{8,24},{16,0},{24,8},{1,17},{9,25},{17,1},{25,9},{2,18},{10... | collective-permute-start | bytes 786440 | tf_op jit(solution)/shard_map/ppermute | solution.py:485
  222.3 26.3 %collective-permute-start.9 = (f32[2,2,128,128]{3,2,1,0:T(8,128)S(1)}, f32[2,2,128,128]{3,2,1,0:T(8,128)S(1)}, u32[]{:S(2)}, u32[]{:S(2)}) collective-permute-start(f32[2,2,128,128]{3,2,1,0:T(8,128)S(1)} %get-tuple-element.48), channel_id=1, source_target_pairs={{0,8},{8,0},{16,24},{24,16},{1,9},{9,1},{17,25},{25,17},{2,10},{10... | collective-permute-start | bytes 786440 | tf_op jit(solution)/shard_map/ppermute | solution.py:485
  224.6 28.1 %collective-permute-start.2 = (f32[2,4,128,128]{3,2,1,0:T(8,128)S(1)}, f32[2,4,128,128]{3,2,1,0:T(8,128)S(1)}, u32[]{:S(2)}, u32[]{:S(2)}) collective-permute-start(f32[2,4,128,128]{3,2,1,0:T(8,128)S(1)} %copy-done.10), channel_id=1, source_target_pairs={{0,24},{8,16},{16,8},{24,0},{1,25},{9,17},{17,9},{25,1},{2,26},{10... | collective-permute-start | bytes 1572872 | tf_op jit(solution)/shard_map/ppermute | solution.py:485
  226.2 55.0 %collective-permute-start.1 = (f32[2,4,128,128]{3,2,1,0:T(8,128)S(1)}, f32[2,4,128,128]{3,2,1,0:T(8,128)S(1)}, u32[]{:S(2)}, u32[]{:S(2)}) collective-permute-start(f32[2,4,128,128]{3,2,1,0:T(8,128)S(1)} %copy-done.9), channel_id=1, source_target_pairs={{0,16},{8,24},{16,0},{24,8},{1,17},{9,25},{17,1},{25,9},{2,18},{10... | collective-permute-start | bytes 1572872 | tf_op jit(solution)/shard_map/ppermute | solution.py:485
  226.2 55.0 %collective-permute-start = (f32[2,4,128,128]{3,2,1,0:T(8,128)S(1)}, f32[2,4,128,128]{3,2,1,0:T(8,128)S(1)}, u32[]{:S(2)}, u32[]{:S(2)}) collective-permute-start(f32[2,4,128,128]{3,2,1,0:T(8,128)S(1)} %copy-done.8), channel_id=1, source_target_pairs={{0,8},{8,0},{16,24},{24,16},{1,9},{9,1},{17,25},{25,17},{2,10},{10... | collective-permute-start | bytes 1572872 | tf_op jit(solution)/shard_map/ppermute | solution.py:485
  229.1 7.9 %copy-start.3 = (f32[8,4,16,8,128]{4,3,2,1,0:T(8,128)S(1)}, f32[8,4,16,8,128]{4,3,2,1,0:T(8,128)}, u32[]{:S(2)}) copy-start(f32[8,4,16,8,128]{4,3,2,1,0:T(8,128)} %copy-done.1) | copy-start | bytes 6291460

commit v4 on v3

--- a/solution.py
+++ b/solution.py
@@ -452,6 +452,11 @@
     )
 
 
+def swap_order(planes):
+    half = planes // 2
+    return [half] + [j for j in range(planes - 1, 0, -1) if j != half]
+
+
 def fast_on_device(*args):
     return fast_body(*args)
 
@@ -471,7 +476,7 @@
     cut = trunc_cut.reshape(1, waves)
     packed = radix * SUBLANES
     swaps = [[(z, z ^ j) for z in range(planes)] for j in range(planes)]
-    order = list(range(planes - 1, 0, -1))
+    order = swap_order(planes)
 
     def north(slot, wind, first_pick, picks, apart):
         return north_call(

time: 291 us -> 291 us (level)
  no operation moved by 1% of the time
where the time goes in v4:
time: 291 us; the launch traced here: 289 us
  waiting for transfers between devices  135 us (46%)
  starting transfers between devices  73 us (25%)
  Pallas kernels  60.6 us (21%)
  local copies, waits for them, and re-layouts  10.8 us (4%)
  other arithmetic  8.75 us (3%)
    ppermute x18, waiting for transfers between devices, swap(): got[j] = lax.ppermute(parts[j], 'height', swaps[j])  99.2 us
    ppermute x18, starting transfers between devices, swap(): got[j] = lax.ppermute(parts[j], 'height', swaps[j])  53.9 us
    all_to_all x4, waiting for transfers between devices, around(): lax.all_to_all(block, ('width', 'row'), split_axis=0, concat_axis=0, tile...  35.4 us
    pallas_call x5, Pallas kernels, north_call(): pl.pallas_call(kernel, grid=(steps,), in_specs=[pl.BlockSpec((1, waves),...  30.5 us
    pallas_call x5, Pallas kernels, east_call(): pl.pallas_call(functools.partial(east_kernel, slot, slots_local, sources,...  30.1 us
    all_to_all x4, starting transfers between devices, around(): lax.all_to_all(block, ('width', 'row'), split_axis=0, concat_axis=0, tile...  19.1 us
  transfers between devices with their start and end apart: 22, of which 9 were waited for; matrix products, arithmetic and copies ran while one was open for 5% of the time, Pallas kernels for 16%

profile of v4, /device:TPU:6, one launch (start us, length us, event | category | flops | bytes accessed | tf_op | source)
XLA Modules:
  0.0 288.8 jit_solution(1202688840881628454)
XLA Ops:
  0.6 6.6 %shard_map.99 = f32[8,4,16,8,128]{4,3,2,1,0:T(8,128)} custom-call(s32[1,128]{1,0:T(1,128)} %bitcast.50, f32[2,2,128,2048]{3,2,1,0:T(8,128)} %vort_ref.9, f32[2,2,128,2048]{3,2,1,0:T(8,128)} %div_ref.9, bf16[2,256,256]{2,1,0:T(8,128)(2,1)} %constant.55.clone.matrix_ref, f32[2,16,128]{2,1,0:T(8,128)} %constant.56.clone.twiddle_ref), custom_call_target="tpu_custom_call" | custom-call | flops 805306368 | bytes 6291456 | tf_op jit(solution)/shard_map/pallas_call | solution.py:234
  7.2 4.2 %all-to-all-start.3 = ((f32[8,4,16,8,128]{4,3,2,1,0:T(8,128)}), f32[8,4,16,8,128]{4,3,2,1,0:T(8,128)S(1)}, u32[]{:S(2)}, u32[]{:S(2)}) async-start(f32[8,4,16,8,128]{4,3,2,1,0:T(8,128)} %shard_map.99), calls=%async_computation.3 | async-start | bytes 4194304 | tf_op jit(solution)/shard_map/all_to_all | solution.py:494
  11.4 6.6 %shard_map.98 = f32[8,4,16,8,128]{4,3,2,1,0:T(8,128)} custom-call(s32[1,128]{1,0:T(1,128)} %bitcast.51, f32[2,2,128,2048]{3,2,1,0:T(8,128)} %vort_ref.9, f32[2,2,128,2048]{3,2,1,0:T(8,128)} %div_ref.9, bf16[2,256,256]{2,1,0:T(8,128)(2,1)} %constant.55.clone.matrix_ref, f32[2,16,128]{2,1,0:T(8,128)} %constant.56.clone.twiddle_ref), custom_call_target="tpu_custom_call" | custom-call | flops 805306368 | bytes 6291456 | tf_op jit(solution)/shard_map/pallas_call | solution.py:234
  18.0 17.7 %all-to-all-done.3 = f32[8,4,16,8,128]{4,3,2,1,0:T(8,128)S(1)} async-done(((f32[8,4,16,8,128]{4,3,2,1,0:T(8,128)}), f32[8,4,16,8,128]{4,3,2,1,0:T(8,128)S(1)}, u32[]{:S(2)}, u32[]{:S(2)}) %all-to-all-start.3) | async-done | bytes 2097184 | tf_op jit(solution)/shard_map/all_to_all | solution.py:494
  35.7 1.4 copy-done.4
  37.0 5.0 %all-to-all-start.2 = ((f32[8,4,16,8,128]{4,3,2,1,0:T(8,128)}), f32[8,4,16,8,128]{4,3,2,1,0:T(8,128)S(1)}, u32[]{:S(2)}, u32[]{:S(2)}) async-start(f32[8,4,16,8,128]{4,3,2,1,0:T(8,128)} %shard_map.98), calls=%async_computation.2 | async-start | bytes 4194304 | tf_op jit(solution)/shard_map/all_to_all | solution.py:494
  42.0 6.6 %shard_map.93 = f32[8,4,16,8,128]{4,3,2,1,0:T(8,128)} custom-call(s32[1,128]{1,0:T(1,128)} %bitcast.52, f32[2,2,128,2048]{3,2,1,0:T(8,128)} %vort_ref.9, f32[2,2,128,2048]{3,2,1,0:T(8,128)} %div_ref.9, bf16[2,256,256]{2,1,0:T(8,128)(2,1)} %constant.55.clone.matrix_ref, f32[2,16,128]{2,1,0:T(8,128)} %constant.56.clone.twiddle_ref), custom_call_target="tpu_custom_call" | custom-call | flops 805306368 | bytes 6291456 | tf_op jit(solution)/shard_map/pallas_call | solution.py:234
  48.6 17.7 %all-to-all-done.2 = f32[8,4,16,8,128]{4,3,2,1,0:T(8,128)S(1)} async-done(((f32[8,4,16,8,128]{4,3,2,1,0:T(8,128)}), f32[8,4,16,8,128]{4,3,2,1,0:T(8,128)S(1)}, u32[]{:S(2)}, u32[]{:S(2)}) %all-to-all-start.2) | async-done | bytes 2097184 | tf_op jit(solution)/shard_map/all_to_all | solution.py:494
  66.2 5.7 %all-to-all-start = ((f32[8,4,16,8,128]{4,3,2,1,0:T(8,128)}), f32[8,4,16,8,128]{4,3,2,1,0:T(8,128)}, u32[]{:S(2)}, u32[]{:S(2)}) async-start(f32[8,4,16,8,128]{4,3,2,1,0:T(8,128)} %shard_map.93), calls=%async_computation | async-start | bytes 4194304 | tf_op jit(solution)/shard_map/all_to_all | solution.py:494
  72.0 5.4 %shard_map.95 = (f32[8,8,8,128]{3,2,1,0:T(8,128)}, f32[8,8,8,128]{3,2,1,0:T(8,128)}, f32[8,8,8,128]{3,2,1,0:T(8,128)}, f32[8,8,8,128]{3,2,1,0:T(8,128)}) custom-call(s32[1,128]{1,0:T(1,128)} %bitcast.53, f32[2,2,128,2048]{3,2,1,0:T(8,128)} %vort_ref.9, f32[2,2,128,2048]{3,2,1,0:T(8,128)} %div_ref.9, bf16[2,256,256]{2,1,0:T(8,128)(2,1)} %constant.55.clone.matrix_ref, ...), custom_call_target="tpu_custom_call" | custom-call | flops 402653184 | bytes 6291456 | tf_op jit(solution)/shard_map/pallas_call | solution.py:234
  77.4 1.6 collective-permute-start.4
  79.0 2.6 collective-permute-start.6
  81.8 5.4 %shard_map.94 = (f32[8,8,8,128]{3,2,1,0:T(8,128)}, f32[8,8,8,128]{3,2,1,0:T(8,128)}, f32[8,8,8,128]{3,2,1,0:T(8,128)}, f32[8,8,8,128]{3,2,1,0:T(8,128)}) custom-call(s32[1,128]{1,0:T(1,128)} %bitcast.54, f32[2,2,128,2048]{3,2,1,0:T(8,128)} %vort_ref.9, f32[2,2,128,2048]{3,2,1,0:T(8,128)} %div_ref.9, bf16[2,256,256]{2,1,0:T(8,128)(2,1)} %constant.55.clone.matrix_ref, ...), custom_call_target="tpu_custom_call" | custom-call | flops 402653184 | bytes 6291456 | tf_op jit(solution)/shard_map/pallas_call | solution.py:234
  87.2 0.7 collective-permute-start.3
  87.9 3.5 %collective-permute-start.5 = (f32[8,8,8,128]{3,2,1,0:T(8,128)}, f32[8,8,8,128]{3,2,1,0:T(8,128)S(1)}, u32[]{:S(2)}, u32[]{:S(2)}) collective-permute-start(f32[8,8,8,128]{3,2,1,0:T(8,128)} %get-tuple-element.26), channel_id=1, source_target_pairs={{0,16},{8,24},{16,0},{24,8},{1,17},{9,25},{17,1},{25,9},{2,18},{10... | collective-permute-start | bytes 786440 | tf_op jit(solution)/shard_map/ppermute | solution.py:490
  91.4 0.4 collective-permute-done.4
  91.8 3.5 %collective-permute-start.7 = (f32[8,8,8,128]{3,2,1,0:T(8,128)}, f32[8,8,8,128]{3,2,1,0:T(8,128)S(1)}, u32[]{:S(2)}, u32[]{:S(2)}) collective-permute-start(f32[8,8,8,128]{3,2,1,0:T(8,128)} %get-tuple-element.28), channel_id=1, source_target_pairs={{0,24},{8,16},{16,8},{24,0},{1,25},{9,17},{17,9},{25,1},{2,26},{10... | collective-permute-start | bytes 786440 | tf_op jit(solution)/shard_map/ppermute | solution.py:490
  95.4 1.0 maximum_bitcast_fusion
  96.3 6.6 %collective-permute-done.3 = f32[8,8,8,128]{3,2,1,0:T(8,128)S(1)} collective-permute-done((f32[8,8,8,128]{3,2,1,0:T(8,128)}, f32[8,8,8,128]{3,2,1,0:T(8,128)S(1)}, u32[]{:S(2)}, u32[]{:S(2)}) %collective-permute-start.3) | collective-permute-done | bytes 262176 | tf_op jit(solution)/shard_map/ppermute | solution.py:490
  103.0 20.0 %collective-permute-done.5 = f32[8,8,8,128]{3,2,1,0:T(8,128)S(1)} collective-permute-done((f32[8,8,8,128]{3,2,1,0:T(8,128)}, f32[8,8,8,128]{3,2,1,0:T(8,128)S(1)}, u32[]{:S(2)}, u32[]{:S(2)}) %collective-permute-start.5) | collective-permute-done | bytes 262176 | tf_op jit(solution)/shard_map/ppermute | solution.py:490
  123.3 1.5 copy.25
  124.8 4.2 %all-to-all-start.1 = ((f32[8,4,16,8,128]{4,3,2,1,0:T(8,128)}), f32[8,4,16,8,128]{4,3,2,1,0:T(8,128)S(1)}, u32[]{:S(2)}, u32[]{:S(2)}) async-start(f32[8,4,16,8,128]{4,3,2,1,0:T(8,128)} %copy.25), calls=%async_computation.1 | async-start | bytes 4194304 | tf_op jit(solution)/shard_map/all_to_all | solution.py:494
  129.0 5.1 %reduce-precision_convert_fusion = (bf16[8,1,128,256]{3,2,1,0:T(8,128)(2,1)S(1)}, bf16[8,1,128,256]{3,2,1,0:T(8,128)(2,1)S(1)}, bf16[8,1,128,256]{3,2,1,0:T(8,128)(2,1)S(1)}, bf16[8,1,128,256]{3,2,1,0:T(8,128)(2,1)S(1)}) fusion(s32[8,128]{1,0:T(8,128)S(1)} %iota_add_fusion), kind=kLoop, calls=%fused_computation.6 | loop fusion | flops 5767168 | bytes 2101248 | tf_op jit(solution)/shard_map/convert_element_type | solution.py:269
  134.3 2.2 maximum_maximum_fusion.refs_1_
  137.0 1.2 slice_bitcast_fusion
  138.2 2.5 collective-permute-start.17
  140.7 4.0 %collective-permute-start.16 = (f32[2,4,128,128]{3,2,1,0:T(8,128)}, f32[2,4,128,128]{3,2,1,0:T(8,128)}, u32[]{:S(2)}, u32[]{:S(2)}) collective-permute-start(f32[2,4,128,128]{3,2,1,0:T(8,128)} %get-tuple-element.41), channel_id=1, source_target_pairs={{0,16},{8,24},{16,0},{24,8},{1,17},{9,25},{17,1},{25,9},{2,18},{10... | collective-permute-start | bytes 1572872 | tf_op jit(solution)/shard_map/ppermute | solution.py:490
  145.1 0.9 slice_bitcast_fusion.6
  146.0 2.4 collective-permute-start.14
  148.4 1.0 collective-permute-start.13
  149.4 1.7 copy.24
  151.1 1.2 slice_bitcast_fusion.3
  152.3 31.0 %collective-permute-done.14.refs_5_ = f32[2,2,128,128]{3,2,1,0:T(8,128)S(1)} collective-permute-done((f32[2,2,128,128]{3,2,1,0:T(8,128)S(1)}, f32[2,2,128,128]{3,2,1,0:T(8,128)S(1)}, u32[]{:S(2)}, u32[]{:S(2)}) %collective-permute-start.14) | collective-permute-done | bytes 262176 | tf_op jit(solution)/shard_map/ppermute | solution.py:490
  183.3 22.1 %collective-permute-start.12 = (f32[2,2,128,128]{3,2,1,0:T(8,128)}, f32[2,2,128,128]{3,2,1,0:T(8,128)S(1)}, u32[]{:S(2)}, u32[]{:S(2)}) collective-permute-start(f32[2,2,128,128]{3,2,1,0:T(8,128)} %get-tuple-element.45), channel_id=1, source_target_pairs={{0,8},{8,0},{16,24},{24,16},{1,9},{9,1},{17,25},{25,17},{2,10},{10... | collective-permute-start | bytes 786440 | tf_op jit(solution)/shard_map/ppermute | solution.py:490
  205.4 5.1 %collective-permute-done.13.refs_4_ = f32[2,2,128,128]{3,2,1,0:T(8,128)S(1)} collective-permute-done((f32[2,2,128,128]{3,2,1,0:T(8,128)S(1)}, f32[2,2,128,128]{3,2,1,0:T(8,128)S(1)}, u32[]{:S(2)}, u32[]{:S(2)}) %collective-permute-start.13) | collective-permute-done | bytes 262176 | tf_op jit(solution)/shard_map/ppermute | solution.py:490
  210.5 2.5 collective-permute-start.11
  212.9 2.2 copy-done
  215.1 6.6 %shard_map.96 = (f32[8,64,2048]{2,1,0:T(8,128)}, f32[8,64,2048]{2,1,0:T(8,128)}) custom-call(s32[8]{0:T(128)S(1)} %copy-done.7, bf16[8,2,256,512]{3,2,1,0:T(8,128)(2,1)S(1)} %copy-done, f32[2,4,4,128,128]{4,3,2,1,0:T(8,128)S(1)} %bitcast.40, f32[2,4,4,128,128]{4,3,2,1,0:T(8,128)S(1)} %bitcast.41, f32[2,4,4,128,128]{4,3,2,1,0:T(8,128)S(1)} %bitcast.42, ...), custom_call_target="tpu_custom_call" | custom-call | flops 3221225472 | bytes 14680064 | tf_op jit(solution)/shard_map/pallas_call | solution.py:415
  221.7 0.5 collective-permute-start.10
  222.3 2.4 collective-permute-start.9
  224.6 1.6 collective-permute-start.2
  226.2 2.8 collective-permute-start
  229.1 7.8 %shard_map.100 = (f32[8,64,2048]{2,1,0:T(8,128)}, f32[8,64,2048]{2,1,0:T(8,128)}) custom-call(s32[8]{0:T(128)S(1)} %copy-done.7, bf16[8,2,256,512]{3,2,1,0:T(8,128)(2,1)S(1)} %copy-done, f32[2,4,4,128,128]{4,3,2,1,0:T(8,128)S(1)} %bitcast.46, f32[2,4,128,128]{3,2,1,0:T(8,128)} %collective-permute-done.15.refs_3_, ...), custom_call_target="tpu_custom_call" | custom-call | flops 3221225472 | bytes 14680064 | tf_op jit(solution)/shard_map/pallas_call | solution.py:415
  236.9 4.0 %shard_map.101 = (f32[8,64,2048]{2,1,0:T(8,128)}, f32[8,64,2048]{2,1,0:T(8,128)}) custom-call(s32[8]{0:T(128)S(1)} %copy-done.7, bf16[8,2,256,512]{3,2,1,0:T(8,128)(2,1)S(1)} %copy-done, f32[2,4,4,128,128]{4,3,2,1,0:T(8,128)S(1)} %bitcast.44, f32[2,2,128,128]{3,2,1,0:T(8,128)S(1)} %collective-permute-done.12.refs_3_, ...), custom_call_target="tpu_custom_call", output_to_operand_aliasing={{0}: (6, {}), {1}: (7, {})} | custom-call | flops 1610612736 | bytes 14680064 | tf_op jit(solution)/shard_map/pallas_call | solution.py:415
  241.0 7.6 %collective-permute-done.9.refs_3_ = f32[2,2,128,128]{3,2,1,0:T(8,128)S(1)} collective-permute-done((f32[2,2,128,128]{3,2,1,0:T(8,128)S(1)}, f32[2,2,128,128]{3,2,1,0:T(8,128)S(1)}, u32[]{:S(2)}, u32[]{:S(2)}) %collective-permute-start.9) | collective-permute-done | bytes 262176 | tf_op jit(solution)/shard_map/ppermute | solution.py:490
  248.5 4.2 %shard_map.102 = (f32[8,64,2048]{2,1,0:T(8,128)}, f32[8,64,2048]{2,1,0:T(8,128)}) custom-call(s32[8]{0:T(128)S(1)} %copy-done.7, bf16[8,2,256,512]{3,2,1,0:T(8,128)(2,1)S(1)} %copy-done, f32[2,4,4,128,128]{4,3,2,1,0:T(8,128)S(1)} %bitcast.45, f32[2,2,128,128]{3,2,1,0:T(8,128)S(1)} %collective-permute-done.9.refs_3_, ...), custom_call_target="tpu_custom_call", output_to_operand_aliasing={{0}: (6, {}), {1}: (7, {})} | custom-call | flops 1610612736 | bytes 14680064 | tf_op jit(solution)/shard_map/pallas_call | solution.py:415
  252.8 28.4 %collective-permute-done.1.refs_4_ = f32[2,4,128,128]{3,2,1,0:T(8,128)S(1)} collective-permute-done((f32[2,4,128,128]{3,2,1,0:T(8,128)S(1)}, f32[2,4,128,128]{3,2,1,0:T(8,128)S(1)}, u32[]{:S(2)}, u32[]{:S(2)}) %collective-permute-start.1) | collective-permute-done | bytes 524320 | tf_op jit(solution)/shard_map/ppermute | solution.py:490
  281.2 7.5 %shard_map.97 = (f32[8,64,2048]{2,1,0:T(8,128)}, f32[8,64,2048]{2,1,0:T(8,128)}) custom-call(s32[8]{0:T(128)S(1)} %copy-done.7, bf16[8,2,256,512]{3,2,1,0:T(8,128)(2,1)S(1)} %copy-done, f32[2,4,4,128,128]{4,3,2,1,0:T(8,128)} %bitcast.2.refs_2_, f32[2,4,128,128]{3,2,1,0:T(8,128)S(1)} %collective-permute-done.refs_3_, ...), custom_call_target="tpu_custom_call", output_to_operand_aliasing={{0}: (6, {}), {1}: (7, {})} | custom-call | flops 3221225472 | bytes 14680064 | tf_op jit(solution)/shard_map/pallas_call | solution.py:415
  (49 shorter events, 1.6 us)
Async XLA Ops:
  7.2 28.4 %all-to-all-start.3 = ((f32[8,4,16,8,128]{4,3,2,1,0:T(8,128)}), f32[8,4,16,8,128]{4,3,2,1,0:T(8,128)S(1)}, u32[]{:S(2)}, u32[]{:S(2)}) async-start(f32[8,4,16,8,128]{4,3,2,1,0:T(8,128)} %shard_map.99), calls=%async_computation.3 | async-start | bytes 4194304 | tf_op jit(solution)/shard_map/all_to_all | solution.py:494
  35.7 1.4 copy-start.4
  37.0 29.2 %all-to-all-start.2 = ((f32[8,4,16,8,128]{4,3,2,1,0:T(8,128)}), f32[8,4,16,8,128]{4,3,2,1,0:T(8,128)S(1)}, u32[]{:S(2)}, u32[]{:S(2)}) async-start(f32[8,4,16,8,128]{4,3,2,1,0:T(8,128)} %shard_map.98), calls=%async_computation.2 | async-start | bytes 4194304 | tf_op jit(solution)/shard_map/all_to_all | solution.py:494
  66.2 11.2 %copy-start.1 = (f32[8,4,16,8,128]{4,3,2,1,0:T(8,128)}, f32[8,4,16,8,128]{4,3,2,1,0:T(8,128)S(1)}, u32[]{:S(2)}) copy-start(f32[8,4,16,8,128]{4,3,2,1,0:T(8,128)S(1)} %all-to-all-done.2) | copy-start | bytes 6291460
  66.2 58.6 %all-to-all-start = ((f32[8,4,16,8,128]{4,3,2,1,0:T(8,128)}), f32[8,4,16,8,128]{4,3,2,1,0:T(8,128)}, u32[]{:S(2)}, u32[]{:S(2)}) async-start(f32[8,4,16,8,128]{4,3,2,1,0:T(8,128)} %shard_map.93), calls=%async_computation | async-start | bytes 4194304 | tf_op jit(solution)/shard_map/all_to_all | solution.py:494
  77.4 14.4 %collective-permute-start.4 = (f32[8,8,8,128]{3,2,1,0:T(8,128)}, f32[8,8,8,128]{3,2,1,0:T(8,128)S(1)}, u32[]{:S(2)}, u32[]{:S(2)}) collective-permute-start(f32[8,8,8,128]{3,2,1,0:T(8,128)} %get-tuple-element.25), channel_id=1, source_target_pairs={{0,8},{8,0},{16,24},{24,16},{1,9},{9,1},{17,25},{25,17},{2,10},{10... | collective-permute-start | bytes 786440 | tf_op jit(solution)/shard_map/ppermute | solution.py:490
  79.0 24.0 %collective-permute-start.6 = (f32[8,8,8,128]{3,2,1,0:T(8,128)}, f32[8,8,8,128]{3,2,1,0:T(8,128)S(1)}, u32[]{:S(2)}, u32[]{:S(2)}) collective-permute-start(f32[8,8,8,128]{3,2,1,0:T(8,128)} %get-tuple-element.27), channel_id=1, source_target_pairs={{0,16},{8,24},{16,0},{24,8},{1,17},{9,25},{17,1},{25,9},{2,18},{10... | collective-permute-start | bytes 786440 | tf_op jit(solution)/shard_map/ppermute | solution.py:490
  81.6 13.8 %copy-start.12 = (f32[8,8,8,128]{3,2,1,0:T(8,128)S(1)}, f32[8,8,8,128]{3,2,1,0:T(8,128)}, u32[]{:S(2)}) copy-start(f32[8,8,8,128]{3,2,1,0:T(8,128)} %get-tuple-element.23) | copy-start | bytes 786436
  81.6 41.5 %collective-permute-start.8 = (f32[8,8,8,128]{3,2,1,0:T(8,128)}, f32[8,8,8,128]{3,2,1,0:T(8,128)S(1)}, u32[]{:S(2)}, u32[]{:S(2)}) collective-permute-start(f32[8,8,8,128]{3,2,1,0:T(8,128)} %get-tuple-element.29), channel_id=1, source_target_pairs={{0,24},{8,16},{16,8},{24,0},{1,25},{9,17},{17,9},{25,1},{2,26},{10... | collective-permute-start | bytes 786440 | tf_op jit(solution)/shard_map/ppermute | solution.py:490
  87.2 15.8 %collective-permute-start.3 = (f32[8,8,8,128]{3,2,1,0:T(8,128)}, f32[8,8,8,128]{3,2,1,0:T(8,128)S(1)}, u32[]{:S(2)}, u32[]{:S(2)}) collective-permute-start(f32[8,8,8,128]{3,2,1,0:T(8,128)} %get-tuple-element.24), channel_id=1, source_target_pairs={{0,8},{8,0},{16,24},{24,16},{1,9},{9,1},{17,25},{25,17},{2,10},{10... | collective-permute-start | bytes 786440 | tf_op jit(solution)/shard_map/ppermute | solution.py:490
  87.9 35.2 %collective-permute-start.5 = (f32[8,8,8,128]{3,2,1,0:T(8,128)}, f32[8,8,8,128]{3,2,1,0:T(8,128)S(1)}, u32[]{:S(2)}, u32[]{:S(2)}) collective-permute-start(f32[8,8,8,128]{3,2,1,0:T(8,128)} %get-tuple-element.26), channel_id=1, source_target_pairs={{0,16},{8,24},{16,0},{24,8},{1,17},{9,25},{17,1},{25,9},{2,18},{10... | collective-permute-start | bytes 786440 | tf_op jit(solution)/shard_map/ppermute | solution.py:490
  91.8 31.3 %collective-permute-start.7 = (f32[8,8,8,128]{3,2,1,0:T(8,128)}, f32[8,8,8,128]{3,2,1,0:T(8,128)S(1)}, u32[]{:S(2)}, u32[]{:S(2)}) collective-permute-start(f32[8,8,8,128]{3,2,1,0:T(8,128)} %get-tuple-element.28), channel_id=1, source_target_pairs={{0,24},{8,16},{16,8},{24,0},{1,25},{9,17},{17,9},{25,1},{2,26},{10... | collective-permute-start | bytes 786440 | tf_op jit(solution)/shard_map/ppermute | solution.py:490
  124.8 88.1 %all-to-all-start.1 = ((f32[8,4,16,8,128]{4,3,2,1,0:T(8,128)}), f32[8,4,16,8,128]{4,3,2,1,0:T(8,128)S(1)}, u32[]{:S(2)}, u32[]{:S(2)}) async-start(f32[8,4,16,8,128]{4,3,2,1,0:T(8,128)} %copy.25), calls=%async_computation.1 | async-start | bytes 4194304 | tf_op jit(solution)/shard_map/all_to_all | solution.py:494
  134.3 2.6 copy-start.5
  136.8 8.0 %copy-start.2 = (f32[8,4,16,8,128]{4,3,2,1,0:T(8,128)S(1)}, f32[8,4,16,8,128]{4,3,2,1,0:T(8,128)}, u32[]{:S(2)}) copy-start(f32[8,4,16,8,128]{4,3,2,1,0:T(8,128)} %copy-done.1) | copy-start | bytes 6291460
  138.2 86.4 %collective-permute-start.17 = (f32[2,4,128,128]{3,2,1,0:T(8,128)}, f32[2,4,128,128]{3,2,1,0:T(8,128)}, u32[]{:S(2)}, u32[]{:S(2)}) collective-permute-start(f32[2,4,128,128]{3,2,1,0:T(8,128)} %get-tuple-element.40), channel_id=1, source_target_pairs={{0,24},{8,16},{16,8},{24,0},{1,25},{9,17},{17,9},{25,1},{2,26},{10... | collective-permute-start | bytes 1572872 | tf_op jit(solution)/shard_map/ppermute | solution.py:490
  140.7 85.5 %collective-permute-start.16 = (f32[2,4,128,128]{3,2,1,0:T(8,128)}, f32[2,4,128,128]{3,2,1,0:T(8,128)}, u32[]{:S(2)}, u32[]{:S(2)}) collective-permute-start(f32[2,4,128,128]{3,2,1,0:T(8,128)} %get-tuple-element.41), channel_id=1, source_target_pairs={{0,16},{8,24},{16,0},{24,8},{1,17},{9,25},{17,1},{25,9},{2,18},{10... | collective-permute-start | bytes 1572872 | tf_op jit(solution)/shard_map/ppermute | solution.py:490
  144.7 81.5 %collective-permute-start.15 = (f32[2,4,128,128]{3,2,1,0:T(8,128)}, f32[2,4,128,128]{3,2,1,0:T(8,128)}, u32[]{:S(2)}, u32[]{:S(2)}) collective-permute-start(f32[2,4,128,128]{3,2,1,0:T(8,128)} %get-tuple-element.42), channel_id=1, source_target_pairs={{0,8},{8,0},{16,24},{24,16},{1,9},{9,1},{17,25},{25,17},{2,10},{10... | collective-permute-start | bytes 1572872 | tf_op jit(solution)/shard_map/ppermute | solution.py:490
  146.0 66.9 %copy-start.7 = (s32[8]{0:T(128)S(1)}, s32[8]{0:T(128)}, u32[]{:S(2)}) copy-start(s32[8]{0:T(128)} %refs_0_.9) | copy-start | bytes 100
  146.0 37.3 %collective-permute-start.14 = (f32[2,2,128,128]{3,2,1,0:T(8,128)S(1)}, f32[2,2,128,128]{3,2,1,0:T(8,128)S(1)}, u32[]{:S(2)}, u32[]{:S(2)}) collective-permute-start(f32[2,2,128,128]{3,2,1,0:T(8,128)S(1)} %get-tuple-element.43), channel_id=1, source_target_pairs={{0,24},{8,16},{16,8},{24,0},{1,25},{9,17},{17,9},{25,1},{2,26},{10... | collective-permute-start | bytes 786440 | tf_op jit(solution)/shard_map/ppermute | solution.py:490
  148.4 62.1 %collective-permute-start.13 = (f32[2,2,128,128]{3,2,1,0:T(8,128)S(1)}, f32[2,2,128,128]{3,2,1,0:T(8,128)S(1)}, u32[]{:S(2)}, u32[]{:S(2)}) collective-permute-start(f32[2,2,128,128]{3,2,1,0:T(8,128)S(1)} %get-tuple-element.44), channel_id=1, source_target_pairs={{0,16},{8,24},{16,0},{24,8},{1,17},{9,25},{17,1},{25,9},{2,18},{10... | collective-permute-start | bytes 786440 | tf_op jit(solution)/shard_map/ppermute | solution.py:490
  183.3 38.4 %collective-permute-start.12 = (f32[2,2,128,128]{3,2,1,0:T(8,128)}, f32[2,2,128,128]{3,2,1,0:T(8,128)S(1)}, u32[]{:S(2)}, u32[]{:S(2)}) collective-permute-start(f32[2,2,128,128]{3,2,1,0:T(8,128)} %get-tuple-element.45), channel_id=1, source_target_pairs={{0,8},{8,0},{16,24},{24,16},{1,9},{9,1},{17,25},{25,17},{2,10},{10... | collective-permute-start | bytes 786440 | tf_op jit(solution)/shard_map/ppermute | solution.py:490
  210.5 11.8 %collective-permute-start.11 = (f32[2,2,128,128]{3,2,1,0:T(8,128)}, f32[2,2,128,128]{3,2,1,0:T(8,128)S(1)}, u32[]{:S(2)}, u32[]{:S(2)}) collective-permute-start(f32[2,2,128,128]{3,2,1,0:T(8,128)} %get-tuple-element.46), channel_id=1, source_target_pairs={{0,24},{8,16},{16,8},{24,0},{1,25},{9,17},{17,9},{25,1},{2,26},{10... | collective-permute-start | bytes 786440 | tf_op jit(solution)/shard_map/ppermute | solution.py:490
  212.9 2.2 copy-start
  215.1 6.6 %copy-start.11 = (f32[2,2,128,128]{3,2,1,0:T(8,128)S(1)}, f32[2,2,128,128]{3,2,1,0:T(8,128)}, u32[]{:S(2)}) copy-start(f32[2,2,128,128]{3,2,1,0:T(8,128)} %get-tuple-element.47) | copy-start | bytes 786436
  215.1 9.5 %copy-start.10 = (f32[2,4,128,128]{3,2,1,0:T(8,128)S(1)}, f32[2,4,128,128]{3,2,1,0:T(8,128)}, u32[]{:S(2)}) copy-start(f32[2,4,128,128]{3,2,1,0:T(8,128)} %get-tuple-element.49) | copy-start | bytes 1572868
  215.1 11.1 %copy-start.9 = (f32[2,4,128,128]{3,2,1,0:T(8,128)S(1)}, f32[2,4,128,128]{3,2,1,0:T(8,128)}, u32[]{:S(2)}) copy-start(f32[2,4,128,128]{3,2,1,0:T(8,128)} %get-tuple-element.50) | copy-start | bytes 1572868
  215.1 11.1 %copy-start.8 = (f32[2,4,128,128]{3,2,1,0:T(8,128)S(1)}, f32[2,4,128,128]{3,2,1,0:T(8,128)}, u32[]{:S(2)}) copy-start(f32[2,4,128,128]{3,2,1,0:T(8,128)} %get-tuple-element.51) | copy-start | bytes 1572868
  215.1 13.9 %copy-start.6 = (f32[8,4,16,8,128]{4,3,2,1,0:T(8,128)S(1)}, f32[8,4,16,8,128]{4,3,2,1,0:T(8,128)}, u32[]{:S(2)}) copy-start(f32[8,4,16,8,128]{4,3,2,1,0:T(8,128)} %copy-done.4) | copy-start | bytes 6291460
  221.7 19.2 %collective-permute-start.10 = (f32[2,2,128,128]{3,2,1,0:T(8,128)S(1)}, f32[2,2,128,128]{3,2,1,0:T(8,128)S(1)}, u32[]{:S(2)}, u32[]{:S(2)}) collective-permute-start(f32[2,2,128,128]{3,2,1,0:T(8,128)S(1)} %copy-done.11), channel_id=1, source_target_pairs={{0,16},{8,24},{16,0},{24,8},{1,17},{9,25},{17,1},{25,9},{2,18},{10... | collective-permute-start | bytes 786440 | tf_op jit(solution)/shard_map/ppermute | solution.py:490
  222.3 26.3 %collective-permute-start.9 = (f32[2,2,128,128]{3,2,1,0:T(8,128)S(1)}, f32[2,2,128,128]{3,2,1,0:T(8,128)S(1)}, u32[]{:S(2)}, u32[]{:S(2)}) collective-permute-start(f32[2,2,128,128]{3,2,1,0:T(8,128)S(1)} %get-tuple-element.48), channel_id=1, source_target_pairs={{0,8},{8,0},{16,24},{24,16},{1,9},{9,1},{17,25},{25,17},{2,10},{10... | collective-permute-start | bytes 786440 | tf_op jit(solution)/shard_map/ppermute | solution.py:490
  224.6 28.1 %collective-permute-start.2 = (f32[2,4,128,128]{3,2,1,0:T(8,128)S(1)}, f32[2,4,128,128]{3,2,1,0:T(8,128)S(1)}, u32[]{:S(2)}, u32[]{:S(2)}) collective-permute-start(f32[2,4,128,128]{3,2,1,0:T(8,128)S(1)} %copy-done.10), channel_id=1, source_target_pairs={{0,24},{8,16},{16,8},{24,0},{1,25},{9,17},{17,9},{25,1},{2,26},{10... | collective-permute-start | bytes 1572872 | tf_op jit(solution)/shard_map/ppermute | solution.py:490
  226.2 55.0 %collective-permute-start.1 = (f32[2,4,128,128]{3,2,1,0:T(8,128)S(1)}, f32[2,4,128,128]{3,2,1,0:T(8,128)S(1)}, u32[]{:S(2)}, u32[]{:S(2)}) collective-permute-start(f32[2,4,128,128]{3,2,1,0:T(8,128)S(1)} %copy-done.9), channel_id=1, source_target_pairs={{0,16},{8,24},{16,0},{24,8},{1,17},{9,25},{17,1},{25,9},{2,18},{10... | collective-permute-start | bytes 1572872 | tf_op jit(solution)/shard_map/ppermute | solution.py:490
  226.2 55.0 %collective-permute-start = (f32[2,4,128,128]{3,2,1,0:T(8,128)S(1)}, f32[2,4,128,128]{3,2,1,0:T(8,128)S(1)}, u32[]{:S(2)}, u32[]{:S(2)}) collective-permute-start(f32[2,4,128,128]{3,2,1,0:T(8,128)S(1)} %copy-done.8), channel_id=1, source_target_pairs={{0,8},{8,0},{16,24},{24,16},{1,9},{9,1},{17,25},{25,17},{2,10},{10... | collective-permute-start | bytes 1572872 | tf_op jit(solution)/shard_map/ppermute | solution.py:490
  229.1 7.9 %copy-start.3 = (f32[8,4,16,8,128]{4,3,2,1,0:T(8,128)S(1)}, f32[8,4,16,8,128]{4,3,2,1,0:T(8,128)}, u32[]{:S(2)}) copy-start(f32[8,4,16,8,128]{4,3,2,1,0:T(8,128)} %copy-done.1) | copy-start | bytes 6291460
